TPU v7x, 32 devices: a whole 2x2x4 slice. The times are simulated.
32 devices in a mesh: dp: 16 (over z, x, core), mp: 2 (over y).
Axes of the slice: x: 2, y: 2, z: 4, core: 2. Of those that a mesh axis runs over, the one named last changes fastest.
Arguments:
- inputs: bfloat16 [32768, 1152], P(('dp', 'mp')), may hold values from -6 to 6
- picture_start: int32 [32768], P('dp'), may hold values from 0 to 31744, as said below
- prenorm_gain: float32 [1152], replicated, may hold values from 0.5 to 1.5
- prenorm_shift: float32 [1152], replicated, may hold values from -2 to 2
- query_weight: bfloat16 [1152, 1152], P('dp', 'mp'), may hold values from -1 to 1
- query_bias: float32 [1152], P('mp'), may hold values from -2 to 2
- key_weight: bfloat16 [1152, 1152], P('dp', 'mp'), may hold values from -0.1875 to 0.1875
- value_weight: bfloat16 [1152, 1152], P('dp', 'mp'), may hold values from -0.1875 to 0.1875
- value_bias: float32 [1152], P('mp'), may hold values from -2 to 2
- output_weight: bfloat16 [1152, 1152], P('mp', 'dp'), may hold values from -0.75 to 0.75
- output_bias: float32 [1152], replicated, may hold values from -2 to 2
- midnorm_gain: float32 [1152], replicated, may hold values from 0.5 to 1.5
- midnorm_shift: float32 [1152], replicated, may hold values from -2 to 2
- hidden_weight: bfloat16 [1152, 4304], P('dp', 'mp'), may hold values from -0.1875 to 0.1875
- hidden_bias: float32 [4304], P('mp'), may hold values from -2 to 2
- project_weight: bfloat16 [4304, 1152], P('mp', 'dp'), may hold values from -0.09375 to 0.09375
- project_bias: float32 [1152], replicated, may hold values from -2 to 2
- cotangent: bfloat16 [32768, 1152], P(('dp', 'mp')), may hold values from -6 to 6
Outputs:
- layer_output: bfloat16 [32768, 1152], P(('dp', 'mp'))
- inputs_gradient: float32 [32768, 1152], P(('dp', 'mp'))
- prenorm_gain_gradient: float32 [1152], replicated
- prenorm_shift_gradient: float32 [1152], replicated
- query_weight_gradient: float32 [1152, 1152], P('dp', 'mp')
- query_bias_gradient: float32 [1152], P('mp')
- key_weight_gradient: float32 [1152, 1152], P('dp', 'mp')
- value_weight_gradient: float32 [1152, 1152], P('dp', 'mp')
- value_bias_gradient: float32 [1152], P('mp')
- output_weight_gradient: float32 [1152, 1152], P('mp', 'dp')
- output_bias_gradient: float32 [1152], replicated
- midnorm_gain_gradient: float32 [1152], replicated
- midnorm_shift_gradient: float32 [1152], replicated
- hidden_weight_gradient: float32 [1152, 4304], P('dp', 'mp')
- hidden_bias_gradient: float32 [4304], P('mp')
- project_weight_gradient: float32 [4304, 1152], P('mp', 'dp')
- project_bias_gradient: float32 [1152], replicated
- logit_peak: float32 [16], P('mp')
- clipped_query: float32 [1152, 1152], P('dp', 'mp')
- clipped_key: float32 [1152, 1152], P('dp', 'mp')
Inputs may be any that keep to these rules, and one draw needn't show every extreme that they name: `picture_start`: for each patch, the index in the whole array of the first patch of its picture. A picture is a run of consecutive patches inside one packed row of 2048 patches (rows begin at multiples of 2048); each picture has 100 to 1024 patches, and every row ends with one picture of exactly 1024 patches.
All inputs are finite; a program needn't handle non-finite values.
Results may differ from a plain program's by a relative error of at most 0.018.
Values may be sent and summed in bfloat16 or wider, within the bound.
A program may use at most 256 MiB of HBM per device.

v0:
```python
from functools import partial

import jax
import jax.numpy as jnp
from jax import lax
from jax.sharding import PartitionSpec as P

HEAD = 72
ROW = 2048


EPSILON = 1e-06
CLIP_LIMIT = 7.0
MASKED_SCORE = -1e30


def feature_sum(partial_rows):
    return lax.psum_scatter(partial_rows, "mp", scatter_dimension=0, tiled=True)


def full_rows(shares):
    return lax.all_gather(shares, "mp", axis=0, tiled=True)


def local_norm(values):
    centre = jnp.mean(values, axis=1, keepdims=True)
    centred = values - centre
    rstd = lax.rsqrt(jnp.mean(centred * centred, axis=1, keepdims=True) + EPSILON)
    return (centred * rstd, rstd)


def norm_backward(grad_normed, normed, rstd, gain):
    scaled = grad_normed * gain
    mean_grad = jnp.mean(scaled, axis=1, keepdims=True)
    mean_cross = jnp.mean(scaled * normed, axis=1, keepdims=True)
    return rstd * (scaled - mean_grad - normed * mean_cross)


def tile_bounds(starts, offset, block_rows):
    row_begin = offset // ROW * ROW
    leading = lax.dynamic_index_in_dim(starts, offset, keepdims=False) - starts[0]
    trailing = lax.dynamic_index_in_dim(starts, offset + block_rows - 1, keepdims=False)
    last_key = jnp.sum((starts <= trailing).astype(jnp.int32)) - 1
    return (row_begin, leading // block_rows, last_key // block_rows + 1)


def tile_scores(query_tile, query_starts, keys, starts, key_begin, block_rows, heads):
    key_tile = lax.dynamic_slice_in_dim(keys, key_begin, block_rows).reshape(
        block_rows, heads, HEAD
    )
    key_starts = lax.dynamic_slice_in_dim(starts, key_begin, block_rows)
    allowed = (query_starts[:, None] == key_starts[None, :])[None]
    scores = jnp.einsum(
        "qhd,khd->hqk", query_tile, key_tile, preferred_element_type=jnp.float32
    ) * HEAD ** (-0.5)
    return (jnp.where(allowed, scores, MASKED_SCORE), allowed, key_tile)


def attention_forward(queries, keys, values, starts):
    tokens, width = queries.shape
    heads = width // HEAD
    block_rows = min(512, ROW)

    def per_block(position, state):
        mixed, log_totals, peaks = state
        offset = position * block_rows
        row_begin, tile_low, tile_high = tile_bounds(starts, offset, block_rows)
        query_tile = lax.dynamic_slice_in_dim(queries, offset, block_rows).reshape(
            block_rows, heads, HEAD
        )
        query_starts = lax.dynamic_slice_in_dim(starts, offset, block_rows)

        def measure(tile_number, running):
            top_now, total_now = running
            scores, allowed, unused = tile_scores(
                query_tile,
                query_starts,
                keys,
                starts,
                row_begin + tile_number * block_rows,
                block_rows,
                heads,
            )
            top_new = jnp.maximum(top_now, jnp.max(scores, axis=2))
            fresh = jnp.sum(jnp.where(allowed, jnp.exp(scores - top_new[:, :, None]), 0.0), axis=2)
            return (top_new, total_now * jnp.exp(top_now - top_new) + fresh)

        top_rows, total_rows = lax.fori_loop(
            tile_low,
            tile_high,
            measure,
            (
                jnp.full((heads, block_rows), MASKED_SCORE, jnp.float32),
                jnp.zeros((heads, block_rows), jnp.float32),
            ),
        )
        log_total = top_rows + jnp.log(total_rows)

        def accumulate(tile_number, summed):
            key_begin = row_begin + tile_number * block_rows
            scores, allowed, unused = tile_scores(
                query_tile, query_starts, keys, starts, key_begin, block_rows, heads
            )
            weights = jnp.exp(scores - log_total[:, :, None]).astype(jnp.bfloat16)
            value_tile = lax.dynamic_slice_in_dim(values, key_begin, block_rows).reshape(
                block_rows, heads, HEAD
            )
            return summed + jnp.einsum(
                "hqk,khd->qhd", weights, value_tile, preferred_element_type=jnp.float32
            )

        summed = lax.fori_loop(
            tile_low, tile_high, accumulate, jnp.zeros((block_rows, heads, HEAD), jnp.float32)
        )
        mixed = lax.dynamic_update_slice_in_dim(mixed, summed.reshape(block_rows, width), offset, 0)
        log_totals = lax.dynamic_update_slice_in_dim(log_totals, log_total, offset, 1)
        peaks = jnp.maximum(peaks, jnp.max(top_rows, axis=1))
        return (mixed, log_totals, peaks)

    initial = (
        jnp.zeros((tokens, width), jnp.float32),
        jnp.zeros((heads, tokens), jnp.float32),
        jnp.full((heads,), MASKED_SCORE, jnp.float32),
    )
    return lax.fori_loop(0, tokens // block_rows, per_block, initial)


def attention_backward(queries, keys, values, starts, log_totals, grad_mixed):
    tokens, width = queries.shape
    heads = width // HEAD
    block_rows = min(512, ROW)

    def per_block(position, state):
        grad_keys, grad_values, grad_queries = state
        offset = position * block_rows
        row_begin, tile_low, tile_high = tile_bounds(starts, offset, block_rows)
        query_tile = lax.dynamic_slice_in_dim(queries, offset, block_rows).reshape(
            block_rows, heads, HEAD
        )
        query_starts = lax.dynamic_slice_in_dim(starts, offset, block_rows)
        grad_tile = lax.dynamic_slice_in_dim(grad_mixed, offset, block_rows).reshape(
            block_rows, heads, HEAD
        )
        log_total = lax.dynamic_slice_in_dim(log_totals, offset, block_rows, 1)

        def probe(tile_number):
            key_begin = row_begin + tile_number * block_rows
            scores, allowed, key_tile = tile_scores(
                query_tile, query_starts, keys, starts, key_begin, block_rows, heads
            )
            weights = jnp.exp(scores - log_total[:, :, None])
            value_tile = lax.dynamic_slice_in_dim(values, key_begin, block_rows).reshape(
                block_rows, heads, HEAD
            )
            grad_weights = jnp.einsum(
                "qhd,khd->hqk", grad_tile, value_tile, preferred_element_type=jnp.float32
            )
            return (key_begin, key_tile, weights, grad_weights)

        def settle(tile_number, delta):
            unused, unused_keys, weights, grad_weights = probe(tile_number)
            return delta + jnp.sum(weights * grad_weights, axis=2)

        delta = lax.fori_loop(
            tile_low, tile_high, settle, jnp.zeros((heads, block_rows), jnp.float32)
        )

        def spread(tile_number, running):
            grad_query, keys_running, values_running = running
            key_begin, key_tile, weights, grad_weights = probe(tile_number)
            grad_scores = (weights * (grad_weights - delta[:, :, None])).astype(jnp.bfloat16)
            grad_query = grad_query + jnp.einsum(
                "hqk,khd->qhd", grad_scores, key_tile, preferred_element_type=jnp.float32
            )
            key_part = jnp.einsum(
                "hqk,qhd->khd", grad_scores, query_tile, preferred_element_type=jnp.float32
            ).reshape(block_rows, width)
            value_part = jnp.einsum(
                "hqk,qhd->khd",
                weights.astype(jnp.bfloat16),
                grad_tile,
                preferred_element_type=jnp.float32,
            ).reshape(block_rows, width)
            keys_running = lax.dynamic_update_slice_in_dim(
                keys_running,
                lax.dynamic_slice_in_dim(keys_running, key_begin, block_rows) + key_part,
                key_begin,
                0,
            )
            values_running = lax.dynamic_update_slice_in_dim(
                values_running,
                lax.dynamic_slice_in_dim(values_running, key_begin, block_rows) + value_part,
                key_begin,
                0,
            )
            return (grad_query, keys_running, values_running)

        grad_query, grad_keys, grad_values = lax.fori_loop(
            tile_low,
            tile_high,
            spread,
            (jnp.zeros((block_rows, heads, HEAD), jnp.float32), grad_keys, grad_values),
        )
        grad_queries = lax.dynamic_update_slice_in_dim(
            grad_queries, grad_query.reshape(block_rows, width), offset, 0
        )
        return (grad_keys, grad_values, grad_queries)

    empty = jnp.zeros((tokens, width), jnp.float32)
    grad_keys, grad_values, grad_queries = lax.fori_loop(
        0, tokens // block_rows, per_block, (empty, empty, empty)
    )
    return (grad_queries * HEAD ** (-0.5), grad_keys * HEAD ** (-0.5), grad_values)


def body(
    inputs,
    picture_start,
    prenorm_gain,
    prenorm_shift,
    query_weight,
    query_bias,
    key_weight,
    value_weight,
    value_bias,
    output_weight,
    output_bias,
    midnorm_gain,
    midnorm_shift,
    hidden_weight,
    hidden_bias,
    project_weight,
    project_bias,
    cotangent,
):
    residual_in = inputs.astype(jnp.float32)
    normed_pre, rstd_pre = local_norm(residual_in)
    attn_in = lax.all_gather(
        (normed_pre * prenorm_gain + prenorm_shift).astype(jnp.bfloat16), "mp", axis=0, tiled=True
    )
    query_full, key_full, value_full, hidden_full = (
        lax.all_gather(query_weight, "dp", axis=0, tiled=True),
        lax.all_gather(key_weight, "dp", axis=0, tiled=True),
        lax.all_gather(value_weight, "dp", axis=0, tiled=True),
        lax.all_gather(hidden_weight, "dp", axis=0, tiled=True),
    )
    output_full, project_full = (
        lax.all_gather(output_weight, "dp", axis=1, tiled=True),
        lax.all_gather(project_weight, "dp", axis=1, tiled=True),
    )
    queries = (
        jnp.dot(attn_in, query_full, preferred_element_type=jnp.float32) + query_bias
    ).astype(jnp.bfloat16)
    keys = jnp.dot(attn_in, key_full, preferred_element_type=jnp.float32).astype(jnp.bfloat16)
    values = (jnp.dot(attn_in, value_full, preferred_element_type=jnp.float32) + value_bias).astype(
        jnp.bfloat16
    )
    mixed, log_totals, peaks = attention_forward(queries, keys, values, picture_start)
    mixed_low = mixed.astype(jnp.bfloat16)
    heads_rows = lax.all_to_all(mixed_low, "mp", split_axis=0, concat_axis=1, tiled=True)
    output_whole = lax.all_gather(output_full, "mp", axis=0, tiled=True)
    residual_mid = (
        residual_in
        + jnp.dot(heads_rows, output_whole, preferred_element_type=jnp.float32)
        + output_bias
    )
    normed_mid, rstd_mid = local_norm(residual_mid)
    mlp_in = lax.all_gather(
        (normed_mid * midnorm_gain + midnorm_shift).astype(jnp.bfloat16), "mp", axis=0, tiled=True
    )
    up_rows = jnp.dot(mlp_in, hidden_full, preferred_element_type=jnp.float32) + hidden_bias
    activated_value, gelu_pull = jax.vjp(partial(jax.nn.gelu, approximate=True), up_rows)
    activated = activated_value.astype(jnp.bfloat16)
    final_rows = (
        residual_mid
        + feature_sum(jnp.dot(activated, project_full, preferred_element_type=jnp.float32))
        + project_bias
    )
    layer_output = final_rows.astype(jnp.bfloat16)
    logit_peak = lax.pmax(peaks, "dp")
    factor = jnp.repeat(jnp.sqrt(CLIP_LIMIT / jnp.maximum(logit_peak, CLIP_LIMIT)), HEAD)
    clipped_query = query_weight.astype(jnp.float32) * factor[None, :]
    clipped_key = key_weight.astype(jnp.float32) * factor[None, :]
    grad_output = cotangent.astype(jnp.float32)
    grad_output_all = full_rows(cotangent)
    project_grad = jnp.einsum(
        "tf,td->fd", activated, grad_output_all, preferred_element_type=jnp.float32
    )
    grad_activated = jnp.einsum(
        "td,fd->tf", grad_output_all, project_full, preferred_element_type=jnp.float32
    )
    grad_up = gelu_pull(grad_activated)[0].astype(jnp.bfloat16)
    hidden_grad = jnp.einsum("td,tf->df", mlp_in, grad_up, preferred_element_type=jnp.float32)
    grad_mid = feature_sum(
        jnp.einsum("tf,df->td", grad_up, hidden_full, preferred_element_type=jnp.float32)
    )
    grad_resid = grad_output + norm_backward(grad_mid, normed_mid, rstd_mid, midnorm_gain)
    grad_branch = grad_resid.astype(jnp.bfloat16)
    grad_branch_all = full_rows(grad_branch)
    output_grad = jnp.einsum(
        "tc,td->cd", mixed_low, grad_branch_all, preferred_element_type=jnp.float32
    )
    grad_mixed = jnp.einsum(
        "td,cd->tc", grad_branch_all, output_full, preferred_element_type=jnp.float32
    ).astype(jnp.bfloat16)
    grad_queries, grad_keys, grad_values = attention_backward(
        queries, keys, values, picture_start, log_totals, grad_mixed
    )
    query_low = grad_queries.astype(jnp.bfloat16)
    key_low = grad_keys.astype(jnp.bfloat16)
    value_low = grad_values.astype(jnp.bfloat16)
    query_grad = jnp.einsum("td,tc->dc", attn_in, query_low, preferred_element_type=jnp.float32)
    key_grad = jnp.einsum("td,tc->dc", attn_in, key_low, preferred_element_type=jnp.float32)
    value_grad = jnp.einsum("td,tc->dc", attn_in, value_low, preferred_element_type=jnp.float32)
    grad_pre_rows = (
        jnp.einsum("tc,dc->td", query_low, query_full, preferred_element_type=jnp.float32)
        + jnp.einsum("tc,dc->td", key_low, key_full, preferred_element_type=jnp.float32)
        + jnp.einsum("tc,dc->td", value_low, value_full, preferred_element_type=jnp.float32)
    )
    grad_pre = feature_sum(grad_pre_rows)
    inputs_gradient = grad_resid + norm_backward(grad_pre, normed_pre, rstd_pre, prenorm_gain)
    query_part, key_part, value_part, hidden_part = (
        lax.psum_scatter(
            query_grad.astype(jnp.bfloat16), "dp", scatter_dimension=0, tiled=True
        ).astype(jnp.float32),
        lax.psum_scatter(
            key_grad.astype(jnp.bfloat16), "dp", scatter_dimension=0, tiled=True
        ).astype(jnp.float32),
        lax.psum_scatter(
            value_grad.astype(jnp.bfloat16), "dp", scatter_dimension=0, tiled=True
        ).astype(jnp.float32),
        lax.psum_scatter(
            hidden_grad.astype(jnp.bfloat16), "dp", scatter_dimension=0, tiled=True
        ).astype(jnp.float32),
    )
    output_part, project_part = (
        lax.psum_scatter(
            output_grad.astype(jnp.bfloat16), "dp", scatter_dimension=1, tiled=True
        ).astype(jnp.float32),
        lax.psum_scatter(
            project_grad.astype(jnp.bfloat16), "dp", scatter_dimension=1, tiled=True
        ).astype(jnp.float32),
    )
    head_parts = lax.psum(
        (
            jnp.sum(query_low.astype(jnp.float32), axis=0),
            jnp.sum(value_low.astype(jnp.float32), axis=0),
            jnp.sum(grad_up.astype(jnp.float32), axis=0),
        ),
        "dp",
    )
    norm_parts = lax.psum(
        (
            jnp.sum(grad_pre * normed_pre, axis=0),
            jnp.sum(grad_pre, axis=0),
            jnp.sum(grad_branch.astype(jnp.float32), axis=0),
            jnp.sum(grad_mid * normed_mid, axis=0),
            jnp.sum(grad_mid, axis=0),
            jnp.sum(grad_output, axis=0),
        ),
        ("dp", "mp"),
    )
    return (
        layer_output,
        inputs_gradient,
        norm_parts[0],
        norm_parts[1],
        query_part,
        head_parts[0],
        key_part,
        value_part,
        head_parts[1],
        output_part,
        norm_parts[2],
        norm_parts[3],
        norm_parts[4],
        hidden_part,
        head_parts[2],
        project_part,
        norm_parts[5],
        logit_peak,
        clipped_query,
        clipped_key,
    )


def solution(mesh):
    placed = (
        P(("dp", "mp"), None),
        P("dp"),
        P(),
        P(),
        P("dp", "mp"),
        P("mp"),
        P("dp", "mp"),
        P("dp", "mp"),
        P("mp"),
        P("mp", "dp"),
        P(),
        P(),
        P(),
        P("dp", "mp"),
        P("mp"),
        P("mp", "dp"),
        P(),
        P(("dp", "mp"), None),
    )
    return jax.shard_map(
        body,
        mesh=mesh,
        in_specs=placed,
        out_specs=(
            P(("dp", "mp"), None),
            P(("dp", "mp"), None),
            P(),
            P(),
            P("dp", "mp"),
            P("mp"),
            P("dp", "mp"),
            P("dp", "mp"),
            P("mp"),
            P("mp", "dp"),
            P(),
            P(),
            P(),
            P("dp", "mp"),
            P("mp"),
            P("mp", "dp"),
            P(),
            P("mp"),
            P("dp", "mp"),
            P("dp", "mp"),
        ),
        check_vma=False,
    )
```

profile of v0, /device:TPU:0, one launch (start us, length us, event | category | flops | bytes accessed | tf_op | source)
XLA Modules:
  0.0 1639.1 jit_solution(10249595136331657946)
XLA Ops:
  17.5 34.6 %all-gather.20.cloned.1.call-done = bf16[576,1152]{0,1:T(8,128)(2,1)} async-done(((bf16[576,72]{0,1:T(8,128)(2,1)}), bf16[576,1152]{0,1:T(8,128)(2,1)}) %all-gather.20.cloned.1.call-update) | async-done | bytes 1327120 | tf_op jit(solution)/shard_map/all_gather | solution.py:248
  57.2 35.1 %all-gather.16.cloned.1.call-done = bf16[1152,576]{1,0:T(8,128)(2,1)} async-done(((bf16[72,576]{1,0:T(8,128)(2,1)}), bf16[1152,576]{1,0:T(8,128)(2,1)}) %all-gather.16.cloned.1.call-update) | async-done | bytes 1327120 | tf_op jit(solution)/shard_map/all_gather | solution.py:243
  92.2 63.6 %all-gather.12.cloned.1.call-done = bf16[2048,1152]{1,0:T(8,128)(2,1)} async-done(((bf16[1024,1152]{1,0:T(8,128)(2,1)}), bf16[2048,1152]{1,0:T(8,128)(2,1)}) %all-gather.12.cloned.1.call-update) | async-done | bytes 4718608 | tf_op jit(solution)/shard_map/all_gather | solution.py:238
  161.9 35.1 %all-gather.14.cloned.1.call-done = bf16[1152,576]{1,0:T(8,128)(2,1)} async-done(((bf16[72,576]{1,0:T(8,128)(2,1)}), bf16[1152,576]{1,0:T(8,128)(2,1)}) %all-gather.14.cloned.1.call-update) | async-done | bytes 1327120 | tf_op jit(solution)/shard_map/all_gather | solution.py:242
  204.5 32.5 %all-gather.18.cloned.1.call-done = bf16[1152,576]{1,0:T(8,128)(2,1)} async-done(((bf16[72,576]{1,0:T(8,128)(2,1)}), bf16[1152,576]{1,0:T(8,128)(2,1)}) %all-gather.18.cloned.1.call-update) | async-done | bytes 1327120 | tf_op jit(solution)/shard_map/all_gather | solution.py:244
  245.2 158.3 %while.245 = (s32[]{:T(128)}, bf16[2048,576]{0,1:T(8,128)(2,1)}, f32[8,2048]{1,0:T(8,128)}, f32[8]{0:T(128)S(1)}, s32[2048]{0:T(1024)}, /*index=5*/bf16[2048,576...) while((s32[]{:T(128)}, bf16[2048,576]{0,1:T(8,128)(2,1)}, ...), condition=%wide.region_11.12_spmd.clone, body=%wide.region_2.11_spmd.clone.sunk | while | flops 931977280 | bytes 32011908 | solution.py:125
  264.2 18.5 %while.249 = (s32[]{:T(128)}, f32[512,8,72]{0,2,1:T(8,128)}, s32[]{:T(128)}, s32[]{:T(128)}, bf16[2048,576]{0,1:T(8,128)(2,1)}, /*index=5*/s32[512]{0:T(512)S(1)...) while((s32[]{:T(128)}, f32[512,8,72]{0,2,1:T(8,128)}, ...), condition=%wide.region_9.9_spmd, body=%wide.region_8.8_spmd.sunk | while | flops 612925440 | bytes 7037135 | solution.py:112
  303.8 18.5 %while.249 = (s32[]{:T(128)}, f32[512,8,72]{0,2,1:T(8,128)}, s32[]{:T(128)}, s32[]{:T(128)}, bf16[2048,576]{0,1:T(8,128)(2,1)}, /*index=5*/s32[512]{0:T(512)S(1)...) while((s32[]{:T(128)}, f32[512,8,72]{0,2,1:T(8,128)}, ...), condition=%wide.region_9.9_spmd, body=%wide.region_8.8_spmd.sunk | while | flops 612925440 | bytes 7037135 | solution.py:112
  343.3 18.5 %while.249 = (s32[]{:T(128)}, f32[512,8,72]{0,2,1:T(8,128)}, s32[]{:T(128)}, s32[]{:T(128)}, bf16[2048,576]{0,1:T(8,128)(2,1)}, /*index=5*/s32[512]{0:T(512)S(1)...) while((s32[]{:T(128)}, f32[512,8,72]{0,2,1:T(8,128)}, ...), condition=%wide.region_9.9_spmd, body=%wide.region_8.8_spmd.sunk | while | flops 612925440 | bytes 7037135 | solution.py:112
  382.8 18.5 %while.249 = (s32[]{:T(128)}, f32[512,8,72]{0,2,1:T(8,128)}, s32[]{:T(128)}, s32[]{:T(128)}, bf16[2048,576]{0,1:T(8,128)(2,1)}, /*index=5*/s32[512]{0:T(512)S(1)...) while((s32[]{:T(128)}, f32[512,8,72]{0,2,1:T(8,128)}, ...), condition=%wide.region_9.9_spmd, body=%wide.region_8.8_spmd.sunk | while | flops 612925440 | bytes 7037135 | solution.py:112
  413.1 28.0 %all-to-all-done = bf16[2,1024,576]{1,2,0:T(8,128)(2,1)} async-done(((bf16[2,1024,576]{1,2,0:T(8,128)(2,1)}), bf16[2,1024,576]{1,2,0:T(8,128)(2,1)}, u32[]{:S(2)}, u32[]{:S(2)}) %all-to-all-start) | async-done | bytes 2359328 | tf_op jit(solution)/shard_map/all_to_all | solution.py:260
  454.3 59.5 %all-gather.24.cloned.1.call-done = bf16[2048,1152]{1,0:T(8,128)(2,1)} async-done(((bf16[1024,1152]{1,0:T(8,128)(2,1)}), bf16[2048,1152]{1,0:T(8,128)(2,1)}) %all-gather.24.cloned.1.call-update) | async-done | bytes 4718608 | tf_op jit(solution)/shard_map/all_gather | solution.py:268
  513.8 18.3 %fusion.66 = f32[2048,2152]{0,1:T(8,128)} fusion(bf16[2048,1152]{1,0:T(8,128)(2,1)} %all-gather.24.cloned.1.call-done, bf16[1152,2152]{1,0:T(8,128)(2,1)} %all-gather.26.cloned.1.call-done), kind=kOutput, calls=%fused_computation.139 | convolution fusion | flops 10154409984 | bytes 27305984 | tf_op jit(solution)/shard_map/dot_general | solution.py:271
  532.1 45.9 %all-gather.30.cloned.1.call-done = bf16[2048,1152]{1,0:T(8,128)(2,1)} async-done(((bf16[1024,1152]{1,0:T(8,128)(2,1)}), bf16[2048,1152]{1,0:T(8,128)(2,1)}) %all-gather.30.cloned.1.call-update) | async-done | bytes 4718608 | tf_op jit(solution)/shard_map/all_gather | solution.py:22
  578.0 56.5 %all-gather.28.cloned.1.call-done = bf16[2152,1152]{0,1:T(8,128)(2,1)} async-done(((bf16[2152,72]{0,1:T(8,128)(2,1)}), bf16[2152,1152]{0,1:T(8,128)(2,1)}) %all-gather.28.cloned.1.call-update) | async-done | bytes 4958224 | tf_op jit(solution)/shard_map/all_gather | solution.py:249
  634.5 33.8 %convert_reduce_fusion.2 = (f32[2152]{0:T(1024)}, bf16[2048,2152]{0,1:T(8,128)(2,1)S(1)}, bf16[2048,2152]{0,1:T(8,128)(2,1)}) fusion(f32[2048,2152]{0,1:T(8,128)} %fusion.66, f32[2152]{0:T(1024)S(1)} %copy-done.35, bf16[2048,1152]{1,0:T(8,128)(2,1)} %all-gather.30.cloned.1.call-done, bf16[2152,1152]{0,1:T(8,128)(2,1)} %all-gather.28.cloned.1.call-done), kind=kOutput, calls=%fused_computation.68 | convolution fusion | flops 10264590336 | bytes 44952384 | tf_op jit(solution)/shard_map/td,fd->tf/dot_general | solution.py:289
  671.8 17.4 %fusion.68 = f32[2048,1152]{1,0:T(8,128)} fusion(bf16[2048,2152]{0,1:T(8,128)(2,1)S(1)} %get-tuple-element.1122, bf16[1152,2152]{1,0:T(8,128)(2,1)} %all-gather.26.cloned.1.call-done), kind=kOutput, calls=%fused_computation.141 | convolution fusion | flops 10154409984 | bytes 23209984 | tf_op jit(solution)/shard_map/tf,df->td/dot_general | solution.py:295
  689.2 18.9 %fusion.67 = f32[2048,1152]{1,0:T(8,128)} fusion(bf16[2048,2152]{0,1:T(8,128)(2,1)} %get-tuple-element.1143, bf16[2152,1152]{0,1:T(8,128)(2,1)} %all-gather.28.cloned.1.call-done), kind=kOutput, calls=%fused_computation.140 | convolution fusion | flops 10154409984 | bytes 23209984 | tf_op jit(solution)/shard_map/dot_general | solution.py:276
  708.2 90.3 %reduce-scatter.24.cloned.1.call-done = f32[1024,1152]{1,0:T(8,128)} async-done(((f32[2048,1152]{1,0:T(8,128)}), f32[1024,1152]{1,0:T(8,128)}) %reduce-scatter.24.cloned.1.call-update) | async-done | bytes 4718608 | tf_op jit(solution)/shard_map/reduce_scatter | solution.py:18
  803.9 107.5 %reduce-scatter.22.cloned.1.call-done = f32[1024,1152]{1,0:T(8,128)} async-done(((f32[2048,1152]{1,0:T(8,128)}), f32[1024,1152]{1,0:T(8,128)}) %reduce-scatter.22.cloned.1.call-update) | async-done | bytes 4718608 | tf_op jit(solution)/shard_map/reduce_scatter | solution.py:18
  954.8 28.6 %all-gather.32.cloned.1.call-done = bf16[2048,1152]{1,0:T(8,128)(2,1)} async-done(((bf16[1024,1152]{1,0:T(8,128)(2,1)}), bf16[2048,1152]{1,0:T(8,128)(2,1)}) %all-gather.32.cloned.1.call-update) | async-done | bytes 4718608 | tf_op jit(solution)/shard_map/all_gather | solution.py:22
  998.7 222.4 %while.242 = (s32[]{:T(128)}, f32[2048,576]{0,1:T(8,128)}, f32[2048,576]{0,1:T(8,128)}, f32[2048,576]{0,1:T(8,128)}, s32[2048]{0:T(1024)}, /*index=5*/bf16[2048,...) while((s32[]{:T(128)}, f32[2048,576]{0,1:T(8,128)}, ...), condition=%wide.region_25.26_spmd, body=%wide.region_18.0_spmd.sunk | while | flops 2146801664 | bytes 94533400 | solution.py:210
  1023.1 29.0 %while.247 = (s32[]{:T(128)}, f32[512,8,72]{0,2,1:T(8,128)}, f32[2048,576]{0,1:T(8,128)}, f32[2048,576]{0,1:T(8,128)}, s32[]{:T(128)}, /*index=5*/s32[]{:T(128)}...) while((s32[]{:T(128)}, f32[512,8,72]{0,2,1:T(8,128)}, ...), condition=%wide.region_24.24_spmd, body=%wide.region_23.23_spmd.sunk | while | flops 1532067840 | bytes 66388328 | solution.py:198
  1078.5 29.1 %while.247 = (s32[]{:T(128)}, f32[512,8,72]{0,2,1:T(8,128)}, f32[2048,576]{0,1:T(8,128)}, f32[2048,576]{0,1:T(8,128)}, s32[]{:T(128)}, /*index=5*/s32[]{:T(128)}...) while((s32[]{:T(128)}, f32[512,8,72]{0,2,1:T(8,128)}, ...), condition=%wide.region_24.24_spmd, body=%wide.region_23.23_spmd.sunk | while | flops 1532067840 | bytes 66388328 | solution.py:198
  1134.0 29.1 %while.247 = (s32[]{:T(128)}, f32[512,8,72]{0,2,1:T(8,128)}, f32[2048,576]{0,1:T(8,128)}, f32[2048,576]{0,1:T(8,128)}, s32[]{:T(128)}, /*index=5*/s32[]{:T(128)}...) while((s32[]{:T(128)}, f32[512,8,72]{0,2,1:T(8,128)}, ...), condition=%wide.region_24.24_spmd, body=%wide.region_23.23_spmd.sunk | while | flops 1532067840 | bytes 66388328 | solution.py:198
  1189.4 29.1 %while.247 = (s32[]{:T(128)}, f32[512,8,72]{0,2,1:T(8,128)}, f32[2048,576]{0,1:T(8,128)}, f32[2048,576]{0,1:T(8,128)}, s32[]{:T(128)}, /*index=5*/s32[]{:T(128)}...) while((s32[]{:T(128)}, f32[512,8,72]{0,2,1:T(8,128)}, ...), condition=%wide.region_24.24_spmd, body=%wide.region_23.23_spmd.sunk | while | flops 1532067840 | bytes 66388328 | solution.py:198
  1283.0 33.1 %pmax.7 = f32[8]{0:T(128)S(1)} all-reduce(f32[8]{0:T(128)S(1)} %copy-done.29), channel_id=1, replica_groups=mesh['dp'=16,'mp'=2] {'dp'}, use_global_device_ids=true, to_apply=%region_53.54 | all-reduce | flops 8 | bytes 64 | tf_op jit(solution)/shard_map/pmax | solution.py:280
  1326.5 57.8 %all-reduce.7 = (f32[576]{0:T(1024)}, f32[576]{0:T(1024)}, f32[2152]{0:T(1024)}) all-reduce(f32[576]{0:T(1024)S(1)} %convert_reduce_fusion.7, f32[576]{0:T(1024)S(1)} %convert_reduce_fusion.6, f32[2152]{0:T(1024)S(1)} %copy-done.30), channel_id=1, replica_groups=mesh['dp'=16,'mp'=2] {'dp'}, use_global_device_ids=true, to_apply=%region_35.36 | all-reduce | flops 3304 | bytes 26432 | tf_op jit(solution)/shard_map/psum | solution.py:344
  1387.5 21.5 %reduce-scatter.32.cloned.1.call-done = bf16[72,576]{1,0:T(8,128)(2,1)} async-done(((bf16[1152,576]{1,0:T(8,128)(2,1)}), bf16[72,576]{1,0:T(8,128)(2,1)}) %reduce-scatter.32.cloned.1.call-update) | async-done | bytes 82960
  1410.6 59.0 %reduce-scatter.34.cloned.1.call-done = bf16[576,72]{0,1:T(8,128)(2,1)} async-done(((bf16[576,1152]{0,1:T(8,128)(2,1)}), bf16[576,72]{0,1:T(8,128)(2,1)}) %reduce-scatter.34.cloned.1.call-update) | async-done | bytes 82960
  1471.2 110.2 %reduce-scatter.26.cloned.1.call-done = f32[1024,1152]{1,0:T(8,128)} async-done(((f32[2048,1152]{1,0:T(8,128)}), f32[1024,1152]{1,0:T(8,128)}) %reduce-scatter.26.cloned.1.call-update) | async-done | bytes 4718608 | tf_op jit(solution)/shard_map/reduce_scatter | solution.py:18
  1585.4 40.6 %all-reduce.6 = (f32[1152]{0:T(1024)}, f32[1152]{0:T(1024)}, f32[1152]{0:T(1024)}, f32[1152]{0:T(1024)}, f32[1152]{0:T(1024)}, /*index=5*/f32[1152]{0:T(1024)}) all-reduce(f32[1152]{0:T(1024)S(1)} %get-tuple-element.980, f32[1152]{0:T(1024)S(1)} %get-tuple-element.985, ...), channel_id=1, replica_groups=mesh['dp'=16,'mp'=2] {'dp','mp'}, use_global_device_ids=true, to_apply=%region_30.31 | all-reduce | flops 6912 | bytes 55296 | tf_op jit(solution)/shard_map/psum | solution.py:352
  (572 shorter events, 668.8 us)
Async XLA Ops:
  7.2 44.9 %all-gather.20.cloned.1.call-start = ((), (), s32[]{:S(2)}) async-start(), calls=%async_computation.14 | async-start | bytes 1566720 | tf_op jit(solution)/shard_map/all_gather | solution.py:248
  8.0 84.3 %all-gather.16.cloned.1.call-start = ((), (), s32[]{:S(2)}) async-start(), calls=%async_computation.12 | async-start | bytes 1566720 | tf_op jit(solution)/shard_map/all_gather | solution.py:243
  8.7 147.1 %all-gather.12.cloned.1.call-start = ((), (), s32[]{:S(2)}) async-start(), calls=%async_computation.10 | async-start | bytes 7077888 | tf_op jit(solution)/shard_map/all_gather | solution.py:238
  16.2 180.8 %all-gather.14.cloned.1.call-start = ((), (), s32[]{:S(2)}) async-start(), calls=%async_computation.11 | async-start | bytes 1566720 | tf_op jit(solution)/shard_map/all_gather | solution.py:242
  16.8 220.2 %all-gather.18.cloned.1.call-start = ((), (), s32[]{:S(2)}) async-start(), calls=%async_computation.13 | async-start | bytes 1566720 | tf_op jit(solution)/shard_map/all_gather | solution.py:244
  17.4 395.7 %all-gather.22.cloned.1.call-start = ((), (), s32[]{:S(2)}) async-start(), calls=%async_computation.15 | async-start | bytes 3981312 | tf_op jit(solution)/shard_map/all_gather | solution.py:261
  54.7 399.6 %all-gather.26.cloned.1.call-start = ((), (), s32[]{:S(2)}) async-start(), calls=%async_computation.17 | async-start | bytes 5326848 | tf_op jit(solution)/shard_map/all_gather | solution.py:245
  407.7 33.4 %all-to-all-start = ((bf16[2,1024,576]{1,2,0:T(8,128)(2,1)}), bf16[2,1024,576]{1,2,0:T(8,128)(2,1)}, u32[]{:S(2)}, u32[]{:S(2)}) async-start(bf16[2,1024,576]{1,2,0:T(8,128)(2,1)} %bitcast.238), calls=%async_computation | async-start | bytes 4718592 | tf_op jit(solution)/shard_map/all_to_all | solution.py:260
  412.6 101.2 %all-gather.24.cloned.1.call-start = ((), (), s32[]{:S(2)}) async-start(), calls=%async_computation.16 | async-start | bytes 7077888 | tf_op jit(solution)/shard_map/all_gather | solution.py:268
  452.9 125.1 %all-gather.30.cloned.1.call-start = ((), (), s32[]{:S(2)}) async-start(), calls=%async_computation.20 | async-start | bytes 7077888 | tf_op jit(solution)/shard_map/all_gather | solution.py:22
  453.6 180.9 %all-gather.28.cloned.1.call-start = ((), (), s32[]{:S(2)}) async-start(), calls=%async_computation.18 | async-start | bytes 5326848 | tf_op jit(solution)/shard_map/all_gather | solution.py:249
  454.2 180.3 %copy-start.35 = (f32[2152]{0:T(1024)S(1)}, f32[2152]{0:T(1024)}, u32[]{:S(2)}) copy-start(f32[2152]{0:T(1024)} %param.44) | copy-start | bytes 25828
  454.2 344.4 %reduce-scatter.24.cloned.1.call-start = ((), (), s32[]{:S(2)}) async-start(), calls=%async_computation.21 | async-start | bytes 14155776 | tf_op jit(solution)/shard_map/reduce_scatter | solution.py:18
  689.2 222.2 %reduce-scatter.22.cloned.1.call-start = ((), (), s32[]{:S(2)}) async-start(), calls=%async_computation.19 | async-start | bytes 14155776 | tf_op jit(solution)/shard_map/reduce_scatter | solution.py:18
  708.1 203.3 %copy-start.8 = (bf16[1024,1152]{1,0:T(8,128)(2,1)S(1)}, bf16[1024,1152]{1,0:T(8,128)(2,1)}, u32[]{:S(2)}) copy-start(bf16[1024,1152]{1,0:T(8,128)(2,1)} %param.47) | copy-start | bytes 7077892
  708.1 203.3 %copy-start.32 = (f32[1152]{0:T(1024)S(1)}, f32[1152]{0:T(1024)}, u32[]{:S(2)}) copy-start(f32[1152]{0:T(1024)} %param.46) | copy-start | bytes 13828
  708.2 275.2 %all-gather.32.cloned.1.call-start = ((), (), s32[]{:S(2)}) async-start(), calls=%async_computation.22 | async-start | bytes 7077888 | tf_op jit(solution)/shard_map/all_gather | solution.py:22
  920.6 396.5 %reduce-scatter.36.cloned.1.call-start = ((), (), s32[]{:S(2)}) async-start(), calls=%async_computation.28 | async-start | bytes 5326848
  937.7 381.3 %reduce-scatter.38.cloned.1.call-start = ((), (), s32[]{:S(2)}) async-start(), calls=%async_computation.29 | async-start | bytes 5326848
  954.7 429.6 %reduce-scatter.28.cloned.1.call-start = ((), (), s32[]{:S(2)}) async-start(), calls=%async_computation.24 | async-start | bytes 1566720
  1230.0 155.9 %reduce-scatter.30.cloned.1.call-start = ((), (), s32[]{:S(2)}) async-start(), calls=%async_computation.25 | async-start | bytes 1566720
  1238.9 170.1 %reduce-scatter.32.cloned.1.call-start = ((), (), s32[]{:S(2)}) async-start(), calls=%async_computation.26 | async-start | bytes 1566720
  1248.1 221.4 %reduce-scatter.34.cloned.1.call-start = ((), (), s32[]{:S(2)}) async-start(), calls=%async_computation.27 | async-start | bytes 1566720
  1255.6 325.7 %reduce-scatter.26.cloned.1.call-start = ((), (), s32[]{:S(2)}) async-start(), calls=%async_computation.23 | async-start | bytes 14155776 | tf_op jit(solution)/shard_map/reduce_scatter | solution.py:18
  1320.8 260.5 %copy-start.6 = (bf16[1024,1152]{1,0:T(8,128)(2,1)S(1)}, bf16[1024,1152]{1,0:T(8,128)(2,1)}, u32[]{:S(2)}) copy-start(bf16[1024,1152]{1,0:T(8,128)(2,1)} %param.30) | copy-start | bytes 7077892
  1320.8 260.5 %copy-start.18 = (f32[1024]{0:T(1024)S(1)}, f32[1024]{0:T(1024)}, u32[]{:S(2)}) copy-start(f32[1024]{0:T(1024)} %copy-done.17) | copy-start | bytes 12292
  1320.8 260.5 %copy-start.20 = (f32[1152]{0:T(1024)S(1)}, f32[1152]{0:T(1024)}, u32[]{:S(2)}) copy-start(f32[1152]{0:T(1024)} %param.32) | copy-start | bytes 13828
  1320.8 260.5 %copy-start.23 = (f32[1024]{0:T(1024)S(1)}, f32[1024]{0:T(1024)}, u32[]{:S(2)}) copy-start(f32[1024]{0:T(1024)} %copy-done.22) | copy-start | bytes 12292
  1326.4 259.0 %copy-start.24 = (f32[1152]{0:T(1024)S(1)}, f32[1152]{0:T(1024)}, u32[]{:S(2)}) copy-start(f32[1152]{0:T(1024)} %get-tuple-element.1123) | copy-start | bytes 13828
  1326.4 259.0 %copy-start.25 = (f32[1152]{0:T(1024)S(1)}, f32[1152]{0:T(1024)}, u32[]{:S(2)}) copy-start(f32[1152]{0:T(1024)} %get-tuple-element.1145) | copy-start | bytes 13828
  1326.4 259.0 %copy-start.26 = (f32[1152]{0:T(1024)S(1)}, f32[1152]{0:T(1024)}, u32[]{:S(2)}) copy-start(f32[1152]{0:T(1024)} %get-tuple-element.978) | copy-start | bytes 13828
  1326.5 259.0 %copy-start.27 = (f32[1152]{0:T(1024)S(1)}, f32[1152]{0:T(1024)}, u32[]{:S(2)}) copy-start(f32[1152]{0:T(1024)} %get-tuple-element.984) | copy-start | bytes 13828
  (74 other events, 589.1 us)
Sparse Core Ops, SparseCore 0:
  10.2 41.8 all-gather.19
  54.2 37.9 all-gather.15
  94.4 61.4 all-gather.11
  157.8 39.1 all-gather.13
  199.0 37.9 all-gather.17
  239.0 38.1 all-gather.21
  279.4 54.5 all-gather.25
  453.0 60.7 all-gather.23
  515.3 62.6 all-gather.29
  580.0 54.4 all-gather.27
  689.3 109.1 reduce-scatter.23
  800.7 110.6 reduce-scatter.21
  920.7 62.6 all-gather.31
  987.2 76.3 reduce-scatter.35
  1067.5 75.4 reduce-scatter.37
  1230.2 57.9 reduce-scatter.27
  1291.7 56.8 reduce-scatter.29
  1352.2 56.7 reduce-scatter.31
  1412.8 56.7 reduce-scatter.33
  1471.7 109.5 reduce-scatter.25
where the time goes:
time: 1650 us; the launch traced here: 1640 us
  waiting for transfers between devices  812 us (49%)
  matrix products  382 us (23%)
  local copies, waits for them, and re-layouts  144 us (9%)
  blocking collectives  132 us (8%)
  other arithmetic  128 us (8%)
  loops' own time  19.2 us (1%)
    reduce_scatter x3, waiting for transfers between devices, feature_sum(): return lax.psum_scatter(partial_rows, 'mp', scatter_dimension=0, tiled=True)  308 us
    unnamed x26, waiting for transfers between devices  84.9 us
    all_gather x2, waiting for transfers between devices, full_rows(): return lax.all_gather(shares, 'mp', axis=0, tiled=True)  74.5 us
    all_gather x1, waiting for transfers between devices, body(): lax.all_gather((normed_pre * prenorm_gain + prenorm_shift).astype(jnp.bfl...  63.6 us
    all_gather x1, waiting for transfers between devices, body(): lax.all_gather((normed_mid * midnorm_gain + midnorm_shift).astype(jnp.bfl...  59.5 us
    psum x1, blocking collectives, body(): lax.psum((jnp.sum(query_low.astype(jnp.float32), axis=0), jnp.sum(value_l...  57.8 us
    all_gather x1, waiting for transfers between devices, body(): lax.all_gather(project_weight, 'dp', axis=1, tiled=True)  56.5 us
    dot_general x16, matrix products, probe(): jnp.einsum('qhd,khd->hqk', grad_tile, value_tile, preferred_element_type=...  49.9 us
  transfers between devices with their start and end apart: 21, of which 15 were waited for; matrix products, arithmetic and copies ran while one was open for 35% of the time, Pallas kernels for 0%

commit v1 on v0

v1 whole, which is shorter than its diff:
```python
import math
from functools import partial

import jax
import jax.numpy as jnp
from jax import lax
from jax.experimental import pallas as pl
from jax.experimental.pallas import tpu as pltpu
from jax.sharding import PartitionSpec as P

HEAD = 72
HEADS = 16
ROW = 2048
HALF = 1024
EPSILON = 1e-06
CLIP_LIMIT = 7.0
MASKED_SCORE = -1e30
FEATURES = 16
PICTURES = 10
QUERY_BLOCK = 256
SCALE = HEAD ** (-0.5)
LOG2E = 1.0 / math.log(2.0)
EXPONENT = SCALE * LOG2E
F32 = jnp.float32
BF16 = jnp.bfloat16


def dot(left, right, left_dim=1, right_dim=0):
    return lax.dot_general(
        left, right, (((left_dim,), (right_dim,)), ((), ())), preferred_element_type=F32
    )


def split_terms(value, count):
    terms = []
    for _ in range(count):
        term = value.astype(BF16).astype(F32)
        terms.append(term)
        value = value - term
    return terms


def query_operand(query, features):
    pad = jnp.zeros((8, query.shape[1]), F32)
    high, low = split_terms(query.astype(F32) * EXPONENT, 2)
    return jnp.concatenate([high, pad, low, pad, features], axis=0).astype(BF16)


def key_operand(key, features):
    pad = jnp.zeros((8, key.shape[1]), F32)
    wide = key.astype(F32)
    stacked = jnp.concatenate([wide, pad, wide, pad, features], axis=0)
    return stacked.T.astype(BF16)


def rows_below(wide, extra):
    width = wide.shape[1]
    row = lax.broadcasted_iota(jnp.int32, (8, width), 0)
    block = jnp.zeros((8, width), F32)
    for position, line in enumerate(extra):
        block = jnp.where(row == position, line, block)
    return jnp.concatenate([wide, block], axis=0)


def forward_kernel(mask_ref, key_mask_ref, query_ref, key_ref, value_ref, mixed_ref, log_ref, top_ref):
    query_rows = query_operand(query_ref[0, 0], mask_ref[...])
    key_rows = key_operand(key_ref[0, 0], key_mask_ref[...])
    value_rows = rows_below(value_ref[0, 0].astype(F32), [jnp.ones((1, 1), F32)]).astype(BF16)
    for begin in range(0, HALF, QUERY_BLOCK):
        block = slice(begin, begin + QUERY_BLOCK)
        scores = dot(key_rows, query_rows[:, block])
        top = jnp.max(scores, axis=0, keepdims=True)
        weights = jnp.exp2(scores - top).astype(BF16)
        summed = dot(value_rows, weights)
        total = summed[HEAD : HEAD + 1]
        mixed_ref[0, :, block] = (summed[:HEAD] / total).astype(BF16)
        log_ref[0, :, block] = top + jnp.log2(total)
        top_ref[0, :, block] = top


def backward_kernel(
    mask_ref, key_mask_ref, query_ref, key_ref, value_ref, mixed_ref, log_ref, grad_ref, out_ref
):
    query, key = query_ref[0, 0], key_ref[0, 0]
    grad = grad_ref[0]
    row = lax.broadcasted_iota(jnp.int32, (FEATURES, HALF), 0)
    features = mask_ref[...]
    for position, term in enumerate(split_terms(-log_ref[0], 3)):
        features = jnp.where(row == PICTURES + position, term, features)
    query_rows = query_operand(query, features)
    key_rows = key_operand(key, key_mask_ref[...])
    grad_wide = grad.astype(F32)
    delta = jnp.sum(grad_wide * mixed_ref[0].astype(F32), axis=0, keepdims=True)
    grad_rows = rows_below(grad_wide, split_terms(-delta, 2)).astype(BF16)
    one = jnp.ones((1, 1), F32)
    value_rows = rows_below(value_ref[0, 0].astype(F32), [one, one]).T.astype(BF16)
    query_cols = query.astype(F32).T.astype(BF16)
    grad_cols = grad_wide.T.astype(BF16)
    grad_key = jnp.zeros((HALF, HEAD), F32)
    grad_value = jnp.zeros((HALF, HEAD), F32)
    for begin in range(0, HALF, QUERY_BLOCK):
        block = slice(begin, begin + QUERY_BLOCK)
        weights = jnp.exp2(dot(key_rows, query_rows[:, block]))
        slopes = dot(value_rows, grad_rows[:, block])
        grad_scores = (weights * slopes).astype(BF16)
        grad_value = grad_value + dot(weights.astype(BF16), grad_cols[block])
        grad_key = grad_key + dot(grad_scores, query_cols[block])
        out_ref[0, 0, :, block] = (dot(key, grad_scores) * SCALE).astype(BF16)
    out_ref[1, 0] = (grad_key * SCALE).T.astype(BF16)
    out_ref[2, 0] = grad_value.T.astype(BF16)


def head_specs():
    features = pl.BlockSpec((FEATURES, HALF), lambda h: (0, 0))
    part = [pl.BlockSpec((1, 1, HEAD, HALF), lambda h, i=i: (i, h, 0, 0)) for i in range(3)]
    head = pl.BlockSpec((1, HEAD, HALF), lambda h: (h, 0, 0))
    line = pl.BlockSpec((1, 1, HALF), lambda h: (h, 0, 0))
    return features, part, head, line


def attention_forward(masks, stacked):
    heads = stacked.shape[1]
    features, part, head, line = head_specs()
    area = heads * HALF * HALF
    return pl.pallas_call(
        forward_kernel,
        grid=(heads,),
        in_specs=[features, features, *part],
        out_specs=(head, line, line),
        out_shape=(
            jax.ShapeDtypeStruct((heads, HEAD, HALF), BF16),
            jax.ShapeDtypeStruct((heads, 1, HALF), F32),
            jax.ShapeDtypeStruct((heads, 1, HALF), F32),
        ),
        cost_estimate=pl.CostEstimate(
            flops=area * 2 * 256 * 2, bytes_accessed=heads * HALF * HEAD * 8, transcendentals=area
        ),
        name="attention_forward",
    )(*masks, stacked, stacked, stacked)


def attention_backward(masks, stacked, mixed, logs, grads):
    heads = stacked.shape[1]
    features, part, head, line = head_specs()
    area = heads * HALF * HALF
    return pl.pallas_call(
        backward_kernel,
        grid=(heads,),
        in_specs=[features, features, *part, head, line, head],
        out_specs=pl.BlockSpec((3, 1, HEAD, HALF), lambda h: (0, h, 0, 0)),
        out_shape=jax.ShapeDtypeStruct((3, heads, HEAD, HALF), BF16),
        cost_estimate=pl.CostEstimate(
            flops=area * 2 * 256 * 5, bytes_accessed=heads * HALF * HEAD * 16, transcendentals=area
        ),
        name="attention_backward",
    )(*masks, stacked, stacked, stacked, mixed, logs, grads)


def picture_masks(starts):
    before = jnp.concatenate([starts[:1], starts[:-1]])
    changes = (starts != before).astype(F32)
    place = lax.iota(jnp.int32, HALF)
    number = jnp.sum(jnp.where(place[:, None] <= place[None, :], changes[:, None], 0.0), axis=0)
    row = lax.broadcasted_iota(jnp.int32, (FEATURES, HALF), 0)
    same = row.astype(F32) == number[None, :]
    listed = row < PICTURES
    mask = jnp.where(listed & ~same, MASKED_SCORE, 0.0)
    key_mask = jnp.where(listed, same.astype(F32), (row < PICTURES + 3).astype(F32))
    return mask, key_mask


def local_norm(values):
    centre = jnp.mean(values, axis=1, keepdims=True)
    centred = values - centre
    rstd = lax.rsqrt(jnp.mean(centred * centred, axis=1, keepdims=True) + EPSILON)
    return centred * rstd, rstd


def norm_backward(grad_normed, normed, rstd, gain):
    scaled = grad_normed * gain
    mean_grad = jnp.mean(scaled, axis=1, keepdims=True)
    mean_cross = jnp.mean(scaled * normed, axis=1, keepdims=True)
    return rstd * (scaled - mean_grad - normed * mean_cross)


def gelu_parts(rows):
    cubic = math.sqrt(2.0 / math.pi) * (rows + 0.044715 * rows * rows * rows)
    bend = jnp.tanh(cubic)
    value = 0.5 * rows * (1.0 + bend)
    slope = 0.5 * (1.0 + bend) + 0.5 * rows * (1.0 - bend * bend) * (
        math.sqrt(2.0 / math.pi) * (1.0 + 3.0 * 0.044715 * rows * rows)
    )
    return value, slope


def total(parts):
    out = parts[0]
    for part in parts[1:]:
        out = out + part
    return out


def body(
    inputs,
    picture_start,
    prenorm_gain,
    prenorm_shift,
    query_weight,
    query_bias,
    key_weight,
    value_weight,
    value_bias,
    output_weight,
    output_bias,
    midnorm_gain,
    midnorm_shift,
    hidden_weight,
    hidden_bias,
    project_weight,
    project_bias,
    cotangent,
    *,
    dp,
    mp,
):
    tokens, width = inputs.shape
    shard = query_weight.shape[1]
    hidden = hidden_weight.shape[1]
    group = HALF // tokens
    me = lax.axis_index("mp")
    groups = [list(range(i, i + group)) for i in range(0, mp, group)]

    def gather(weight):
        whole = lax.all_gather(weight, ("mp", "dp"), axis=0, tiled=True)
        return whole.reshape(mp, width, weight.shape[1])

    def scatter(parts):
        columns = parts[0].shape[1]
        lanes = -columns % 256
        whole = jnp.concatenate([part.astype(BF16) for part in parts], axis=0)
        whole = jnp.pad(whole, ((0, 0), (0, lanes)))
        mine = lax.psum_scatter(whole, ("mp", "dp"), scatter_dimension=0, tiled=True)
        return mine[:, :columns].astype(F32)

    def to_heads(part):
        kinds = part.shape[0]
        if group == 1:
            return part
        part = part.reshape(kinds, group, HEADS // group, HEAD, tokens).transpose(1, 0, 2, 3, 4)
        part = lax.all_to_all(part, "mp", 0, 0, axis_index_groups=groups, tiled=True)
        return part.transpose(1, 2, 3, 0, 4).reshape(kinds, HEADS // group, HEAD, HALF)

    def from_heads(part):
        kinds = part.shape[0]
        if group == 1:
            return part
        part = part.reshape(kinds, HEADS // group, HEAD, group, tokens).transpose(3, 0, 1, 2, 4)
        part = lax.all_to_all(part, "mp", 0, 0, axis_index_groups=groups, tiled=True)
        return part.transpose(1, 0, 2, 3, 4).reshape(kinds, HEADS, HEAD, tokens)

    query_bias_all, value_bias_all, hidden_bias_all = (
        lax.all_gather(item, "mp", axis=0, tiled=False)
        for item in (query_bias, value_bias, hidden_bias)
    )
    half = me // group
    starts = lax.dynamic_slice_in_dim(picture_start, half * HALF, HALF)
    masks = picture_masks(starts)

    attn_weights = gather(jnp.concatenate([query_weight, key_weight, value_weight], axis=1))
    output_all = gather(output_weight.T)
    hidden_all = gather(hidden_weight)
    project_all = gather(project_weight.T)

    residual_in = inputs.astype(F32)
    normed_pre, rstd_pre = local_norm(residual_in)
    attn_in = (normed_pre * prenorm_gain + prenorm_shift).astype(BF16)

    stacks = []
    for j in range(mp):
        bias = jnp.concatenate(
            [query_bias_all[j], jnp.zeros((shard,), F32), value_bias_all[j]], axis=0
        )
        rows = (dot(attn_weights[j], attn_in, 0, 1) + bias[:, None]).astype(BF16)
        stacks.append(rows.reshape(3, shard // HEAD, HEAD, tokens))
    if group == 1:
        pieces = stacks
    else:
        pieces = [to_heads(jnp.concatenate(stacks, axis=1))]
    mixed_pieces, log_pieces, tops = [], [], []
    for piece in pieces:
        mixed_piece, log_piece, top_piece = attention_forward(masks, piece)
        mixed_pieces.append(mixed_piece)
        log_pieces.append(log_piece)
        tops.append(jnp.max(top_piece, axis=(1, 2)))
    peak_here = jnp.concatenate(tops) / LOG2E
    if group == 1:
        mixed = [piece.reshape(shard, tokens) for piece in mixed_pieces]
    else:
        rows = from_heads(mixed_pieces[0][None])[0].reshape(mp, shard, tokens)
        mixed = [rows[j] for j in range(mp)]
        spread = jnp.full((HEADS,), MASKED_SCORE, F32)
        peak_here = lax.dynamic_update_slice_in_dim(
            spread, peak_here, (me % group) * (HEADS // group), 0
        )
    peak_all = lax.pmax(peak_here, ("dp", "mp"))
    logit_peak = lax.dynamic_slice_in_dim(peak_all, me * (HEADS // mp), HEADS // mp)
    factor = jnp.repeat(jnp.sqrt(CLIP_LIMIT / jnp.maximum(logit_peak, CLIP_LIMIT)), HEAD)
    clipped_query = query_weight.astype(F32) * factor[None, :]
    clipped_key = key_weight.astype(F32) * factor[None, :]

    residual_mid = (
        residual_in + total([dot(mixed[j], output_all[j], 0, 1) for j in range(mp)]) + output_bias
    )
    normed_mid, rstd_mid = local_norm(residual_mid)
    mlp_in = (normed_mid * midnorm_gain + midnorm_shift).astype(BF16)
    activated, slopes = [], []
    for j in range(mp):
        value, slope = gelu_parts(dot(mlp_in, hidden_all[j]) + hidden_bias_all[j])
        activated.append(value.astype(BF16))
        slopes.append(slope.astype(BF16))
    project_parts = [dot(cotangent, activated[j], 0, 0) for j in range(mp)]
    project_grad = scatter(project_parts)
    grad_up = [
        (dot(cotangent, project_all[j]) * slopes[j].astype(F32)).astype(BF16) for j in range(mp)
    ]
    hidden_grad = scatter([dot(mlp_in, grad_up[j], 0, 0) for j in range(mp)])
    final_rows = (
        residual_mid
        + total([dot(activated[j], project_all[j], 1, 1) for j in range(mp)])
        + project_bias
    )
    layer_output = final_rows.astype(BF16)

    grad_output = cotangent.astype(F32)
    grad_mid = total([dot(grad_up[j], hidden_all[j], 1, 1) for j in range(mp)])
    grad_resid = grad_output + norm_backward(grad_mid, normed_mid, rstd_mid, midnorm_gain)
    grad_branch = grad_resid.astype(BF16)
    output_grad = scatter([dot(grad_branch, mixed[j], 0, 1) for j in range(mp)])
    grad_mixed = [
        dot(output_all[j], grad_branch, 0, 1).astype(BF16).reshape(shard // HEAD, HEAD, tokens)
        for j in range(mp)
    ]
    if group > 1:
        grad_mixed = [to_heads(jnp.concatenate(grad_mixed, axis=0)[None])[0]]
    grad_pieces = [
        attention_backward(masks, piece, mixed_piece, log_piece, grads)
        for piece, mixed_piece, log_piece, grads in zip(
            pieces, mixed_pieces, log_pieces, grad_mixed
        )
    ]
    if group > 1:
        whole = from_heads(grad_pieces[0]).reshape(3, mp, shard // HEAD, HEAD, tokens)
        grad_pieces = [whole[:, j] for j in range(mp)]
    grad_rows = [piece.reshape(3 * shard, tokens) for piece in grad_pieces]
    attn_grad = scatter([dot(attn_in, grad_rows[j], 0, 1) for j in range(mp)])
    grad_pre = total([dot(grad_rows[j], attn_weights[j], 0, 1) for j in range(mp)])
    inputs_gradient = grad_resid + norm_backward(grad_pre, normed_pre, rstd_pre, prenorm_gain)

    row_sums = [jnp.sum(rows.astype(F32), axis=1) for rows in grad_rows]
    head_parts = (
        jnp.stack([sums[:shard] for sums in row_sums]),
        jnp.stack([sums[2 * shard :] for sums in row_sums]),
        jnp.stack([jnp.sum(part.astype(F32), axis=0) for part in grad_up]),
    )
    norm_parts = (
        jnp.sum(grad_pre * normed_pre, axis=0),
        jnp.sum(grad_pre, axis=0),
        jnp.sum(grad_branch.astype(F32), axis=0),
        jnp.sum(grad_mid * normed_mid, axis=0),
        jnp.sum(grad_mid, axis=0),
        jnp.sum(grad_output, axis=0),
    )
    flat = jnp.concatenate([item.reshape(-1) for item in (*head_parts, *norm_parts)])
    flat = lax.psum(flat, ("dp", "mp"))
    ends = [mp * shard, mp * shard, mp * hidden] + [width] * 6
    sums, at = [], 0
    for size in ends:
        sums.append(flat[at : at + size])
        at += size
    query_bias_grad, value_bias_grad, hidden_bias_grad = (
        lax.dynamic_index_in_dim(item.reshape(mp, -1), me, keepdims=False) for item in sums[:3]
    )
    return (
        layer_output,
        inputs_gradient,
        sums[3],
        sums[4],
        attn_grad[:, :shard],
        query_bias_grad,
        attn_grad[:, shard : 2 * shard],
        attn_grad[:, 2 * shard :],
        value_bias_grad,
        output_grad.T,
        sums[5],
        sums[6],
        sums[7],
        hidden_grad,
        hidden_bias_grad,
        project_grad.T,
        sums[8],
        logit_peak,
        clipped_query,
        clipped_key,
    )


def solution(mesh):
    rows = P(("dp", "mp"), None)
    split = P("dp", "mp")
    turned = P("mp", "dp")
    heads = P("mp")
    whole = P()
    placed = (
        rows, P("dp"), whole, whole, split, heads, split, split, heads, turned, whole, whole, whole,
        split, heads, turned, whole, rows,
    )
    given = (
        rows, rows, whole, whole, split, heads, split, split, heads, turned, whole, whole, whole,
        split, heads, turned, whole, heads, split, split,
    )
    return jax.shard_map(
        partial(body, dp=mesh.shape["dp"], mp=mesh.shape["mp"]),
        mesh=mesh,
        in_specs=placed,
        out_specs=given,
        check_vma=False,
    )
```

time: 1650 us -> 955 us (0.58)
  waiting for transfers between devices: 812 us -> 363 us
  matrix products: 382 us -> 230 us
  Pallas kernels: 0 us -> 102 us
  other arithmetic: 128 us -> 43.2 us
  local copies, waits for them, and re-layouts: 144 us -> 98.4 us
  blocking collectives: 132 us -> 91.3 us
  loops' own time: 19.2 us -> 0 us
    reduce_scatter x3 -> x0, waiting for transfers between devices: 308 us -> none  [feature_sum(): return lax.psum_scatter(partial_rows, 'mp', scatter_dimension=0, tiled=True)]
    all_gather x11 -> x4, waiting for transfers between devices: 392 us -> 184 us  [gather(): whole = lax.all_gather(weight, ('mp', 'dp'), axis=0, tiled=True)]
    dot_general x90 -> x24, matrix products: 382 us -> 230 us  [dot(): lax.dot_general(left, right, (((left_dim,), (right_dim,)), ((), ())), pre...]
    pallas_call x0 -> x4, Pallas kernels: none -> 102 us  [the longest x2 51.6 us: attention_forward(): pl.pallas_call(forward_kernel, grid=(heads,), in_specs=[features, feature...]
    unnamed x26 -> x12, waiting for transfers between devices: 84.9 us -> 178 us
    dynamic_slice x100 -> x4, local copies, waits for them, and re-layouts: 94 us -> 2.54 us  [the longest x3 1.85 us: body(): lax.dynamic_index_in_dim(item.reshape(mp, -1), me, keepdims=False)]
    psum x2 -> x1, blocking collectives: 98.4 us -> 41.2 us  [body(): flat = lax.psum(flat, ('dp', 'mp'))]
    unnamed x74 -> x105, local copies, waits for them, and re-layouts: 6.3 us -> 59.5 us
  transfers between devices with their start and end apart: 21 -> 8, of which waited for: 15 -> 6; matrix products, arithmetic and copies ran while one was open for 35% -> 30% of each run, Pallas kernels for 0% -> 11%
where the time goes in v1:
time: 955 us; the launch traced here: 944 us
  waiting for transfers between devices  363 us (38%)
  matrix products  230 us (24%)
  Pallas kernels  102 us (11%)
  local copies, waits for them, and re-layouts  98.4 us (10%)
  blocking collectives  91.3 us (10%)
  other arithmetic  43.2 us (5%)
  between operations  16.5 us (2%)
    dot_general x24, matrix products, dot(): lax.dot_general(left, right, (((left_dim,), (right_dim,)), ((), ())), pre...  230 us
    all_gather x4, waiting for transfers between devices, gather(): whole = lax.all_gather(weight, ('mp', 'dp'), axis=0, tiled=True)  184 us
    unnamed x12, waiting for transfers between devices  178 us
    unnamed x105, local copies, waits for them, and re-layouts  59.5 us
    pallas_call x2, Pallas kernels, attention_forward(): pl.pallas_call(forward_kernel, grid=(heads,), in_specs=[features, feature...  51.6 us
    pallas_call x2, Pallas kernels, attention_backward(): pl.pallas_call(backward_kernel, grid=(heads,), in_specs=[features, featur...  50 us
    psum x1, blocking collectives, body(): flat = lax.psum(flat, ('dp', 'mp'))  41.2 us
    pmax x1, blocking collectives, body(): peak_all = lax.pmax(peak_here, ('dp', 'mp'))  39.8 us
  transfers between devices with their start and end apart: 8, of which 6 were waited for; matrix products, arithmetic and copies ran while one was open for 30% of the time, Pallas kernels for 11%

profile of v1, /device:TPU:0, one launch (start us, length us, event | category | flops | bytes accessed | tf_op | source)
XLA Modules:
  0.0 943.9 jit_solution(10318280450000734407)
XLA Ops:
  17.8 10.3 %all-reduce.7 = (f32[1152]{0:T(1024)S(1)}, f32[1152]{0:T(1024)S(1)}, f32[4304]{0:T(1024)S(1)}) all-reduce(f32[1152]{0:T(1024)S(1)} %dynamic-update-slice, f32[1152]{0:T(1024)S(1)} %dynamic-update-slice.1, f32[4304]{0:T(1024)S(1)} %dynamic-update-slice.2), channel_id=2, replica_groups=mesh['dp'=16,'mp'=2] {'mp'}, use_global_device_ids=true, to_apply=%add.4 | all-reduce | flops 6608 | bytes 52864
  33.6 57.3 %all-gather.8.cloned.1.call-done = bf16[2304,1728]{1,0:T(8,128)(2,1)} async-done(((bf16[72,1728]{1,0:T(8,128)(2,1)}), bf16[2304,1728]{1,0:T(8,128)(2,1)}) %all-gather.8.cloned.1.call-update) | async-done | bytes 7962640 | tf_op jit(solution)/shard_map/all_gather | solution.py:234
  90.9 9.3 add_convert_fusion.1
  100.2 25.6 %attention_forward.2 = (bf16[8,72,1024]{2,1,0:T(8,128)(2,1)}, f32[8,1,1024]{2,1,0:T(1,128)}, f32[8,1,1024]{2,1,0:T(1,128)}) custom-call(f32[16,1024]{1,0:T(8,128)} %get-tuple-element.131.mask_ref, f32[16,1024]{1,0:T(8,128)} %get-tuple-element.130.key_mask_ref, bf16[3,8,72,1024]{3,2,1,0:T(8,128)(2,1)} %bitcast.66, bf16[3,8,72,1024]{3,2,1,0:T(8,128)(2,1)} %bitcast.67, ...), custom_call_target="tpu_custom_call" | custom-call | flops 8589934592 | bytes 4718592 | tf_op jit(solution)/shard_map/attention_forward/pallas_call | solution.py:125
  125.8 25.3 %all-gather.10.cloned.1.call-done = bf16[2304,576]{1,0:T(8,128)(2,1)} async-done(((bf16[72,576]{1,0:T(8,128)(2,1)}), bf16[2304,576]{1,0:T(8,128)(2,1)}) %all-gather.10.cloned.1.call-update) | async-done | bytes 2654224 | tf_op jit(solution)/shard_map/all_gather | solution.py:234
  164.8 26.0 %attention_forward.3 = (bf16[8,72,1024]{2,1,0:T(8,128)(2,1)}, f32[8,1,1024]{2,1,0:T(1,128)}, f32[8,1,1024]{2,1,0:T(1,128)}) custom-call(f32[16,1024]{1,0:T(8,128)} %get-tuple-element.131.mask_ref, f32[16,1024]{1,0:T(8,128)} %get-tuple-element.130.key_mask_ref, bf16[3,8,72,1024]{3,2,1,0:T(8,128)(2,1)} %bitcast.72, bf16[3,8,72,1024]{3,2,1,0:T(8,128)(2,1)} %bitcast.73, ...), custom_call_target="tpu_custom_call" | custom-call | flops 8589934592 | bytes 4718592 | tf_op jit(solution)/shard_map/attention_forward/pallas_call | solution.py:125
  200.8 36.0 %all-gather.12.cloned.1.call-done = bf16[2304,2152]{1,0:T(8,128)(2,1)} async-done(((bf16[72,2152]{1,0:T(8,128)(2,1)}), bf16[2304,2152]{1,0:T(8,128)(2,1)}) %all-gather.12.cloned.1.call-update) | async-done | bytes 9916432 | tf_op jit(solution)/shard_map/all_gather | solution.py:234
  236.8 11.2 %fusion.41 = f32[1024,2152]{0,1:T(8,128)} fusion(bf16[1024,1152]{1,0:T(8,128)(2,1)} %add_convert_fusion.3, bf16[2304,2152]{1,0:T(8,128)(2,1)} %all-gather.12.cloned.1.call-done), kind=kOutput, calls=%fused_computation.78 | convolution fusion | flops 5077204992 | bytes 16187392 | tf_op jit(solution)/shard_map/dot_general | solution.py:29
  256.4 65.7 %all-gather.14.cloned.1.call-done = bf16[2304,2152]{1,0:T(8,128)(2,1)} async-done(((bf16[72,2152]{1,0:T(8,128)(2,1)}), bf16[2304,2152]{1,0:T(8,128)(2,1)}) %all-gather.14.cloned.1.call-update) | async-done | bytes 9916432 | tf_op jit(solution)/shard_map/all_gather | solution.py:234
  322.1 17.0 %convert_reduce_fusion.1 = (f32[2152]{0:T(1024)}, bf16[1024,2152]{0,1:T(8,128)(2,1)S(1)}) fusion(f32[1024,2152]{0,1:T(8,128)} %fusion.41, f32[2152]{0:T(1024)S(1)} %get-tuple-element.121, bf16[1024,1152]{1,0:T(8,128)(2,1)} %param.35, bf16[2304,2152]{1,0:T(8,128)(2,1)} %all-gather.14.cloned.1.call-done), kind=kOutput, calls=%fused_computation.27 | convolution fusion | flops 5130090496 | bytes 20611904 | tf_op jit(solution)/shard_map/dot_general | solution.py:29
  339.2 12.4 %fusion.39 = f32[1024,1152]{1,0:T(8,128)} fusion(bf16[1024,2152]{0,1:T(8,128)(2,1)S(1)} %get-tuple-element.141, bf16[2304,2152]{1,0:T(8,128)(2,1)} %all-gather.12.cloned.1.call-done), kind=kOutput, calls=%fused_computation.76 | convolution fusion | flops 5077204992 | bytes 14139392 | tf_op jit(solution)/shard_map/dot_general | solution.py:29
  351.6 17.8 %convert_reduce_fusion = (f32[2152]{0:T(1024)}, bf16[1024,2152]{0,1:T(8,128)(2,1)}) fusion(f32[1024,2152]{0,1:T(8,128)} %fusion.34, f32[2152]{0:T(1024)S(1)} %get-tuple-element.120, bf16[1024,1152]{1,0:T(8,128)(2,1)S(1)} %copy-done.3, bf16[2304,2152]{1,0:T(8,128)(2,1)} %all-gather.14.cloned.1.call-done), kind=kOutput, calls=%fused_computation.26 | convolution fusion | flops 5130090496 | bytes 20611904 | tf_op jit(solution)/shard_map/dot_general | solution.py:29
  369.4 13.1 %multiply_reduce_fusion = (f32[1152]{0:T(1024)}, f32[1024]{0:T(1024)S(1)}, f32[1024]{0:T(1024)S(1)}, f32[1152]{0:T(1024)}, f32[1024,1152]{1,0:T(8,128)S(1)}) fusion(f32[1024,1152]{1,0:T(8,128)S(1)} %bitcast.55, f32[1024]{0:T(1024)S(1)} %add_rsqrt_fusion, f32[1024]{0:T(1024)S(1)} %broadcast_multiply_fusion.4, f32[1152]{0:T(1024)S(1)} %copy-done.15, ...), kind=kOutput, calls=%fused_computation.59 | convolution fusion | flops 5088997376 | bytes 23606784 | tf_op jit(solution)/shard_map/dot_general | solution.py:29
  405.7 25.1 %attention_backward.3 = bf16[3,8,72,1024]{3,2,1,0:T(8,128)(2,1)} custom-call(f32[16,1024]{1,0:T(8,128)} %get-tuple-element.131.mask_ref, f32[16,1024]{1,0:T(8,128)} %get-tuple-element.130.key_mask_ref, bf16[3,8,72,1024]{3,2,1,0:T(8,128)(2,1)} %bitcast.75, bf16[3,8,72,1024]{3,2,1,0:T(8,128)(2,1)} %bitcast.76, bf16[3,8,72,1024]{3,2,1,0:T(8,128)(2,1)} %bitcast.77, ...), custom_call_target="tpu_custom_call" | custom-call | flops 21474836480 | bytes 9437184 | tf_op jit(solution)/shard_map/attention_backward/pallas_call | solution.py:146
  430.8 9.8 %convolution_convert_fusion.4 = bf16[1152,1728]{0,1:T(8,128)(2,1)} fusion(bf16[1728,1024]{1,0:T(8,128)(2,1)} %bitcast.58, bf16[1024,1152]{1,0:T(8,128)(2,1)S(1)} %copy-done.1, f32[1152]{0:T(1024)S(1)} %copy-done.30, f32[1152]{0:T(1024)S(1)} %copy-done.22, f32[1024]{0:T(1024)S(1)} %add_rsqrt_fusion.1, f32[1024]{0:T(1024)S(1)} %broadcast_multiply_fusion.5), kind=kOutput, calls=%fused_computation.33 | convolution fusion | flops 4085932032 | bytes 9896960 | tf_op jit(solution)/shard_map/dot_general | solution.py:29
  443.4 24.9 %attention_backward.2 = bf16[3,8,72,1024]{3,2,1,0:T(8,128)(2,1)} custom-call(f32[16,1024]{1,0:T(8,128)} %get-tuple-element.131.mask_ref, f32[16,1024]{1,0:T(8,128)} %get-tuple-element.130.key_mask_ref, bf16[3,8,72,1024]{3,2,1,0:T(8,128)(2,1)} %bitcast.69, bf16[3,8,72,1024]{3,2,1,0:T(8,128)(2,1)} %bitcast.70, bf16[3,8,72,1024]{3,2,1,0:T(8,128)(2,1)} %bitcast.71, ...), custom_call_target="tpu_custom_call" | custom-call | flops 21474836480 | bytes 9437184 | tf_op jit(solution)/shard_map/attention_backward/pallas_call | solution.py:146
  468.3 9.5 %convolution_convert_fusion.5 = bf16[1152,1728]{0,1:T(8,128)(2,1)} fusion(bf16[1728,1024]{1,0:T(8,128)(2,1)} %bitcast.60, bf16[1024,1152]{1,0:T(8,128)(2,1)S(1)} %copy-done.1, f32[1152]{0:T(1024)S(1)} %copy-done.30, f32[1152]{0:T(1024)S(1)} %copy-done.22, f32[1024]{0:T(1024)S(1)} %add_rsqrt_fusion.1, f32[1024]{0:T(1024)S(1)} %broadcast_multiply_fusion.5), kind=kOutput, calls=%fused_computation.34 | convolution fusion | flops 4085932032 | bytes 9896960 | tf_op jit(solution)/shard_map/dot_general | solution.py:29
  484.9 11.8 %copy.68 = bf16[2304,1728]{1,0:T(8,128)(2,1)} copy(bf16[2304,1728]{0,1:T(8,128)(2,1)} %pad_maximum_fusion.2) | data formatting | bytes 15925248
  524.9 14.3 %copy.70 = bf16[2304,2152]{1,0:T(8,128)(2,1)} copy(bf16[2304,2152]{0,1:T(8,128)(2,1)} %pad_maximum_fusion) | data formatting | bytes 19832832
  539.2 9.1 pad.17.clone
  548.9 13.1 %fusion.1 = bf16[1152,2152]{0,1:T(8,128)(2,1)S(1)} fusion(bf16[1024,1152]{1,0:T(8,128)(2,1)} %param.35, f32[1024,2152]{0,1:T(8,128)} %fusion.34, f32[2152]{0:T(1024)S(1)} %copy-done.17), kind=kOutput, calls=%fused_computation.11 | convolution fusion | flops 5101720576 | bytes 16140704 | tf_op jit(solution)/shard_map/dot_general | solution.py:29
  562.0 10.9 %fusion = bf16[1152,2152]{0,1:T(8,128)(2,1)S(1)} fusion(bf16[1024,1152]{1,0:T(8,128)(2,1)S(1)} %copy-done.4, f32[1024,2152]{0,1:T(8,128)} %fusion.41, f32[2152]{0:T(1024)S(1)} %copy-done.19), kind=kOutput, calls=%fused_computation.10 | convolution fusion | flops 5101720576 | bytes 16140704 | tf_op jit(solution)/shard_map/dot_general | solution.py:29
  577.3 14.1 %copy.71 = bf16[2304,2152]{1,0:T(8,128)(2,1)} copy(bf16[2304,2152]{0,1:T(8,128)(2,1)} %pad_maximum_fusion.1) | data formatting | bytes 19832832
  591.3 8.7 pad.18.clone
  601.2 39.8 %pmax.7 = f32[16]{0:T(128)S(1)} all-reduce(f32[16]{0:T(128)S(1)} %maximum_multiply_fusion), channel_id=1, replica_groups=mesh['dp'=16,'mp'=2] {'dp','mp'}, use_global_device_ids=true, to_apply=%region_26.27 | all-reduce | flops 16 | bytes 128 | tf_op jit(solution)/shard_map/pmax | solution.py:305
  648.4 8.7 fusion.45
  657.2 10.9 %fusion.28 = (f32[1152]{0:T(1024)S(1)}, f32[1024]{0:T(1024)S(1)}, f32[1024]{0:T(1024)S(1)}, f32[1152]{0:T(1024)S(1)}, f32[1024,1152]{1,0:T(8,128)}) fusion(bf16[1024,1152]{1,0:T(8,128)(2,1)S(1)} %copy-done.1, f32[1024]{0:T(1024)S(1)} %add_rsqrt_fusion.1, f32[1024]{0:T(1024)S(1)} %broadcast_multiply_fusion.5, f32[1152]{0:T(1024)S(1)} %copy-done.22, ...), kind=kOutput, calls=%fused_computation.56 | convolution fusion | flops 4089835520 | bytes 19494400 | tf_op jit(solution)/shard_map/dot_general | solution.py:29
  668.1 41.2 %psum.7 = f32[13520]{0:T(1024)S(1)} all-reduce(f32[13520]{0:T(1024)S(1)} %concatenate.34), channel_id=1, replica_groups=mesh['dp'=16,'mp'=2] {'dp','mp'}, use_global_device_ids=true, to_apply=%region_19.20 | all-reduce | flops 13520 | bytes 108160 | tf_op jit(solution)/shard_map/psum | solution.py:374
  718.4 16.7 %fusion.37 = f32[1024,1152]{1,0:T(8,128)} fusion(bf16[2304,2152]{1,0:T(8,128)(2,1)} %all-gather.14.cloned.1.call-done, f32[1024,2152]{0,1:T(8,128)} %fusion.41, f32[2152]{0:T(1024)S(1)} %copy-done.19), kind=kOutput, calls=%fused_computation.74 | convolution fusion | flops 5099241472 | bytes 18555296 | tf_op jit(solution)/shard_map/dot_general | solution.py:29
  735.2 14.5 %add_convert_fusion.2 = bf16[1024,1152]{1,0:T(8,128)(2,1)} fusion(f32[1024,1152]{1,0:T(8,128)S(1)} %bitcast.57, f32[1024,1152]{1,0:T(8,128)} %fusion.37, bf16[2304,2152]{1,0:T(8,128)(2,1)} %all-gather.14.cloned.1.call-done, f32[1152]{0:T(1024)S(1)} %copy-done.31, f32[1024,2152]{0,1:T(8,128)S(1)} %bitcast.85, f32[2152]{0:T(1024)S(1)} %copy-done.17), kind=kOutput, calls=%fused_computation.62 | convolution fusion | flops 5103960064 | bytes 25637792 | tf_op jit(solution)/shard_map/dot_general | solution.py:29
  755.4 31.3 %reduce-scatter.17.cloned.1.call-done = bf16[72,2304]{1,0:T(8,128)(2,1)} async-done(((bf16[2304,2304]{1,0:T(8,128)(2,1)}), bf16[72,2304]{1,0:T(8,128)(2,1)}) %reduce-scatter.17.cloned.1.call-update) | async-done | bytes 331792
  789.1 144.9 %reduce-scatter.19.cloned.1.call-done = bf16[72,2304]{1,0:T(8,128)(2,1)} async-done(((bf16[2304,2304]{1,0:T(8,128)(2,1)}), bf16[72,2304]{1,0:T(8,128)(2,1)}) %reduce-scatter.19.cloned.1.call-update) | async-done | bytes 331792
  (204 shorter events, 141.2 us)
Async XLA Ops:
  7.2 24.8 %copy-start.1 = (bf16[1024,1152]{1,0:T(8,128)(2,1)S(1)}, bf16[1024,1152]{1,0:T(8,128)(2,1)}, u32[]{:S(2)}) copy-start(bf16[1024,1152]{1,0:T(8,128)(2,1)} %param.18) | copy-start | bytes 7077892
  7.2 83.7 %copy-start.30 = (f32[1152]{0:T(1024)S(1)}, f32[1152]{0:T(1024)}, u32[]{:S(2)}) copy-start(f32[1152]{0:T(1024)} %param.21) | copy-start | bytes 13828
  7.2 83.7 %copy-start.22 = (f32[1152]{0:T(1024)S(1)}, f32[1152]{0:T(1024)}, u32[]{:S(2)}) copy-start(f32[1152]{0:T(1024)} %param.20) | copy-start | bytes 13828
  7.2 83.7 %all-gather.8.cloned.1.call-start = ((), (), s32[]{:S(2)}) async-start(), calls=%async_computation.4 | async-start | bytes 8515584 | tf_op jit(solution)/shard_map/all_gather | solution.py:234
  9.2 141.8 %all-gather.10.cloned.1.call-start = ((), (), s32[]{:S(2)}) async-start(), calls=%async_computation.5 | async-start | bytes 3041280 | tf_op jit(solution)/shard_map/all_gather | solution.py:234
  10.0 226.8 %all-gather.12.cloned.1.call-start = ((), (), s32[]{:S(2)}) async-start(), calls=%async_computation.6 | async-start | bytes 10340352 | tf_op jit(solution)/shard_map/all_gather | solution.py:234
  10.7 311.4 %all-gather.14.cloned.1.call-start = ((), (), s32[]{:S(2)}) async-start(), calls=%async_computation.7 | async-start | bytes 10340352 | tf_op jit(solution)/shard_map/all_gather | solution.py:234
  11.3 738.4 %reduce-scatter.15.cloned.1.call-start = ((), (), s32[]{:S(2)}) async-start(), calls=%async_computation.9 | async-start | bytes 3649536
  32.9 289.3 %copy-start.18 = (f32[2152]{0:T(1024)}, f32[2152]{0:T(1024)S(1)}, u32[]{:S(2)}) copy-start(f32[2152]{0:T(1024)S(1)} %get-tuple-element.121) | copy-start | bytes 25828
  32.9 318.7 %copy-start.16 = (f32[2152]{0:T(1024)}, f32[2152]{0:T(1024)S(1)}, u32[]{:S(2)}) copy-start(f32[2152]{0:T(1024)S(1)} %get-tuple-element.120) | copy-start | bytes 25828
  164.8 26.0 %copy-start.29 = (f32[1152]{0:T(1024)S(1)}, f32[1152]{0:T(1024)}, u32[]{:S(2)}) copy-start(f32[1152]{0:T(1024)} %param.28) | copy-start | bytes 13828
  236.8 11.2 %copy-start.5 = (bf16[1024,1152]{1,0:T(8,128)(2,1)S(1)}, bf16[1024,1152]{1,0:T(8,128)(2,1)}, u32[]{:S(2)}) copy-start(bf16[1024,1152]{1,0:T(8,128)(2,1)} %add_convert_fusion.3) | copy-start | bytes 7077892
  236.8 11.2 %copy-start.26 = (bf16[2304,2152]{1,0:T(8,128)(2,1)S(1)}, bf16[2304,2152]{1,0:T(8,128)(2,1)}, u32[]{:S(2)}) copy-start(bf16[2304,2152]{1,0:T(8,128)(2,1)} %all-gather.12.cloned.1.call-done) | copy-start | bytes 29749252
  339.2 12.4 %copy-start.34 = (bf16[1024,2152]{0,1:T(8,128)(2,1)}, bf16[1024,2152]{0,1:T(8,128)(2,1)S(1)}, u32[]{:S(2)}) copy-start(bf16[1024,2152]{0,1:T(8,128)(2,1)S(1)} %get-tuple-element.141) | copy-start | bytes 13221892
  339.2 12.4 %copy-start.3 = (bf16[1024,1152]{1,0:T(8,128)(2,1)S(1)}, bf16[1024,1152]{1,0:T(8,128)(2,1)}, u32[]{:S(2)}) copy-start(bf16[1024,1152]{1,0:T(8,128)(2,1)} %param.35) | copy-start | bytes 7077892
  339.2 30.2 %slice-start = ((s8[4718592]{0:T(1024)(128)(4,1)}), s8[4194304]{0:T(1024)(128)(4,1)S(1)}, s32[]{:S(2)}) async-start(s8[4718592]{0:T(1024)(128)(4,1)} %bitcast.54), calls=%async_computation.12 | async-start | bytes 8388608
  351.6 17.8 %slice-start.1 = ((s8[4718592]{0:T(1024)(128)(4,1)}), s8[524288]{0:T(1024)(128)(4,1)S(1)}, s32[]{:S(2)}) async-start(s8[4718592]{0:T(1024)(128)(4,1)} %bitcast.54), calls=%async_computation.13 | async-start | bytes 1048576
  400.8 350.8 %reduce-scatter.13.cloned.1.call-start = ((), (), s32[]{:S(2)}) async-start(), calls=%async_computation.8 | async-start | bytes 8515584
  503.9 282.8 %reduce-scatter.17.cloned.1.call-start = ((), (), s32[]{:S(2)}) async-start(), calls=%async_computation.10 | async-start | bytes 10948608
  548.2 13.8 %copy-start.19 = (f32[2152]{0:T(1024)S(1)}, f32[2152]{0:T(1024)}, u32[]{:S(2)}) copy-start(f32[2152]{0:T(1024)} %copy-done.18) | copy-start | bytes 25828
  548.3 385.8 %reduce-scatter.19.cloned.1.call-start = ((), (), s32[]{:S(2)}) async-start(), calls=%async_computation.11 | async-start | bytes 10948608
  548.9 13.1 %copy-start.4 = (bf16[1024,1152]{1,0:T(8,128)(2,1)S(1)}, bf16[1024,1152]{1,0:T(8,128)(2,1)}, u32[]{:S(2)}) copy-start(bf16[1024,1152]{1,0:T(8,128)(2,1)} %param.35) | copy-start | bytes 7077892
  600.0 41.7 %copy-start.9 = (bf16[72,576]{1,0:T(8,128)(2,1)S(1)}, bf16[72,576]{1,0:T(8,128)(2,1)}, u32[]{:S(2)}) copy-start(bf16[72,576]{1,0:T(8,128)(2,1)} %param.22) | copy-start | bytes 248836
  600.0 41.7 %copy-start.10 = (bf16[72,576]{1,0:T(8,128)(2,1)S(1)}, bf16[72,576]{1,0:T(8,128)(2,1)}, u32[]{:S(2)}) copy-start(bf16[72,576]{1,0:T(8,128)(2,1)} %param.24) | copy-start | bytes 248836
  600.0 48.2 %copy-start.21 = (f32[2152]{0:T(1024)S(1)}, f32[2152]{0:T(1024)}, u32[]{:S(2)}) copy-start(f32[2152]{0:T(1024)} %get-tuple-element.138) | copy-start | bytes 25828
  600.0 48.2 %copy-start.20 = (f32[2152]{0:T(1024)S(1)}, f32[2152]{0:T(1024)}, u32[]{:S(2)}) copy-start(f32[2152]{0:T(1024)} %get-tuple-element.140) | copy-start | bytes 25828
  712.2 23.0 %slice-start.2 = ((s8[4718592]{0:T(1024)(128)(4,1)}), s8[4194304]{0:T(1024)(128)(4,1)S(1)}, s32[]{:S(2)}) async-start(s8[4718592]{0:T(1024)(128)(4,1)} %bitcast.56), calls=%async_computation.14 | async-start | bytes 8388608
  712.2 23.0 %slice-start.4 = ((s8[8814592]{0:T(1024)(128)(4,1)}), s8[4194304]{0:T(1024)(128)(4,1)S(1)}, s32[]{:S(2)}) async-start(s8[8814592]{0:T(1024)(128)(4,1)} %bitcast.84), calls=%async_computation.16 | async-start | bytes 8388608
  718.4 16.8 %slice-start.3 = ((s8[4718592]{0:T(1024)(128)(4,1)}), s8[524288]{0:T(1024)(128)(4,1)S(1)}, s32[]{:S(2)}) async-start(s8[4718592]{0:T(1024)(128)(4,1)} %bitcast.56), calls=%async_computation.15 | async-start | bytes 1048576
  718.4 16.8 %copy-start.31 = (f32[1152]{0:T(1024)S(1)}, f32[1152]{0:T(1024)}, u32[]{:S(2)}) copy-start(f32[1152]{0:T(1024)} %param.34) | copy-start | bytes 13828
  718.4 16.8 %slice-start.5 = ((s8[8814592]{0:T(1024)(128)(4,1)}), s8[4194304]{0:T(1024)(128)(4,1)S(1)}, s32[]{:S(2)}) async-start(s8[8814592]{0:T(1024)(128)(4,1)} %bitcast.84), calls=%async_computation.17 | async-start | bytes 8388608
  718.4 16.8 %slice-start.6 = ((s8[8814592]{0:T(1024)(128)(4,1)}), s8[425984]{0:T(1024)(128)(4,1)S(1)}, s32[]{:S(2)}) async-start(s8[8814592]{0:T(1024)(128)(4,1)} %bitcast.84), calls=%async_computation.18 | async-start | bytes 851968
  (18 other events, 103.8 us)
Sparse Core Ops, SparseCore 0:
  11.5 79.3 all-gather.7
  93.7 57.3 all-gather.9
  153.9 82.8 all-gather.11
  239.5 82.5 all-gather.13
  401.0 101.9 reduce-scatter.14
  508.7 130.9 reduce-scatter.12
  645.7 140.9 reduce-scatter.16
  792.8 141.1 reduce-scatter.18

commit v2 on v1

--- a/solution.py
+++ b/solution.py
@@ -169,6 +169,250 @@
     return mask, key_mask
 
 
+LINE = 4
+SEAM = 40
+MESH = pl.DeviceIdType.MESH
+
+
+def place_of():
+    at, y = lax.axis_index("dp"), lax.axis_index("mp")
+    return at // 4, (at // 2) % 2, y, at % 2
+
+
+def device_of(z, x, y, core):
+    return ((z * 2 + x) * 2 + core, y)
+
+
+def neighbours(z, x, y, core):
+    return (
+        device_of(z, x, y, 1 - core), device_of(z, 1 - x, y, core), device_of(z, x, 1 - y, core)
+    )
+
+
+def enter(z, x, y, core):
+    barrier = pltpu.get_barrier_semaphore()
+    for device in neighbours(z, x, y, core):
+        pl.semaphore_signal(barrier, inc=1, device_id=device, device_id_type=MESH)
+
+    @pl.when(z > 0)
+    def _():
+        pl.semaphore_signal(barrier, inc=1, device_id=device_of(z - 1, x, y, core), device_id_type=MESH)
+
+    @pl.when(z < LINE - 1)
+    def _():
+        pl.semaphore_signal(barrier, inc=1, device_id=device_of(z + 1, x, y, core), device_id_type=MESH)
+
+    pl.semaphore_wait(barrier, 3 + jnp.where(z > 0, 1, 0) + jnp.where(z < LINE - 1, 1, 0))
+
+
+def gather_kernel(count, *refs):
+    shards, wholes = refs[:count], refs[count : 2 * count]
+    own_sem, z_send, z_recv, side_send, side_recv, core_send, core_recv = refs[2 * count :]
+    z, x, y, core = place_of()
+    rows = shards[0].shape[0]
+    parts = (pl.ds(0, SEAM), pl.ds(SEAM, rows - SEAM))
+    other, across_x, across_y = neighbours(z, x, y, core)
+
+    def spot(a, zz, xx, yy, part=None):
+        view = wholes[a].at[yy, (zz * 2 + xx) * 2 + core]
+        return view if part is None else view.at[parts[part]]
+
+    def along_z(a, zz, upward, source):
+        return pltpu.make_async_remote_copy(
+            spot(a, zz, x, y), spot(a, zz, x, y),
+            z_send.at[a, zz, 1 if upward else 0], z_recv.at[a, zz],
+            device_of(source + (1 if upward else -1), x, y, core), MESH,
+        )
+
+    def sideways(a, half, stage, zz, flip):
+        first = half == 0
+        over_x = first == (stage == 0)
+        xx = x if over_x else (1 - x if flip else x)
+        yy = y if not over_x else (1 - y if flip else y)
+        block = spot(a, zz, xx, yy, half)
+        slot = zz * 2 + (1 if flip else 0)
+        return pltpu.make_async_remote_copy(
+            block, block, side_send.at[a, half, stage, slot], side_recv.at[a, half, stage, slot],
+            across_x if over_x else across_y, MESH,
+        )
+
+    def arrival(a, half, stage, zz, flip):
+        first = half == 0
+        over_x = first == (stage == 0)
+        xx = 1 - x if over_x else (1 - x if flip else x)
+        yy = 1 - y if not over_x else (1 - y if flip else y)
+        block = spot(a, zz, xx, yy, half)
+        slot = zz * 2 + (1 if flip else 0)
+        return pltpu.make_async_remote_copy(
+            block, block, side_send.at[a, half, stage, slot], side_recv.at[a, half, stage, slot],
+            across_x if over_x else across_y, MESH,
+        )
+
+    def hand_over(a, half, zz, fx, fy):
+        xx = 1 - x if fx else x
+        yy = 1 - y if fy else y
+        block = spot(a, zz, xx, yy, half)
+        slot = zz * 4 + (2 if fx else 0) + (1 if fy else 0)
+        return pltpu.make_async_remote_copy(
+            block, block, core_send.at[a, half, slot], core_recv.at[a, half, slot], other, MESH
+        )
+
+    def handed(a, half, zz, fx, fy):
+        xx = 1 - x if fx else x
+        yy = 1 - y if fy else y
+        block = wholes[a].at[yy, (zz * 2 + xx) * 2 + 1 - core].at[parts[half]]
+        slot = zz * 4 + (2 if fx else 0) + (1 if fy else 0)
+        return pltpu.make_async_remote_copy(
+            block, block, core_send.at[a, half, slot], core_recv.at[a, half, slot], other, MESH
+        )
+
+    def launch_line_block(a, zz):
+        for half in range(2):
+            sideways(a, half, 0, zz, False).start()
+            sideways(a, half, 1, zz, False).start()
+            hand_over(a, half, zz, False, False).start()
+
+    def stage_begin(a):
+        own = pltpu.make_async_copy(shards[a], spot(a, z, x, y), own_sem.at[a])
+        own.start()
+        own.wait()
+
+        @pl.when(z < LINE - 1)
+        def _():
+            along_z(a, z, True, z).start()
+
+        @pl.when(z > 0)
+        def _():
+            along_z(a, z, False, z).start()
+
+        launch_line_block(a, z)
+
+    def stage_hop(a, hop):
+        @pl.when(z >= hop)
+        def _():
+            origin = z - hop
+            along_z(a, origin, True, z - 1).wait_recv()
+
+            @pl.when(z < LINE - 1)
+            def _():
+                along_z(a, origin, True, z).start()
+
+            launch_line_block(a, origin)
+
+        @pl.when(z < LINE - hop)
+        def _():
+            origin = z + hop
+            along_z(a, origin, False, z + 1).wait_recv()
+
+            @pl.when(z > 0)
+            def _():
+                along_z(a, origin, False, z).start()
+
+            launch_line_block(a, origin)
+
+    def stage_turn(a):
+        for zz in range(LINE):
+            for half in range(2):
+                arrival(a, half, 0, zz, False).wait_recv()
+                sideways(a, half, 1, zz, True).start()
+                hand_over(a, half, zz, half == 0, half == 1).start()
+
+    def stage_last(a):
+        for zz in range(LINE):
+            for half in range(2):
+                arrival(a, half, 1, zz, False).wait_recv()
+                hand_over(a, half, zz, half == 1, half == 0).start()
+                arrival(a, half, 1, zz, True).wait_recv()
+                hand_over(a, half, zz, True, True).start()
+
+    def stage_close(a):
+        for zz in range(LINE):
+            for half in range(2):
+                for fx in (False, True):
+                    for fy in (False, True):
+                        handed(a, half, zz, fx, fy).wait_recv()
+                        hand_over(a, half, zz, fx, fy).wait_send()
+                sideways(a, half, 0, zz, False).wait_send()
+                sideways(a, half, 1, zz, False).wait_send()
+                sideways(a, half, 1, zz, True).wait_send()
+
+            @pl.when(jnp.logical_and(z >= zz, z < LINE - 1))
+            def _():
+                along_z(a, zz, True, z).wait_send()
+
+            @pl.when(jnp.logical_and(z <= zz, z > 0))
+            def _():
+                along_z(a, zz, False, z).wait_send()
+
+    enter(z, x, y, core)
+    stages = [
+        stage_begin, partial(stage_hop, hop=1), partial(stage_hop, hop=2), partial(stage_hop, hop=3),
+        stage_turn, stage_last, stage_close,
+    ]
+    for step in range(len(stages) + count - 1):
+        for a in range(count):
+            if 0 <= step - a < len(stages):
+                stages[step - a](a)
+
+
+def gather_blocks(shards, mp):
+    count, rows = len(shards), shards[0].shape[0]
+    dp = 16
+    anywhere = pl.BlockSpec(memory_space=pl.ANY)
+    dma = pltpu.SemaphoreType.DMA
+    sent = sum(item.size * 2 for item in shards) * 15
+    wholes = pl.pallas_call(
+        partial(gather_kernel, count),
+        in_specs=[anywhere] * count,
+        out_specs=[anywhere] * count,
+        out_shape=[jax.ShapeDtypeStruct((mp, dp, rows, item.shape[1]), BF16) for item in shards],
+        scratch_shapes=[
+            dma((count,)), dma((count, LINE, 2)), dma((count, LINE)), dma((count, 2, 2, 8)),
+            dma((count, 2, 2, 8)), dma((count, 2, 16)), dma((count, 2, 16)),
+        ],
+        compiler_params=pltpu.CompilerParams(collective_id=0, has_side_effects=True),
+        cost_estimate=pl.CostEstimate(flops=0, bytes_accessed=sent, transcendentals=0),
+        name="gather_blocks",
+    )(*shards)
+    return [whole.reshape(mp, dp * rows, whole.shape[-1]) for whole in wholes]
+
+
+def gradient_kernel(count, left_ref, *refs):
+    rights, out_ref = refs[:count], refs[count]
+    columns = rights[0].shape[0]
+    for j in range(count):
+
+        @pl.when(pl.program_id(0) == j)
+        def _():
+            out_ref[0, :, :columns] = dot(left_ref[...], rights[j][...], 1, 1).astype(BF16)
+
+    if columns < out_ref.shape[2]:
+        extra = out_ref.shape[2] - columns
+        out_ref[0, :, columns:] = jnp.zeros((out_ref.shape[1], extra), BF16)
+
+
+def weight_gradient(left, rights, lanes):
+    width, tokens = left.shape
+    count, columns = len(rights), rights[0].shape[0]
+    padded = columns + -columns % lanes
+    tile = 384
+    whole = lambda j, m: (0, 0)
+    return pl.pallas_call(
+        partial(gradient_kernel, count),
+        grid=(count, width // tile),
+        in_specs=[pl.BlockSpec((tile, tokens), lambda j, m: (m, 0))]
+        + [pl.BlockSpec((columns, tokens), whole)] * count,
+        out_specs=pl.BlockSpec((1, tile, padded), lambda j, m: (j, m, 0)),
+        out_shape=jax.ShapeDtypeStruct((count, width, padded), BF16),
+        cost_estimate=pl.CostEstimate(
+            flops=2 * width * tokens * columns * count,
+            bytes_accessed=2 * count * (width * padded + columns * tokens) + 2 * width * tokens,
+            transcendentals=0,
+        ),
+        name="weight_gradient",
+    )(left, *rights)
+
+
 def local_norm(values):
     centre = jnp.mean(values, axis=1, keepdims=True)
     centred = values - centre
@@ -230,17 +474,17 @@
     me = lax.axis_index("mp")
     groups = [list(range(i, i + group)) for i in range(0, mp, group)]
 
+    fitted = dp == 16 and mp == 2
+    lanes = 256
+
     def gather(weight):
         whole = lax.all_gather(weight, ("mp", "dp"), axis=0, tiled=True)
         return whole.reshape(mp, width, weight.shape[1])
 
-    def scatter(parts):
-        columns = parts[0].shape[1]
-        lanes = -columns % 256
-        whole = jnp.concatenate([part.astype(BF16) for part in parts], axis=0)
-        whole = jnp.pad(whole, ((0, 0), (0, lanes)))
+    def scatter(parts, columns):
+        whole = parts.reshape(mp * width, parts.shape[2])
         mine = lax.psum_scatter(whole, ("mp", "dp"), scatter_dimension=0, tiled=True)
-        return mine[:, :columns].astype(F32)
+        return lax.optimization_barrier(mine)[:, :columns].astype(F32)
 
     def to_heads(part):
         kinds = part.shape[0]
@@ -266,10 +510,17 @@
     starts = lax.dynamic_slice_in_dim(picture_start, half * HALF, HALF)
     masks = picture_masks(starts)
 
-    attn_weights = gather(jnp.concatenate([query_weight, key_weight, value_weight], axis=1))
-    output_all = gather(output_weight.T)
-    hidden_all = gather(hidden_weight)
-    project_all = gather(project_weight.T)
+    attn_shard = jnp.concatenate([query_weight, key_weight, value_weight], axis=1)
+    if fitted:
+        attn_weights, output_all = gather_blocks([attn_shard, output_weight.T], mp)
+        attn_weights, hidden_shard, project_shard = lax.optimization_barrier(
+            (attn_weights, hidden_weight, project_weight)
+        )
+    else:
+        attn_weights, output_all = gather(attn_shard), gather(output_weight.T)
+        hidden_shard, project_shard = hidden_weight, project_weight
+    hidden_all = gather(hidden_shard)
+    project_all = gather(project_shard.T)
 
     residual_in = inputs.astype(F32)
     normed_pre, rstd_pre = local_norm(residual_in)
@@ -302,12 +553,6 @@
         peak_here = lax.dynamic_update_slice_in_dim(
             spread, peak_here, (me % group) * (HEADS // group), 0
         )
-    peak_all = lax.pmax(peak_here, ("dp", "mp"))
-    logit_peak = lax.dynamic_slice_in_dim(peak_all, me * (HEADS // mp), HEADS // mp)
-    factor = jnp.repeat(jnp.sqrt(CLIP_LIMIT / jnp.maximum(logit_peak, CLIP_LIMIT)), HEAD)
-    clipped_query = query_weight.astype(F32) * factor[None, :]
-    clipped_key = key_weight.astype(F32) * factor[None, :]
-
     residual_mid = (
         residual_in + total([dot(mixed[j], output_all[j], 0, 1) for j in range(mp)]) + output_bias
     )
@@ -315,27 +560,33 @@
     mlp_in = (normed_mid * midnorm_gain + midnorm_shift).astype(BF16)
     activated, slopes = [], []
     for j in range(mp):
-        value, slope = gelu_parts(dot(mlp_in, hidden_all[j]) + hidden_bias_all[j])
+        value, slope = gelu_parts(dot(hidden_all[j], mlp_in, 0, 1) + hidden_bias_all[j][:, None])
         activated.append(value.astype(BF16))
         slopes.append(slope.astype(BF16))
-    project_parts = [dot(cotangent, activated[j], 0, 0) for j in range(mp)]
-    project_grad = scatter(project_parts)
+    activated, slopes = lax.optimization_barrier((activated, slopes))
+    project_parts = weight_gradient(cotangent.T, activated, lanes)
+    project_parts, late_cotangent = lax.optimization_barrier((project_parts, cotangent))
+    project_grad = scatter(project_parts, hidden)
     grad_up = [
-        (dot(cotangent, project_all[j]) * slopes[j].astype(F32)).astype(BF16) for j in range(mp)
+        (dot(project_all[j], late_cotangent, 0, 1) * slopes[j].astype(F32)).astype(BF16)
+        for j in range(mp)
     ]
-    hidden_grad = scatter([dot(mlp_in, grad_up[j], 0, 0) for j in range(mp)])
+    grad_up = lax.optimization_barrier(grad_up)
+    hidden_parts = weight_gradient(mlp_in.T, grad_up, lanes)
+    hidden_parts, grad_up, activated = lax.optimization_barrier((hidden_parts, grad_up, activated))
+    hidden_grad = scatter(hidden_parts, hidden)
     final_rows = (
         residual_mid
-        + total([dot(activated[j], project_all[j], 1, 1) for j in range(mp)])
+        + total([dot(activated[j], project_all[j], 0, 1) for j in range(mp)])
         + project_bias
     )
     layer_output = final_rows.astype(BF16)
 
     grad_output = cotangent.astype(F32)
-    grad_mid = total([dot(grad_up[j], hidden_all[j], 1, 1) for j in range(mp)])
+    grad_mid = total([dot(grad_up[j], hidden_all[j], 0, 1) for j in range(mp)])
     grad_resid = grad_output + norm_backward(grad_mid, normed_mid, rstd_mid, midnorm_gain)
     grad_branch = grad_resid.astype(BF16)
-    output_grad = scatter([dot(grad_branch, mixed[j], 0, 1) for j in range(mp)])
+    output_grad = scatter(weight_gradient(grad_branch.T, mixed, lanes), shard)
     grad_mixed = [
         dot(output_all[j], grad_branch, 0, 1).astype(BF16).reshape(shard // HEAD, HEAD, tokens)
         for j in range(mp)
@@ -352,7 +603,7 @@
         whole = from_heads(grad_pieces[0]).reshape(3, mp, shard // HEAD, HEAD, tokens)
         grad_pieces = [whole[:, j] for j in range(mp)]
     grad_rows = [piece.reshape(3 * shard, tokens) for piece in grad_pieces]
-    attn_grad = scatter([dot(attn_in, grad_rows[j], 0, 1) for j in range(mp)])
+    attn_grad = scatter(weight_gradient(attn_in.T, grad_rows, lanes), 3 * shard)
     grad_pre = total([dot(grad_rows[j], attn_weights[j], 0, 1) for j in range(mp)])
     inputs_gradient = grad_resid + norm_backward(grad_pre, normed_pre, rstd_pre, prenorm_gain)
 
@@ -360,7 +611,7 @@
     head_parts = (
         jnp.stack([sums[:shard] for sums in row_sums]),
         jnp.stack([sums[2 * shard :] for sums in row_sums]),
-        jnp.stack([jnp.sum(part.astype(F32), axis=0) for part in grad_up]),
+        jnp.stack([jnp.sum(part.astype(F32), axis=1) for part in grad_up]),
     )
     norm_parts = (
         jnp.sum(grad_pre * normed_pre, axis=0),
@@ -370,13 +621,20 @@
         jnp.sum(grad_mid, axis=0),
         jnp.sum(grad_output, axis=0),
     )
-    flat = jnp.concatenate([item.reshape(-1) for item in (*head_parts, *norm_parts)])
+    slot = lax.axis_index("dp") * mp + me
+    peak_slots = jnp.where(lax.iota(jnp.int32, dp * mp)[:, None] == slot, peak_here[None, :], 0.0)
+    flat = jnp.concatenate([item.reshape(-1) for item in (*head_parts, *norm_parts, peak_slots)])
     flat = lax.psum(flat, ("dp", "mp"))
     ends = [mp * shard, mp * shard, mp * hidden] + [width] * 6
     sums, at = [], 0
     for size in ends:
         sums.append(flat[at : at + size])
         at += size
+    peak_all = jnp.max(flat[at:].reshape(dp * mp, HEADS), axis=0)
+    logit_peak = lax.dynamic_slice_in_dim(peak_all, me * (HEADS // mp), HEADS // mp)
+    factor = jnp.repeat(jnp.sqrt(CLIP_LIMIT / jnp.maximum(logit_peak, CLIP_LIMIT)), HEAD)
+    clipped_query = query_weight.astype(F32) * factor[None, :]
+    clipped_key = key_weight.astype(F32) * factor[None, :]
     query_bias_grad, value_bias_grad, hidden_bias_grad = (
         lax.dynamic_index_in_dim(item.reshape(mp, -1), me, keepdims=False) for item in sums[:3]
     )

time: 955 us -> 872 us (0.913)
  Pallas kernels: 102 us -> 229 us
  matrix products: 230 us -> 150 us
  local copies, waits for them, and re-layouts: 98.4 us -> 32.6 us
  blocking collectives: 91.3 us -> 47.7 us
  waiting for transfers between devices: 363 us -> 345 us
    reduce_scatter x0 -> x4, waiting for transfers between devices: none -> 338 us  [scatter(): lax.psum_scatter(whole, ('mp', 'dp'), scatter_dimension=0, tiled=True)]
    all_gather x4 -> x2, waiting for transfers between devices: 184 us -> 5.42 us  [gather(): whole = lax.all_gather(weight, ('mp', 'dp'), axis=0, tiled=True)]
    unnamed x12 -> x6, waiting for transfers between devices: 178 us -> 1.78 us
    pallas_call x0 -> x5, Pallas kernels: none -> 128 us  [the longest x1 68.4 us: gather_blocks(): pl.pallas_call(partial(gather_kernel, count), in_specs=[anywhere] * count...]
    dot_general x24 -> x16, matrix products: 230 us -> 150 us  [dot(): lax.dot_general(left, right, (((left_dim,), (right_dim,)), ((), ())), pre...]
    pmax x1 -> x0, blocking collectives: 39.8 us -> none  [body(): peak_all = lax.pmax(peak_here, ('dp', 'mp'))]
    unnamed x105 -> x91, local copies, waits for them, and re-layouts: 59.5 us -> 22.6 us
    pad x4 -> x0, local copies, waits for them, and re-layouts: 28.8 us -> none  [scatter(): whole = jnp.pad(whole, ((0, 0), (0, lanes)))]
  transfers between devices with their start and end apart: 8 -> 6, of which waited for: 6 -> 4; matrix products, arithmetic and copies ran while one was open for 30% -> 20% of each run, Pallas kernels for 11% -> 16%
where the time goes in v2:
time: 872 us; the launch traced here: 863 us
  waiting for transfers between devices  345 us (40%)
  Pallas kernels  229 us (26%)
  matrix products  150 us (17%)
  blocking collectives  47.7 us (5%)
  other arithmetic  41.3 us (5%)
  local copies, waits for them, and re-layouts  32.6 us (4%)
  between operations  16.4 us (2%)
    reduce_scatter x4, waiting for transfers between devices, scatter(): lax.psum_scatter(whole, ('mp', 'dp'), scatter_dimension=0, tiled=True)  338 us
    dot_general x16, matrix products, dot(): lax.dot_general(left, right, (((left_dim,), (right_dim,)), ((), ())), pre...  150 us
    pallas_call x1, Pallas kernels, gather_blocks(): pl.pallas_call(partial(gather_kernel, count), in_specs=[anywhere] * count...  68.4 us
    pallas_call x4, Pallas kernels, weight_gradient(): pl.pallas_call(partial(gradient_kernel, count), grid=(count, width // til...  59.2 us
    pallas_call x2, Pallas kernels, attention_forward(): pl.pallas_call(forward_kernel, grid=(heads,), in_specs=[features, feature...  51.7 us
    pallas_call x2, Pallas kernels, attention_backward(): pl.pallas_call(backward_kernel, grid=(heads,), in_specs=[features, featur...  50.1 us
    psum x1, blocking collectives, body(): flat = lax.psum(flat, ('dp', 'mp'))  39.7 us
    unnamed x91, local copies, waits for them, and re-layouts  22.6 us
  transfers between devices with their start and end apart: 6, of which 4 were waited for; matrix products, arithmetic and copies ran while one was open for 20% of the time, Pallas kernels for 16%

profile of v2, /device:TPU:0, one launch (start us, length us, event | category | flops | bytes accessed | tf_op | source)
XLA Modules:
  0.0 862.8 jit_solution(11933068839559862688)
XLA Ops:
  9.0 68.4 %gather_blocks.1 = (bf16[2,16,72,1728]{3,2,1,0:T(8,128)(2,1)}, bf16[2,16,72,576]{3,2,1,0:T(8,128)(2,1)}) custom-call(bf16[72,1728]{1,0:T(8,128)(2,1)} %concatenate.23.refs_0_, bf16[72,576]{1,0:T(8,128)(2,1)} %bitcast.81), custom_call_target="tpu_custom_call" | custom-call | bytes 4976640 | tf_op jit(solution)/shard_map/gather_blocks/pallas_call | solution.py:364
  84.9 4.8 copy.67
  90.6 8.0 all-reduce.3
  103.8 9.0 %add_convert_fusion.1 = bf16[1728,1024]{1,0:T(8,128)(2,1)} fusion(f32[1728]{0:T(1024)S(1)} %concatenate.24, bf16[2,1152,1728]{2,1,0:T(8,128)(2,1)} %bitcast.83, bf16[1024,1152]{0,1:T(8,128)(2,1)S(1)} %copy.64, f32[1152]{0:T(1024)S(1)} %copy-done.26, f32[1152]{0:T(1024)S(1)} %copy-done.21, f32[1024]{0:T(1024)S(1)} %add_rsqrt_fusion.1, ...), kind=kOutput, calls=%fused_computation.27 | convolution fusion | flops 4087480320 | bytes 10051328 | tf_op jit(solution)/shard_map/dot_general | solution.py:29
  112.8 25.8 %attention_forward.2 = (bf16[8,72,1024]{2,1,0:T(8,128)(2,1)}, f32[8,1,1024]{2,1,0:T(1,128)}, f32[8,1,1024]{2,1,0:T(1,128)}) custom-call(f32[16,1024]{1,0:T(8,128)} %get-tuple-element.174.mask_ref, f32[16,1024]{1,0:T(8,128)} %get-tuple-element.173.key_mask_ref, bf16[3,8,72,1024]{3,2,1,0:T(8,128)(2,1)} %bitcast.93, bf16[3,8,72,1024]{3,2,1,0:T(8,128)(2,1)} %bitcast.94, ...), custom_call_target="tpu_custom_call" | custom-call | flops 8589934592 | bytes 4718592 | tf_op jit(solution)/shard_map/attention_forward/pallas_call | solution.py:125
  138.6 5.9 fusion.74
  144.5 9.0 %add_convert_fusion = bf16[1728,1024]{1,0:T(8,128)(2,1)} fusion(f32[1728]{0:T(1024)S(1)} %concatenate.25, bf16[2,1152,1728]{2,1,0:T(8,128)(2,1)} %bitcast.84, bf16[1024,1152]{0,1:T(8,128)(2,1)S(1)} %copy.64, f32[1152]{0:T(1024)S(1)} %copy-done.26, f32[1152]{0:T(1024)S(1)} %copy-done.21, f32[1024]{0:T(1024)S(1)} %add_rsqrt_fusion.1, ...), kind=kOutput, calls=%fused_computation.26 | convolution fusion | flops 4087480320 | bytes 10051328 | tf_op jit(solution)/shard_map/dot_general | solution.py:29
  153.5 25.9 %attention_forward.3 = (bf16[8,72,1024]{2,1,0:T(8,128)(2,1)}, f32[8,1,1024]{2,1,0:T(1,128)}, f32[8,1,1024]{2,1,0:T(1,128)}) custom-call(f32[16,1024]{1,0:T(8,128)} %get-tuple-element.174.mask_ref, f32[16,1024]{1,0:T(8,128)} %get-tuple-element.173.key_mask_ref, bf16[3,8,72,1024]{3,2,1,0:T(8,128)(2,1)} %bitcast.87, bf16[3,8,72,1024]{3,2,1,0:T(8,128)(2,1)} %bitcast.88, ...), custom_call_target="tpu_custom_call" | custom-call | flops 8589934592 | bytes 4718592 | tf_op jit(solution)/shard_map/attention_forward/pallas_call | solution.py:125
  179.5 5.5 fusion.73
  189.3 18.2 %fusion.8 = (bf16[2152,1024]{1,0:T(8,128)(2,1)}, bf16[2152,1024]{1,0:T(8,128)(2,1)}) fusion(f32[2152]{0:T(1024)S(1)} %get-tuple-element.164, bf16[2304,2152]{1,0:T(8,128)(2,1)} %all-gather.8.cloned.1.call-done, f32[1024,1152]{0,1:T(8,128)} %copy-done, f32[1152]{0:T(1024)S(1)} %copy-done.29, f32[1152]{0:T(1024)S(1)} %copy-done.16, ...), kind=kOutput, calls=%fused_computation.12 | convolution fusion | flops 5129379840 | bytes 18572704 | tf_op jit(solution)/shard_map/dot_general | solution.py:29
  207.5 15.0 %fusion.13 = (bf16[2152,1024]{1,0:T(8,128)(2,1)}, bf16[2152,1024]{1,0:T(8,128)(2,1)}) fusion(f32[2152]{0:T(1024)S(1)} %get-tuple-element.163, bf16[2304,2152]{1,0:T(8,128)(2,1)S(1)} %copy-done.33, f32[1024,1152]{0,1:T(8,128)S(1)} %copy-done.1, f32[1152]{0:T(1024)S(1)} %copy-done.29, f32[1152]{0:T(1024)S(1)} %copy-done.16, f32[1024]{0:T(1024)S(1)} %add_rsqrt_fusion, ...), kind=kOutput, calls=%fused_computation.17 | convolution fusion | flops 5129379840 | bytes 18583552 | tf_op jit(solution)/shard_map/dot_general | solution.py:29
  222.5 17.9 %weight_gradient.4 = bf16[2,1152,2304]{2,1,0:T(8,128)(2,1)} custom-call(bf16[1152,1024]{1,0:T(8,128)(2,1)} %bitcast.66, bf16[2152,1024]{1,0:T(8,128)(2,1)} %get-tuple-element.58.refs_0_, bf16[2152,1024]{1,0:T(8,128)(2,1)} %get-tuple-element.59.refs_1_), custom_call_target="tpu_custom_call" | custom-call | flops 10154409984 | bytes 21790720 | tf_op jit(solution)/shard_map/weight_gradient/pallas_call | solution.py:400
  240.4 5.4 all-gather.6.cloned.1.call-done
  245.8 10.9 %multiply_convert_fusion.refs_1_ = bf16[2152,1024]{1,0:T(8,128)(2,1)} fusion(bf16[2152,1024]{1,0:T(8,128)(2,1)} %get-tuple-element.55, bf16[1024,1152]{1,0:T(8,128)(2,1)S(1)} %copy-done.11, bf16[2304,2152]{1,0:T(8,128)(2,1)} %all-gather.6.cloned.1.call-done), kind=kOutput, calls=%fused_computation.20 | convolution fusion | flops 5083815936 | bytes 16187392 | tf_op jit(solution)/shard_map/dot_general | solution.py:29
  256.7 9.4 %multiply_convert_fusion.1.refs_0_ = bf16[2152,1024]{1,0:T(8,128)(2,1)} fusion(bf16[2152,1024]{1,0:T(8,128)(2,1)} %get-tuple-element.54, bf16[1024,1152]{1,0:T(8,128)(2,1)S(1)} %copy-done.11, bf16[2304,2152]{1,0:T(8,128)(2,1)S(1)} %copy-done.32), kind=kOutput, calls=%fused_computation.21 | convolution fusion | flops 5083815936 | bytes 16187392 | tf_op jit(solution)/shard_map/dot_general | solution.py:29
  266.1 18.0 %weight_gradient.5 = bf16[2,1152,2304]{2,1,0:T(8,128)(2,1)} custom-call(bf16[1152,1024]{1,0:T(8,128)(2,1)} %fusion.93.left_ref, bf16[2152,1024]{1,0:T(8,128)(2,1)} %multiply_convert_fusion.1.refs_0_, bf16[2152,1024]{1,0:T(8,128)(2,1)} %multiply_convert_fusion.refs_1_), custom_call_target="tpu_custom_call" | custom-call | flops 10154409984 | bytes 21790720 | tf_op jit(solution)/shard_map/weight_gradient/pallas_call | solution.py:400
  284.1 10.5 %fusion.34 = f32[1024,1152]{0,1:T(8,128)} fusion(bf16[2152,1024]{1,0:T(8,128)(2,1)} %multiply_convert_fusion.1.refs_0_, bf16[2304,2152]{1,0:T(8,128)(2,1)} %all-gather.8.cloned.1.call-done), kind=kOutput, calls=%fused_computation.62 | convolution fusion | flops 5077204992 | bytes 14139392 | tf_op jit(solution)/shard_map/dot_general | solution.py:29
  294.6 12.4 %multiply_reduce_fusion = (f32[1152]{0:T(1024)S(1)}, f32[1024]{0:T(1024)S(1)}, f32[1024]{0:T(1024)S(1)}, f32[1152]{0:T(1024)S(1)}, f32[1024,1152]{0,1:T(8,128)S(1)}) fusion(f32[1024,1152]{0,1:T(8,128)} %copy-done, f32[1024]{0:T(1024)S(1)} %add_rsqrt_fusion, f32[1024]{0:T(1024)S(1)} %broadcast_multiply_fusion.4, f32[1152]{0:T(1024)S(1)} %copy-done.16, ...), kind=kOutput, calls=%fused_computation.48 | convolution fusion | flops 5088997376 | bytes 23606784 | tf_op jit(solution)/shard_map/dot_general | solution.py:29
  312.4 8.9 %weight_gradient.7 = bf16[2,1152,768]{2,1,0:T(8,128)(2,1)} custom-call(bf16[1152,1024]{1,0:T(8,128)(2,1)} %bitcast.75, bf16[576,1024]{1,0:T(8,128)(2,1)} %bitcast.102, bf16[576,1024]{1,0:T(8,128)(2,1)} %bitcast.100), custom_call_target="tpu_custom_call" | custom-call | flops 2717908992 | bytes 8257536 | tf_op jit(solution)/shard_map/weight_gradient/pallas_call | solution.py:400
  321.3 25.1 %attention_backward.2 = bf16[3,8,72,1024]{3,2,1,0:T(8,128)(2,1)} custom-call(f32[16,1024]{1,0:T(8,128)} %get-tuple-element.174.mask_ref, f32[16,1024]{1,0:T(8,128)} %get-tuple-element.173.key_mask_ref, bf16[3,8,72,1024]{3,2,1,0:T(8,128)(2,1)} %bitcast.96, bf16[3,8,72,1024]{3,2,1,0:T(8,128)(2,1)} %bitcast.97, bf16[3,8,72,1024]{3,2,1,0:T(8,128)(2,1)} %bitcast.98, ...), custom_call_target="tpu_custom_call" | custom-call | flops 21474836480 | bytes 9437184 | tf_op jit(solution)/shard_map/attention_backward/pallas_call | solution.py:146
  346.4 10.2 %fusion.44 = f32[1024,1152]{0,1:T(8,128)} fusion(bf16[1728,1024]{1,0:T(8,128)(2,1)} %bitcast.71, bf16[2,1152,1728]{2,1,0:T(8,128)(2,1)} %bitcast.85), kind=kOutput, calls=%fused_computation.76 | convolution fusion | flops 4076863488 | bytes 12386304 | tf_op jit(solution)/shard_map/dot_general | solution.py:29
  359.3 25.0 %attention_backward.3 = bf16[3,8,72,1024]{3,2,1,0:T(8,128)(2,1)} custom-call(f32[16,1024]{1,0:T(8,128)} %get-tuple-element.174.mask_ref, f32[16,1024]{1,0:T(8,128)} %get-tuple-element.173.key_mask_ref, bf16[3,8,72,1024]{3,2,1,0:T(8,128)(2,1)} %bitcast.90, bf16[3,8,72,1024]{3,2,1,0:T(8,128)(2,1)} %bitcast.91, bf16[3,8,72,1024]{3,2,1,0:T(8,128)(2,1)} %bitcast.92, ...), custom_call_target="tpu_custom_call" | custom-call | flops 21474836480 | bytes 9437184 | tf_op jit(solution)/shard_map/attention_backward/pallas_call | solution.py:146
  384.4 9.4 %convolution_add_fusion = f32[1024,1152]{0,1:T(8,128)S(1)} fusion(f32[1024,1152]{0,1:T(8,128)} %fusion.44, bf16[1728,1024]{1,0:T(8,128)(2,1)} %bitcast.73, bf16[2,1152,1728]{2,1,0:T(8,128)(2,1)} %bitcast.86), kind=kOutput, calls=%fused_computation.54 | convolution fusion | flops 4078043136 | bytes 17104896 | tf_op jit(solution)/shard_map/dot_general | solution.py:29
  398.1 14.5 %weight_gradient.6 = bf16[2,1152,1792]{2,1,0:T(8,128)(2,1)} custom-call(bf16[1152,1024]{1,0:T(8,128)(2,1)} %get-tuple-element.149.left_ref, bf16[1728,1024]{1,0:T(8,128)(2,1)} %bitcast.72, bf16[1728,1024]{1,0:T(8,128)(2,1)} %bitcast.74), custom_call_target="tpu_custom_call" | custom-call | flops 8153726976 | bytes 17694720 | tf_op jit(solution)/shard_map/weight_gradient/pallas_call | solution.py:400
  426.3 10.3 %convert_reduce_fusion.5 = (f32[1152]{0:T(1024)S(1)}, f32[1024,1152]{0,1:T(8,128)}) fusion(bf16[1024,1152]{0,1:T(8,128)(2,1)} %copy.67, f32[1024]{0:T(1024)S(1)} %broadcast_multiply_fusion, f32[1024]{0:T(1024)S(1)} %copy-done.18, bf16[1024,1152]{0,1:T(8,128)(2,1)S(1)} %copy-done.3, f32[1024]{0:T(1024)S(1)} %broadcast_multiply_fusion.1, ...), kind=kLoop, calls=%fused_computation.31 | loop fusion | flops 22412160 | bytes 23639552 | tf_op jit(solution)/shard_map/reduce_sum | solution.py:622
  436.7 39.7 %psum.7 = f32[14032]{0:T(1024)S(1)} all-reduce(f32[14032]{0:T(1024)S(1)} %concatenate.27), channel_id=1, replica_groups=mesh['dp'=16,'mp'=2] {'dp','mp'}, use_global_device_ids=true, to_apply=%region_21.22 | all-reduce | flops 14032 | bytes 112256 | tf_op jit(solution)/shard_map/psum | solution.py:627
  476.5 9.0 %fusion.38 = f32[1024,1152]{0,1:T(8,128)S(1)} fusion(bf16[2152,1024]{1,0:T(8,128)(2,1)} %get-tuple-element.58.refs_0_, bf16[2304,2152]{1,0:T(8,128)(2,1)} %all-gather.6.cloned.1.call-done), kind=kOutput, calls=%fused_computation.66 | convolution fusion | flops 5077204992 | bytes 14139392 | tf_op jit(solution)/shard_map/dot_general | solution.py:29
  485.6 10.4 %add_convert_fusion.2 = bf16[1024,1152]{0,1:T(8,128)(2,1)} fusion(f32[1024,1152]{0,1:T(8,128)S(1)} %bitcast.65, f32[1024,1152]{0,1:T(8,128)S(1)} %fusion.38, bf16[2152,1024]{1,0:T(8,128)(2,1)} %get-tuple-element.59.refs_1_, bf16[2304,2152]{1,0:T(8,128)(2,1)} %all-gather.6.cloned.1.call-done, f32[1152]{0:T(1024)S(1)} %copy-done.35), kind=kOutput, calls=%fused_computation.51 | convolution fusion | flops 5081923584 | bytes 21221888 | tf_op jit(solution)/shard_map/dot_general | solution.py:29
  502.0 6.2 copy.76
  512.4 47.0 %reduce-scatter.5.cloned.1.call-done = bf16[72,1792]{1,0:T(8,128)(2,1)} async-done(((bf16[2304,1792]{1,0:T(8,128)(2,1)}), bf16[72,1792]{1,0:T(8,128)(2,1)}) %reduce-scatter.5.cloned.1.call-update) | async-done | bytes 258064 | tf_op jit(solution)/shard_map/reduce_scatter | solution.py:486
  561.3 145.2 %reduce-scatter.11.cloned.1.call-done = bf16[72,2304]{1,0:T(8,128)(2,1)} async-done(((bf16[2304,2304]{1,0:T(8,128)(2,1)}), bf16[72,2304]{1,0:T(8,128)(2,1)}) %reduce-scatter.11.cloned.1.call-update) | async-done | bytes 331792 | tf_op jit(solution)/shard_map/reduce_scatter | solution.py:486
  708.4 145.3 %reduce-scatter.9.cloned.1.call-done = bf16[72,2304]{1,0:T(8,128)(2,1)} async-done(((bf16[2304,2304]{1,0:T(8,128)(2,1)}), bf16[72,2304]{1,0:T(8,128)(2,1)}) %reduce-scatter.9.cloned.1.call-update) | async-done | bytes 331792 | tf_op jit(solution)/shard_map/reduce_scatter | solution.py:486
  (180 shorter events, 60.1 us)
Async XLA Ops:
  7.2 182.1 %all-gather.8.cloned.1.call-start = ((), (), s32[]{:S(2)}) async-start(), calls=%async_computation.5 | async-start | bytes 10340352 | tf_op jit(solution)/shard_map/all_gather | solution.py:481
  77.4 168.4 %all-gather.6.cloned.1.call-start = ((), (), s32[]{:S(2)}) async-start(), calls=%async_computation.4 | async-start | bytes 10340352 | tf_op jit(solution)/shard_map/all_gather | solution.py:481
  78.2 432.7 %reduce-scatter.7.cloned.1.call-start = ((), (), s32[]{:S(2)}) async-start(), calls=%async_computation.7 | async-start | bytes 3649536 | tf_op jit(solution)/shard_map/reduce_scatter | solution.py:486
  82.0 8.3 copy-start.25
  82.0 16.9 %copy-start.28 = (s32[2048]{0:T(1024)S(1)}, s32[2048]{0:T(1024)}, u32[]{:S(2)}) copy-start(s32[2048]{0:T(1024)} %param.19) | copy-start | bytes 24580
  84.9 94.5 %copy-start.2 = (bf16[1024,1152]{0,1:T(8,128)(2,1)}, bf16[1024,1152]{0,1:T(8,128)(2,1)S(1)}, u32[]{:S(2)}) copy-start(bf16[1024,1152]{0,1:T(8,128)(2,1)S(1)} %copy.64) | copy-start | bytes 7077892
  100.4 44.1 %copy-start.17 = (f32[1024]{0:T(1024)}, f32[1024]{0:T(1024)S(1)}, u32[]{:S(2)}) copy-start(f32[1024]{0:T(1024)S(1)} %broadcast_multiply_fusion.5) | copy-start | bytes 12292
  101.1 43.4 %copy-start.19 = (f32[1024]{0:T(1024)}, f32[1024]{0:T(1024)S(1)}, u32[]{:S(2)}) copy-start(f32[1024]{0:T(1024)S(1)} %add_rsqrt_fusion.1) | copy-start | bytes 12292
  153.5 26.0 %copy-start.34 = (f32[1152]{0:T(1024)S(1)}, f32[1152]{0:T(1024)}, u32[]{:S(2)}) copy-start(f32[1152]{0:T(1024)} %param.28) | copy-start | bytes 13828
  189.3 18.2 %copy-start.1 = (f32[1024,1152]{0,1:T(8,128)S(1)}, f32[1024,1152]{0,1:T(8,128)}, u32[]{:S(2)}) copy-start(f32[1024,1152]{0,1:T(8,128)} %copy-done) | copy-start | bytes 14155780
  189.3 18.2 %copy-start.33 = (bf16[2304,2152]{1,0:T(8,128)(2,1)S(1)}, bf16[2304,2152]{1,0:T(8,128)(2,1)}, u32[]{:S(2)}) copy-start(bf16[2304,2152]{1,0:T(8,128)(2,1)} %all-gather.8.cloned.1.call-done) | copy-start | bytes 29749252
  222.5 23.3 %copy-start.11 = (bf16[1024,1152]{1,0:T(8,128)(2,1)S(1)}, bf16[1024,1152]{1,0:T(8,128)(2,1)}, u32[]{:S(2)}) copy-start(bf16[1024,1152]{1,0:T(8,128)(2,1)} %param.35) | copy-start | bytes 7077892
  245.8 10.9 %copy-start.32 = (bf16[2304,2152]{1,0:T(8,128)(2,1)S(1)}, bf16[2304,2152]{1,0:T(8,128)(2,1)}, u32[]{:S(2)}) copy-start(bf16[2304,2152]{1,0:T(8,128)(2,1)} %all-gather.6.cloned.1.call-done) | copy-start | bytes 29749252
  284.1 10.5 %copy-start.7 = (bf16[2152,1024]{1,0:T(8,128)(2,1)S(1)}, bf16[2152,1024]{1,0:T(8,128)(2,1)}, u32[]{:S(2)}) copy-start(bf16[2152,1024]{1,0:T(8,128)(2,1)} %multiply_convert_fusion.refs_1_) | copy-start | bytes 13221892
  284.1 23.0 %slice-start = ((s8[4718592]{0:T(1024)(128)(4,1)}), s8[4194304]{0:T(1024)(128)(4,1)S(1)}, s32[]{:S(2)}) async-start(s8[4718592]{0:T(1024)(128)(4,1)} %bitcast.62), calls=%async_computation.10 | async-start | bytes 8388608
  294.6 12.4 %slice-start.1 = ((s8[4718592]{0:T(1024)(128)(4,1)}), s8[524288]{0:T(1024)(128)(4,1)S(1)}, s32[]{:S(2)}) async-start(s8[4718592]{0:T(1024)(128)(4,1)} %bitcast.62), calls=%async_computation.11 | async-start | bytes 1048576
  294.6 12.4 %copy-start.4 = (bf16[1024,1152]{0,1:T(8,128)(2,1)S(1)}, bf16[1024,1152]{0,1:T(8,128)(2,1)}, u32[]{:S(2)}) copy-start(bf16[1024,1152]{0,1:T(8,128)(2,1)} %copy.67) | copy-start | bytes 7077892
  321.2 238.2 %reduce-scatter.5.cloned.1.call-start = ((), (), s32[]{:S(2)}) async-start(), calls=%async_computation.6 | async-start | bytes 8515584 | tf_op jit(solution)/shard_map/reduce_scatter | solution.py:486
  346.4 10.2 %copy-start.10 = (bf16[1024,1152]{0,1:T(8,128)(2,1)S(1)}, bf16[1024,1152]{0,1:T(8,128)(2,1)}, u32[]{:S(2)}) copy-start(bf16[1024,1152]{0,1:T(8,128)(2,1)} %copy-done.9) | copy-start | bytes 7077892
  346.4 10.2 %copy-start.12 = (bf16[1,16,72,576]{3,2,1,0:T(8,128)(2,1)S(1)}, bf16[1,16,72,576]{3,2,1,0:T(8,128)(2,1)}, u32[]{:S(2)}) copy-start(bf16[1,16,72,576]{3,2,1,0:T(8,128)(2,1)} %get-tuple-element.147) | copy-start | bytes 3981316
  384.4 9.5 %copy-start.3 = (bf16[1024,1152]{0,1:T(8,128)(2,1)S(1)}, bf16[1024,1152]{0,1:T(8,128)(2,1)}, u32[]{:S(2)}) copy-start(bf16[1024,1152]{0,1:T(8,128)(2,1)} %copy-done.2) | copy-start | bytes 7077892
  384.4 9.5 %copy-start.18 = (f32[1024]{0:T(1024)S(1)}, f32[1024]{0:T(1024)}, u32[]{:S(2)}) copy-start(f32[1024]{0:T(1024)} %copy-done.17) | copy-start | bytes 12292
  384.4 9.5 %copy-start.20 = (f32[1024]{0:T(1024)S(1)}, f32[1024]{0:T(1024)}, u32[]{:S(2)}) copy-start(f32[1024]{0:T(1024)} %copy-done.19) | copy-start | bytes 12292
  384.4 9.5 %copy-start.22 = (f32[1152]{0:T(1024)S(1)}, f32[1152]{0:T(1024)}, u32[]{:S(2)}) copy-start(f32[1152]{0:T(1024)} %param.20) | copy-start | bytes 13828
  384.4 9.5 %copy-start.27 = (f32[1152]{0:T(1024)S(1)}, f32[1152]{0:T(1024)}, u32[]{:S(2)}) copy-start(f32[1152]{0:T(1024)} %param.21) | copy-start | bytes 13828
  412.6 293.9 %reduce-scatter.11.cloned.1.call-start = ((), (), s32[]{:S(2)}) async-start(), calls=%async_computation.9 | async-start | bytes 10948608 | tf_op jit(solution)/shard_map/reduce_scatter | solution.py:486
  413.2 440.5 %reduce-scatter.9.cloned.1.call-start = ((), (), s32[]{:S(2)}) async-start(), calls=%async_computation.8 | async-start | bytes 10948608 | tf_op jit(solution)/shard_map/reduce_scatter | solution.py:486
  426.3 59.2 %slice-start.2 = ((s8[4718592]{0:T(1024)(128)(4,1)}), s8[524288]{0:T(1024)(128)(4,1)S(1)}, s32[]{:S(2)}) async-start(s8[4718592]{0:T(1024)(128)(4,1)} %bitcast.64), calls=%async_computation.12 | async-start | bytes 1048576
  476.5 9.1 %slice-start.3 = ((s8[4718592]{0:T(1024)(128)(4,1)}), s8[4194304]{0:T(1024)(128)(4,1)S(1)}, s32[]{:S(2)}) async-start(s8[4718592]{0:T(1024)(128)(4,1)} %bitcast.64), calls=%async_computation.13 | async-start | bytes 8388608
  476.5 9.1 %copy-start.35 = (f32[1152]{0:T(1024)S(1)}, f32[1152]{0:T(1024)}, u32[]{:S(2)}) copy-start(f32[1152]{0:T(1024)} %param.34) | copy-start | bytes 13828
  502.0 8.1 copy-start.14
  502.0 8.1 copy-start.15
  (14 other events, 45.7 us)
Sparse Core Ops, SparseCore 0:
  77.6 82.7 all-gather.7
  163.2 82.5 all-gather.5
  321.4 101.9 reduce-scatter.6
  429.1 130.2 reduce-scatter.4
  565.4 141.1 reduce-scatter.10
  712.4 141.1 reduce-scatter.8

commit v3 on v2

--- a/solution.py
+++ b/solution.py
@@ -170,7 +170,6 @@
 
 
 LINE = 4
-SEAM = 40
 MESH = pl.DeviceIdType.MESH
 
 
@@ -189,7 +188,7 @@
     )
 
 
-def enter(z, x, y, core):
+def enter(z, x, y, core, leap=None):
     barrier = pltpu.get_barrier_semaphore()
     for device in neighbours(z, x, y, core):
         pl.semaphore_signal(barrier, inc=1, device_id=device, device_id_type=MESH)
@@ -202,78 +201,78 @@
     def _():
         pl.semaphore_signal(barrier, inc=1, device_id=device_of(z + 1, x, y, core), device_id_type=MESH)
 
-    pl.semaphore_wait(barrier, 3 + jnp.where(z > 0, 1, 0) + jnp.where(z < LINE - 1, 1, 0))
-
-
-def gather_kernel(count, *refs):
-    shards, wholes = refs[:count], refs[count : 2 * count]
-    own_sem, z_send, z_recv, side_send, side_recv, core_send, core_recv = refs[2 * count :]
+    if leap is not None:
+        pl.semaphore_signal(barrier, inc=1, device_id=device_of(leap, x, y, core), device_id_type=MESH)
+    base = 3 if leap is None else 4
+    pl.semaphore_wait(barrier, base + jnp.where(z > 0, 1, 0) + jnp.where(z < LINE - 1, 1, 0))
+
+
+def chunks_of(widths, pieces):
+    chunks = []
+    for array, (width, count) in enumerate(zip(widths, pieces)):
+        tiles = -(-width // 128)
+        edges = [min(width, tiles * i // count * 128) for i in range(count + 1)]
+        for begin, end in zip(edges[:-1], edges[1:]):
+            chunks.append((array, begin, end - begin, len(chunks) % 2 == 0))
+    return chunks
+
+
+def run_stages(stages, count):
+    for step in range(len(stages) + count - 1):
+        for chunk in range(count):
+            if 0 <= step - chunk < len(stages):
+                stages[step - chunk](chunk)
+
+
+def gather_kernel(arrays, chunks, *refs):
+    shards, wholes = refs[:arrays], refs[arrays : 2 * arrays]
+    own_sem, z_send, z_recv, side_send, side_recv, core_send, core_recv = refs[2 * arrays :]
     z, x, y, core = place_of()
-    rows = shards[0].shape[0]
-    parts = (pl.ds(0, SEAM), pl.ds(SEAM, rows - SEAM))
     other, across_x, across_y = neighbours(z, x, y, core)
 
-    def spot(a, zz, xx, yy, part=None):
-        view = wholes[a].at[yy, (zz * 2 + xx) * 2 + core]
-        return view if part is None else view.at[parts[part]]
+    def spot(a, zz, xx, yy, holder):
+        array, begin, size, _ = chunks[a]
+        return wholes[array].at[yy, (zz * 2 + xx) * 2 + holder, :, pl.ds(begin, size)]
+
+    def remote(block, send, recv, device):
+        return pltpu.make_async_remote_copy(block, block, send, recv, device, MESH)
 
     def along_z(a, zz, upward, source):
-        return pltpu.make_async_remote_copy(
-            spot(a, zz, x, y), spot(a, zz, x, y),
-            z_send.at[a, zz, 1 if upward else 0], z_recv.at[a, zz],
-            device_of(source + (1 if upward else -1), x, y, core), MESH,
-        )
-
-    def sideways(a, half, stage, zz, flip):
-        first = half == 0
-        over_x = first == (stage == 0)
-        xx = x if over_x else (1 - x if flip else x)
-        yy = y if not over_x else (1 - y if flip else y)
-        block = spot(a, zz, xx, yy, half)
+        return remote(
+            spot(a, zz, x, y, core), z_send.at[a, zz, 1 if upward else 0], z_recv.at[a, zz],
+            device_of(source + (1 if upward else -1), x, y, core),
+        )
+
+    def sideways(a, stage, zz, flip, landing=False):
+        over_x = chunks[a][3] == (stage == 0)
+        near, far = (x, y) if over_x else (y, x)
+        near, far = 1 - near if landing else near, 1 - far if flip else far
+        xx, yy = (near, far) if over_x else (far, near)
         slot = zz * 2 + (1 if flip else 0)
-        return pltpu.make_async_remote_copy(
-            block, block, side_send.at[a, half, stage, slot], side_recv.at[a, half, stage, slot],
-            across_x if over_x else across_y, MESH,
-        )
-
-    def arrival(a, half, stage, zz, flip):
-        first = half == 0
-        over_x = first == (stage == 0)
-        xx = 1 - x if over_x else (1 - x if flip else x)
-        yy = 1 - y if not over_x else (1 - y if flip else y)
-        block = spot(a, zz, xx, yy, half)
-        slot = zz * 2 + (1 if flip else 0)
-        return pltpu.make_async_remote_copy(
-            block, block, side_send.at[a, half, stage, slot], side_recv.at[a, half, stage, slot],
-            across_x if over_x else across_y, MESH,
-        )
-
-    def hand_over(a, half, zz, fx, fy):
+        return remote(
+            spot(a, zz, xx, yy, core), side_send.at[a, stage, slot], side_recv.at[a, stage, slot],
+            across_x if over_x else across_y,
+        )
+
+    def hand_over(a, zz, fx, fy, landing=False):
         xx = 1 - x if fx else x
         yy = 1 - y if fy else y
-        block = spot(a, zz, xx, yy, half)
         slot = zz * 4 + (2 if fx else 0) + (1 if fy else 0)
-        return pltpu.make_async_remote_copy(
-            block, block, core_send.at[a, half, slot], core_recv.at[a, half, slot], other, MESH
-        )
-
-    def handed(a, half, zz, fx, fy):
-        xx = 1 - x if fx else x
-        yy = 1 - y if fy else y
-        block = wholes[a].at[yy, (zz * 2 + xx) * 2 + 1 - core].at[parts[half]]
-        slot = zz * 4 + (2 if fx else 0) + (1 if fy else 0)
-        return pltpu.make_async_remote_copy(
-            block, block, core_send.at[a, half, slot], core_recv.at[a, half, slot], other, MESH
+        return remote(
+            spot(a, zz, xx, yy, 1 - core if landing else core),
+            core_send.at[a, slot], core_recv.at[a, slot], other,
         )
 
     def launch_line_block(a, zz):
-        for half in range(2):
-            sideways(a, half, 0, zz, False).start()
-            sideways(a, half, 1, zz, False).start()
-            hand_over(a, half, zz, False, False).start()
+        sideways(a, 0, zz, False).start()
+        sideways(a, 1, zz, False).start()
+        hand_over(a, zz, False, False).start()
 
     def stage_begin(a):
-        own = pltpu.make_async_copy(shards[a], spot(a, z, x, y), own_sem.at[a])
+        array, begin, size, _ = chunks[a]
+        own = pltpu.make_async_copy(
+            shards[array].at[:, pl.ds(begin, size)], spot(a, z, x, y, core), own_sem.at[a]
+        )
         own.start()
         own.wait()
 
@@ -290,51 +289,48 @@
     def stage_hop(a, hop):
         @pl.when(z >= hop)
         def _():
-            origin = z - hop
-            along_z(a, origin, True, z - 1).wait_recv()
+            along_z(a, z - hop, True, z - 1).wait_recv()
 
             @pl.when(z < LINE - 1)
             def _():
-                along_z(a, origin, True, z).start()
-
-            launch_line_block(a, origin)
+                along_z(a, z - hop, True, z).start()
+
+            launch_line_block(a, z - hop)
 
         @pl.when(z < LINE - hop)
         def _():
-            origin = z + hop
-            along_z(a, origin, False, z + 1).wait_recv()
+            along_z(a, z + hop, False, z + 1).wait_recv()
 
             @pl.when(z > 0)
             def _():
-                along_z(a, origin, False, z).start()
-
-            launch_line_block(a, origin)
+                along_z(a, z + hop, False, z).start()
+
+            launch_line_block(a, z + hop)
 
     def stage_turn(a):
+        over_x = chunks[a][3]
         for zz in range(LINE):
-            for half in range(2):
-                arrival(a, half, 0, zz, False).wait_recv()
-                sideways(a, half, 1, zz, True).start()
-                hand_over(a, half, zz, half == 0, half == 1).start()
+            sideways(a, 0, zz, False, landing=True).wait_recv()
+            sideways(a, 1, zz, True).start()
+            hand_over(a, zz, over_x, not over_x).start()
 
     def stage_last(a):
+        over_x = chunks[a][3]
         for zz in range(LINE):
-            for half in range(2):
-                arrival(a, half, 1, zz, False).wait_recv()
-                hand_over(a, half, zz, half == 1, half == 0).start()
-                arrival(a, half, 1, zz, True).wait_recv()
-                hand_over(a, half, zz, True, True).start()
+            sideways(a, 1, zz, False, landing=True).wait_recv()
+            hand_over(a, zz, not over_x, over_x).start()
+            sideways(a, 1, zz, True, landing=True).wait_recv()
+            hand_over(a, zz, True, True).start()
 
     def stage_close(a):
         for zz in range(LINE):
-            for half in range(2):
-                for fx in (False, True):
-                    for fy in (False, True):
-                        handed(a, half, zz, fx, fy).wait_recv()
-                        hand_over(a, half, zz, fx, fy).wait_send()
-                sideways(a, half, 0, zz, False).wait_send()
-                sideways(a, half, 1, zz, False).wait_send()
-                sideways(a, half, 1, zz, True).wait_send()
+            for fx in (False, True):
+                for fy in (False, True):
+                    hand_over(a, zz, fx, fy, landing=True).wait_recv()
+                    hand_over(a, zz, fx, fy).wait_send()
+            sideways(a, 0, zz, False).wait_send()
+            sideways(a, 1, zz, False).wait_send()
+            sideways(a, 1, zz, True).wait_send()
 
             @pl.when(jnp.logical_and(z >= zz, z < LINE - 1))
             def _():
@@ -345,36 +341,237 @@
                 along_z(a, zz, False, z).wait_send()
 
     enter(z, x, y, core)
-    stages = [
-        stage_begin, partial(stage_hop, hop=1), partial(stage_hop, hop=2), partial(stage_hop, hop=3),
-        stage_turn, stage_last, stage_close,
-    ]
-    for step in range(len(stages) + count - 1):
-        for a in range(count):
-            if 0 <= step - a < len(stages):
-                stages[step - a](a)
-
-
-def gather_blocks(shards, mp):
-    count, rows = len(shards), shards[0].shape[0]
-    dp = 16
+    hops = [partial(stage_hop, hop=hop) for hop in range(1, LINE)]
+    run_stages([stage_begin, *hops, stage_turn, stage_last, stage_close], len(chunks))
+
+
+def gather_blocks(shards, pieces, mp):
+    rows, dp = shards[0].shape[0], 16
+    chunks = chunks_of([item.shape[1] for item in shards], pieces)
+    count = len(chunks)
     anywhere = pl.BlockSpec(memory_space=pl.ANY)
     dma = pltpu.SemaphoreType.DMA
     sent = sum(item.size * 2 for item in shards) * 15
     wholes = pl.pallas_call(
-        partial(gather_kernel, count),
-        in_specs=[anywhere] * count,
-        out_specs=[anywhere] * count,
+        partial(gather_kernel, len(shards), chunks),
+        in_specs=[anywhere] * len(shards),
+        out_specs=[anywhere] * len(shards),
         out_shape=[jax.ShapeDtypeStruct((mp, dp, rows, item.shape[1]), BF16) for item in shards],
         scratch_shapes=[
-            dma((count,)), dma((count, LINE, 2)), dma((count, LINE)), dma((count, 2, 2, 8)),
-            dma((count, 2, 2, 8)), dma((count, 2, 16)), dma((count, 2, 16)),
+            dma((count,)), dma((count, LINE, 2)), dma((count, LINE)), dma((count, 2, 8)),
+            dma((count, 2, 8)), dma((count, 16)), dma((count, 16)),
         ],
         compiler_params=pltpu.CompilerParams(collective_id=0, has_side_effects=True),
         cost_estimate=pl.CostEstimate(flops=0, bytes_accessed=sent, transcendentals=0),
         name="gather_blocks",
     )(*shards)
     return [whole.reshape(mp, dp * rows, whole.shape[-1]) for whole in wholes]
+
+
+def scatter_kernel(arrays, chunks, *refs):
+    grads, vector = refs[:arrays], refs[arrays]
+    outs, vector_out = refs[arrays + 1 : 2 * arrays + 1], refs[2 * arrays + 1]
+    count = len(chunks)
+    rest = refs[2 * arrays + 2 :]
+    held, first, second, third, up, down = (rest[i * count : (i + 1) * count] for i in range(6))
+    passed = rest[6 * count]
+    (
+        load_sem, core_send, core_recv, one_send, one_recv, two_send, two_recv, up_send, up_recv,
+        down_send, down_recv, vec_send, vec_recv,
+    ) = rest[6 * count + 1 :]
+    z, x, y, core = place_of()
+    other, across_x, across_y = neighbours(z, x, y, core)
+    leap = jnp.where(z < 2, z + 2, z - 2)
+    pair = z + 1 - 2 * (z % 2)
+    remote = lambda src, dst, send, recv, device: pltpu.make_async_remote_copy(
+        src, dst, send, recv, device, MESH
+    )
+
+    def quarter(a, flip_near, flip_far):
+        over_x = chunks[a][3]
+        fx, fy = (flip_near, flip_far) if over_x else (flip_far, flip_near)
+        return (1 - x if fx else x), (1 - y if fy else y)
+
+    quarters = ((True, True), (True, False), (False, True), (False, False))
+
+    def source(a, xx, yy, holder):
+        array, begin, size, _ = chunks[a]
+        return grads[array].at[yy, :, xx, holder, :, pl.ds(begin, size)]
+
+    def load(a, i):
+        xx, yy = quarter(a, *quarters[i])
+        return pltpu.make_async_copy(source(a, xx, yy, core), held[a].at[i], load_sem.at[a, i])
+
+    def share(a, i):
+        xx, yy = quarter(a, *quarters[i])
+        return remote(
+            source(a, xx, yy, 1 - core), first[a].at[i], core_send.at[a, i], core_recv.at[a, i], other
+        )
+
+    def near(a):
+        return across_x if chunks[a][3] else across_y
+
+    def far(a):
+        return across_y if chunks[a][3] else across_x
+
+    def cross_one(a, i):
+        return remote(
+            held[a].at[i], second[a].at[i], one_send.at[a, i], one_recv.at[a, i], near(a)
+        )
+
+    def cross_two(a):
+        return remote(held[a].at[2], third[a], two_send.at[a], two_recv.at[a], far(a))
+
+    def add_rows(target, slot, term):
+        def one(zz, unused):
+            target[slot, zz] = (target[slot, zz].astype(F32) + term[zz].astype(F32)).astype(BF16)
+            return unused
+
+        lax.fori_loop(0, LINE, one, 0)
+
+    def add_block(a, d, term):
+        held[a][3, d] = (held[a][3, d].astype(F32) + term[d].astype(F32)).astype(BF16)
+
+    def lift(a, d):
+        return remote(
+            held[a].at[3, d], up[a].at[d], up_send.at[a, d], up_recv.at[a, d],
+            device_of(z + 1, x, y, core),
+        )
+
+    def drop(a, d):
+        return remote(
+            held[a].at[3, d], down[a].at[d], down_send.at[a, d], down_recv.at[a, d],
+            device_of(z - 1, x, y, core),
+        )
+
+    def stage_begin(a):
+        for i in range(4):
+            share(a, i).start()
+            load(a, i).start()
+
+    def stage_share(a):
+        for i in range(4):
+            load(a, i).wait()
+            share(a, i).wait_recv()
+            add_rows(held[a], i, first[a].at[i])
+            if i < 2:
+                cross_one(a, i).start()
+
+    def stage_one(a):
+        cross_one(a, 0).wait_recv()
+        add_rows(held[a], 2, second[a].at[0])
+        cross_two(a).start()
+        cross_one(a, 1).wait_recv()
+        add_rows(held[a], 3, second[a].at[1])
+
+    def stage_two(a):
+        cross_two(a).wait_recv()
+        add_rows(held[a], 3, third[a])
+
+    def stage_line(a, hop):
+        for way in (True, False):
+            position = hop if way else LINE - 1 - hop
+            beyond = range(LINE - 1, position, -1) if way else range(position)
+
+            @pl.when(z == position)
+            def _():
+                for d in beyond:
+                    if hop > 0:
+                        (lift if way else drop)(a, d).wait_recv()
+                        add_block(a, d, (up if way else down)[a])
+                    (lift if way else drop)(a, d).start()
+
+    def stage_finish(a):
+        array, begin, size, _ = chunks[a]
+        for d in range(LINE):
+
+            @pl.when(z == d)
+            def _():
+                own = held[a][3, d].astype(F32)
+                if d > 0:
+                    lift(a, d).wait_recv()
+                    own = own + up[a][d].astype(F32)
+                if d < LINE - 1:
+                    drop(a, d).wait_recv()
+                    own = own + down[a][d].astype(F32)
+                outs[array][:, begin : begin + size] = own
+
+    def stage_close(a):
+        for i in range(4):
+            share(a, i).wait_send()
+        cross_one(a, 0).wait_send()
+        cross_one(a, 1).wait_send()
+        cross_two(a).wait_send()
+        for d in range(LINE):
+
+            @pl.when(z < d)
+            def _():
+                lift(a, d).wait_send()
+
+            @pl.when(z > d)
+            def _():
+                drop(a, d).wait_send()
+
+    hops = (other, across_x, across_y, device_of(pair, x, y, core), device_of(leap, x, y, core))
+
+    def exchange(k):
+        return remote(passed.at[k], passed.at[k + 5], vec_send.at[k], vec_recv.at[k], hops[k])
+
+    def vector_step(step):
+        if step == 0:
+            passed[0] = vector[...]
+            exchange(0).start()
+        elif step <= 5:
+            k = step - 1
+            exchange(k).wait()
+            summed = passed[k] + passed[k + 5]
+            if step < 5:
+                passed[k + 1] = summed
+                exchange(k + 1).start()
+            else:
+                vector_out[...] = summed
+
+    enter(z, x, y, core, leap)
+    line = [partial(stage_line, hop=hop) for hop in range(LINE - 1)]
+    stages = [stage_begin, stage_share, stage_one, stage_two, *line, stage_finish, stage_close]
+    for step in range(len(stages) + count - 1):
+        vector_step(step)
+        for chunk in range(count):
+            if 0 <= step - chunk < len(stages):
+                stages[step - chunk](chunk)
+
+
+def scatter_blocks(parts, pieces, vector, mp):
+    dp = 16
+    columns = [part.shape[-1] for part in parts]
+    rows = parts[0].shape[1] // dp
+    chunks = chunks_of(columns, pieces)
+    count = len(chunks)
+    sizes = [chunk[2] for chunk in chunks]
+    dma = pltpu.SemaphoreType.DMA
+    vmem = pl.BlockSpec(memory_space=pltpu.VMEM)
+    lines = -(-vector.shape[0] // 1024) * 8
+    padded = jnp.pad(vector, (0, lines * 128 - vector.shape[0])).reshape(lines, 128)
+    blocks = lambda *lead: [pltpu.VMEM((*lead, LINE, rows, size), BF16) for size in sizes]
+    sent = sum(columns) * rows * 2 * 30
+    *outs, summed = pl.pallas_call(
+        partial(scatter_kernel, len(parts), chunks),
+        in_specs=[pl.BlockSpec(memory_space=pl.ANY)] * len(parts) + [vmem],
+        out_specs=[vmem] * (len(parts) + 1),
+        out_shape=[jax.ShapeDtypeStruct((rows, width), F32) for width in columns]
+        + [jax.ShapeDtypeStruct((lines, 128), F32)],
+        scratch_shapes=[
+            *blocks(4), *blocks(4), *blocks(2), *blocks(), *blocks(), *blocks(),
+            pltpu.VMEM((10, lines, 128), F32),
+            dma((count, 4)), dma((count, 4)), dma((count, 4)), dma((count, 2)), dma((count, 2)),
+            dma((count,)), dma((count,)), dma((count, LINE)), dma((count, LINE)), dma((count, LINE)),
+            dma((count, LINE)), dma((5,)), dma((5,)),
+        ],
+        compiler_params=pltpu.CompilerParams(collective_id=1, has_side_effects=True),
+        cost_estimate=pl.CostEstimate(flops=0, bytes_accessed=sent, transcendentals=0),
+        name="scatter_blocks",
+    )(*[part.reshape(mp, LINE, 2, 2, rows, part.shape[-1]) for part in parts], padded)
+    return outs, summed.reshape(-1)[: vector.shape[0]]
 
 
 def gradient_kernel(count, left_ref, *refs):
@@ -512,7 +709,7 @@
 
     attn_shard = jnp.concatenate([query_weight, key_weight, value_weight], axis=1)
     if fitted:
-        attn_weights, output_all = gather_blocks([attn_shard, output_weight.T], mp)
+        attn_weights, output_all = gather_blocks([attn_shard, output_weight.T], (2, 2), mp)
         attn_weights, hidden_shard, project_shard = lax.optimization_barrier(
             (attn_weights, hidden_weight, project_weight)
         )
@@ -566,7 +763,8 @@
     activated, slopes = lax.optimization_barrier((activated, slopes))
     project_parts = weight_gradient(cotangent.T, activated, lanes)
     project_parts, late_cotangent = lax.optimization_barrier((project_parts, cotangent))
-    project_grad = scatter(project_parts, hidden)
+    with jax.named_scope("scatter_project"):
+        project_grad = scatter(project_parts, hidden)
     grad_up = [
         (dot(project_all[j], late_cotangent, 0, 1) * slopes[j].astype(F32)).astype(BF16)
         for j in range(mp)
@@ -574,7 +772,8 @@
     grad_up = lax.optimization_barrier(grad_up)
     hidden_parts = weight_gradient(mlp_in.T, grad_up, lanes)
     hidden_parts, grad_up, activated = lax.optimization_barrier((hidden_parts, grad_up, activated))
-    hidden_grad = scatter(hidden_parts, hidden)
+    with jax.named_scope("scatter_hidden"):
+        hidden_grad = scatter(hidden_parts, hidden)
     final_rows = (
         residual_mid
         + total([dot(activated[j], project_all[j], 0, 1) for j in range(mp)])
@@ -586,7 +785,7 @@
     grad_mid = total([dot(grad_up[j], hidden_all[j], 0, 1) for j in range(mp)])
     grad_resid = grad_output + norm_backward(grad_mid, normed_mid, rstd_mid, midnorm_gain)
     grad_branch = grad_resid.astype(BF16)
-    output_grad = scatter(weight_gradient(grad_branch.T, mixed, lanes), shard)
+    output_parts = weight_gradient(grad_branch.T, mixed, 1 if fitted else lanes)
     grad_mixed = [
         dot(output_all[j], grad_branch, 0, 1).astype(BF16).reshape(shard // HEAD, HEAD, tokens)
         for j in range(mp)
@@ -603,7 +802,7 @@
         whole = from_heads(grad_pieces[0]).reshape(3, mp, shard // HEAD, HEAD, tokens)
         grad_pieces = [whole[:, j] for j in range(mp)]
     grad_rows = [piece.reshape(3 * shard, tokens) for piece in grad_pieces]
-    attn_grad = scatter(weight_gradient(attn_in.T, grad_rows, lanes), 3 * shard)
+    attn_parts = weight_gradient(attn_in.T, grad_rows, 1 if fitted else lanes)
     grad_pre = total([dot(grad_rows[j], attn_weights[j], 0, 1) for j in range(mp)])
     inputs_gradient = grad_resid + norm_backward(grad_pre, normed_pre, rstd_pre, prenorm_gain)
 
@@ -624,7 +823,12 @@
     slot = lax.axis_index("dp") * mp + me
     peak_slots = jnp.where(lax.iota(jnp.int32, dp * mp)[:, None] == slot, peak_here[None, :], 0.0)
     flat = jnp.concatenate([item.reshape(-1) for item in (*head_parts, *norm_parts, peak_slots)])
-    flat = lax.psum(flat, ("dp", "mp"))
+    if fitted:
+        output_parts, project_grad = lax.optimization_barrier((output_parts, project_grad))
+        (attn_grad, output_grad), flat = scatter_blocks([attn_parts, output_parts], (2, 2), flat, mp)
+    else:
+        attn_grad, output_grad = scatter(attn_parts, 3 * shard), scatter(output_parts, shard)
+        flat = lax.psum(flat, ("dp", "mp"))
     ends = [mp * shard, mp * shard, mp * hidden] + [width] * 6
     sums, at = [], 0
     for size in ends:

time: 872 us -> 618 us (0.71)
  waiting for transfers between devices: 345 us -> 6.68 us
  Pallas kernels: 229 us -> 347 us
  blocking collectives: 47.7 us -> 8.41 us
  local copies, waits for them, and re-layouts: 32.6 us -> 42.8 us
    reduce_scatter x4 -> x2, waiting for transfers between devices: 338 us -> 0.01 us  [scatter(): lax.psum_scatter(whole, ('mp', 'dp'), scatter_dimension=0, tiled=True)]
    pallas_call x1 -> x2, Pallas kernels: 68.4 us -> 186 us  [the longest x1 112 us: scatter_blocks(): pl.pallas_call(partial(scatter_kernel, len(parts), chunks), in_specs=[pl....]
    psum x1 -> x0, blocking collectives: 39.7 us -> none  [body(): flat = lax.psum(flat, ('dp', 'mp'))]
    unnamed x91 -> x98, local copies, waits for them, and re-layouts: 22.6 us -> 27.5 us
  transfers between devices with their start and end apart: 6 -> 4, of which waited for: 4 -> 1; matrix products, arithmetic and copies ran while one was open for 20% -> 35% of each run, Pallas kernels for 16% -> 45%
where the time goes in v3:
time: 618 us; the launch traced here: 608 us
  Pallas kernels  347 us (56%)
  matrix products  149 us (24%)
  local copies, waits for them, and re-layouts  42.8 us (7%)
  other arithmetic  38.2 us (6%)
  between operations  16.2 us (3%)
  blocking collectives  8.41 us (1%)
  waiting for transfers between devices  6.68 us (1%)
    dot_general x16, matrix products, dot(): lax.dot_general(left, right, (((left_dim,), (right_dim,)), ((), ())), pre...  149 us
    pallas_call x1, Pallas kernels, scatter_blocks(): pl.pallas_call(partial(scatter_kernel, len(parts), chunks), in_specs=[pl....  112 us
    pallas_call x1, Pallas kernels, gather_blocks(): pl.pallas_call(partial(gather_kernel, len(shards), chunks), in_specs=[any...  73.6 us
    pallas_call x4, Pallas kernels, weight_gradient(): pl.pallas_call(partial(gradient_kernel, count), grid=(count, width // til...  60.1 us
    pallas_call x2, Pallas kernels, attention_forward(): pl.pallas_call(forward_kernel, grid=(heads,), in_specs=[features, feature...  51.7 us
    pallas_call x2, Pallas kernels, attention_backward(): pl.pallas_call(backward_kernel, grid=(heads,), in_specs=[features, featur...  49.7 us
    unnamed x98, local copies, waits for them, and re-layouts  27.5 us
  transfers between devices with their start and end apart: 4, of which 1 were waited for; matrix products, arithmetic and copies ran while one was open for 35% of the time, Pallas kernels for 45%

profile of v3, /device:TPU:0, one launch (start us, length us, event | category | flops | bytes accessed | tf_op | source)
XLA Modules:
  0.0 608.3 jit_solution(5427850481625035983)
XLA Ops:
  9.0 73.6 %gather_blocks.1 = (bf16[2,16,72,1728]{3,2,1,0:T(8,128)(2,1)}, bf16[2,16,72,576]{3,2,1,0:T(8,128)(2,1)}) custom-call(bf16[72,1728]{1,0:T(8,128)(2,1)} %concatenate.23.refs_0_, bf16[72,576]{1,0:T(8,128)(2,1)} %bitcast.88), custom_call_target="tpu_custom_call" | custom-call | bytes 4976640 | tf_op jit(solution)/shard_map/gather_blocks/pallas_call | solution.py:355
  90.1 4.8 copy.67
  95.8 8.4 %all-reduce.4 = (f32[1152]{0:T(1024)S(1)}, f32[1152]{0:T(1024)S(1)}, f32[4304]{0:T(1024)S(1)}) all-reduce(f32[1152]{0:T(1024)S(1)} %dynamic-update-slice, f32[1152]{0:T(1024)S(1)} %dynamic-update-slice.1, f32[4304]{0:T(1024)S(1)} %dynamic-update-slice.2), channel_id=2, replica_groups=mesh['dp'=16,'mp'=2] {'mp'}, use_global_device_ids=true, to_apply=%add.1 | all-reduce | flops 6608 | bytes 52864
  109.2 8.9 %add_convert_fusion.1 = bf16[1728,1024]{1,0:T(8,128)(2,1)} fusion(f32[1728]{0:T(1024)S(1)} %concatenate.24, bf16[2,1152,1728]{2,1,0:T(8,128)(2,1)} %bitcast.92, bf16[1024,1152]{0,1:T(8,128)(2,1)S(1)} %copy.64, f32[1152]{0:T(1024)S(1)} %copy-done.23, f32[1152]{0:T(1024)S(1)} %copy-done.18, f32[1024]{0:T(1024)S(1)} %add_rsqrt_fusion.1, ...), kind=kOutput, calls=%fused_computation.27 | convolution fusion | flops 4087480320 | bytes 10051328 | tf_op jit(solution)/shard_map/dot_general | solution.py:29
  118.2 25.8 %attention_forward.2 = (bf16[8,72,1024]{2,1,0:T(8,128)(2,1)}, f32[8,1,1024]{2,1,0:T(1,128)}, f32[8,1,1024]{2,1,0:T(1,128)}) custom-call(f32[16,1024]{1,0:T(8,128)} %get-tuple-element.184.mask_ref, f32[16,1024]{1,0:T(8,128)} %get-tuple-element.183.key_mask_ref, bf16[3,8,72,1024]{3,2,1,0:T(8,128)(2,1)} %bitcast.96, bf16[3,8,72,1024]{3,2,1,0:T(8,128)(2,1)} %bitcast.97, ...), custom_call_target="tpu_custom_call" | custom-call | flops 8589934592 | bytes 4718592 | tf_op jit(solution)/shard_map/attention_forward/pallas_call | solution.py:125
  143.9 5.9 fusion.75
  149.9 9.0 %add_convert_fusion = bf16[1728,1024]{1,0:T(8,128)(2,1)} fusion(f32[1728]{0:T(1024)S(1)} %concatenate.25, bf16[2,1152,1728]{2,1,0:T(8,128)(2,1)} %bitcast.93, bf16[1024,1152]{0,1:T(8,128)(2,1)S(1)} %copy.64, f32[1152]{0:T(1024)S(1)} %copy-done.23, f32[1152]{0:T(1024)S(1)} %copy-done.18, f32[1024]{0:T(1024)S(1)} %add_rsqrt_fusion.1, ...), kind=kOutput, calls=%fused_computation.26 | convolution fusion | flops 4087480320 | bytes 10051328 | tf_op jit(solution)/shard_map/dot_general | solution.py:29
  158.8 26.0 %attention_forward.3 = (bf16[8,72,1024]{2,1,0:T(8,128)(2,1)}, f32[8,1,1024]{2,1,0:T(1,128)}, f32[8,1,1024]{2,1,0:T(1,128)}) custom-call(f32[16,1024]{1,0:T(8,128)} %get-tuple-element.184.mask_ref, f32[16,1024]{1,0:T(8,128)} %get-tuple-element.183.key_mask_ref, bf16[3,8,72,1024]{3,2,1,0:T(8,128)(2,1)} %bitcast.102, bf16[3,8,72,1024]{3,2,1,0:T(8,128)(2,1)} %bitcast.103, ...), custom_call_target="tpu_custom_call" | custom-call | flops 8589934592 | bytes 4718592 | tf_op jit(solution)/shard_map/attention_forward/pallas_call | solution.py:125
  184.8 5.5 fusion.74
  193.1 18.2 %fusion.8 = (bf16[2152,1024]{1,0:T(8,128)(2,1)}, bf16[2152,1024]{1,0:T(8,128)(2,1)}) fusion(f32[2152]{0:T(1024)S(1)} %get-tuple-element.174, bf16[2304,2152]{1,0:T(8,128)(2,1)} %all-gather.8.cloned.1.call-done, f32[1024,1152]{0,1:T(8,128)} %copy-done, f32[1152]{0:T(1024)S(1)} %copy-done.27, f32[1152]{0:T(1024)S(1)} %copy-done.13, ...), kind=kOutput, calls=%fused_computation.12 | convolution fusion | flops 5129379840 | bytes 18572704 | tf_op jit(solution)/shard_map/dot_general | solution.py:29
  211.3 14.9 %fusion.13 = (bf16[2152,1024]{1,0:T(8,128)(2,1)}, bf16[2152,1024]{1,0:T(8,128)(2,1)}) fusion(f32[2152]{0:T(1024)S(1)} %get-tuple-element.173, bf16[2304,2152]{1,0:T(8,128)(2,1)S(1)} %copy-done.30, f32[1024,1152]{0,1:T(8,128)S(1)} %copy-done.1, f32[1152]{0:T(1024)S(1)} %copy-done.27, f32[1152]{0:T(1024)S(1)} %copy-done.13, f32[1024]{0:T(1024)S(1)} %add_rsqrt_fusion, ...), kind=kOutput, calls=%fused_computation.17 | convolution fusion | flops 5129379840 | bytes 18583552 | tf_op jit(solution)/shard_map/dot_general | solution.py:29
  226.3 18.0 %weight_gradient.4 = bf16[2,1152,2304]{2,1,0:T(8,128)(2,1)} custom-call(bf16[1152,1024]{1,0:T(8,128)(2,1)} %bitcast.67, bf16[2152,1024]{1,0:T(8,128)(2,1)} %get-tuple-element.63.refs_0_, bf16[2152,1024]{1,0:T(8,128)(2,1)} %get-tuple-element.64.refs_1_), custom_call_target="tpu_custom_call" | custom-call | flops 10154409984 | bytes 21790720 | tf_op jit(solution)/shard_map/weight_gradient/pallas_call | solution.py:597
  250.6 5.9 all-gather.6.cloned.1.call-done
  256.6 10.9 %multiply_convert_fusion.refs_1_ = bf16[2152,1024]{1,0:T(8,128)(2,1)} fusion(bf16[2152,1024]{1,0:T(8,128)(2,1)} %get-tuple-element.60, bf16[1024,1152]{1,0:T(8,128)(2,1)S(1)} %copy-done.9, bf16[2304,2152]{1,0:T(8,128)(2,1)} %all-gather.6.cloned.1.call-done), kind=kOutput, calls=%fused_computation.20 | convolution fusion | flops 5083815936 | bytes 16187392 | tf_op jit(solution)/shard_map/dot_general | solution.py:29
  267.4 9.6 %multiply_convert_fusion.1.refs_0_ = bf16[2152,1024]{1,0:T(8,128)(2,1)} fusion(bf16[2152,1024]{1,0:T(8,128)(2,1)} %get-tuple-element.59, bf16[1024,1152]{1,0:T(8,128)(2,1)S(1)} %copy-done.9, bf16[2304,2152]{1,0:T(8,128)(2,1)S(1)} %copy-done.31), kind=kOutput, calls=%fused_computation.21 | convolution fusion | flops 5083815936 | bytes 16187392 | tf_op jit(solution)/shard_map/dot_general | solution.py:29
  277.0 18.1 %weight_gradient.5 = bf16[2,1152,2304]{2,1,0:T(8,128)(2,1)} custom-call(bf16[1152,1024]{1,0:T(8,128)(2,1)} %fusion.94.left_ref, bf16[2152,1024]{1,0:T(8,128)(2,1)} %multiply_convert_fusion.1.refs_0_, bf16[2152,1024]{1,0:T(8,128)(2,1)} %multiply_convert_fusion.refs_1_), custom_call_target="tpu_custom_call" | custom-call | flops 10154409984 | bytes 21790720 | tf_op jit(solution)/shard_map/weight_gradient/pallas_call | solution.py:597
  299.9 11.1 %fusion.34 = f32[1024,1152]{0,1:T(8,128)} fusion(bf16[2152,1024]{1,0:T(8,128)(2,1)} %multiply_convert_fusion.1.refs_0_, bf16[2304,2152]{1,0:T(8,128)(2,1)} %all-gather.8.cloned.1.call-done), kind=kOutput, calls=%fused_computation.62 | convolution fusion | flops 5077204992 | bytes 14139392 | tf_op jit(solution)/shard_map/dot_general | solution.py:29
  311.1 13.5 %multiply_reduce_fusion = (f32[1152]{0:T(1024)S(1)}, f32[1024]{0:T(1024)S(1)}, f32[1024]{0:T(1024)S(1)}, f32[1152]{0:T(1024)S(1)}, f32[1024,1152]{0,1:T(8,128)}) fusion(f32[1024,1152]{0,1:T(8,128)S(1)} %bitcast.64, f32[1024]{0:T(1024)S(1)} %add_rsqrt_fusion, f32[1024]{0:T(1024)S(1)} %broadcast_multiply_fusion.4, f32[1152]{0:T(1024)S(1)} %copy-done.13, ...), kind=kOutput, calls=%fused_computation.48 | convolution fusion | flops 5088997376 | bytes 23606784 | tf_op jit(solution)/shard_map/dot_general | solution.py:29
  324.6 9.0 %fusion.38 = f32[1024,1152]{0,1:T(8,128)} fusion(bf16[2152,1024]{1,0:T(8,128)(2,1)} %get-tuple-element.63.refs_0_, bf16[2304,2152]{1,0:T(8,128)(2,1)S(1)} %bitcast.91), kind=kOutput, calls=%fused_computation.66 | convolution fusion | flops 5077204992 | bytes 14139392 | tf_op jit(solution)/shard_map/dot_general | solution.py:29
  333.5 10.2 %add_convert_fusion.2 = bf16[1024,1152]{0,1:T(8,128)(2,1)} fusion(f32[1024,1152]{0,1:T(8,128)S(1)} %bitcast.64, f32[1024,1152]{0,1:T(8,128)} %fusion.38, bf16[2152,1024]{1,0:T(8,128)(2,1)} %get-tuple-element.64.refs_1_, bf16[2304,2152]{1,0:T(8,128)(2,1)S(1)} %bitcast.91, f32[1152]{0:T(1024)S(1)} %copy-done.33), kind=kOutput, calls=%fused_computation.51 | convolution fusion | flops 5081923584 | bytes 21225472 | tf_op jit(solution)/shard_map/dot_general | solution.py:29
  343.8 4.7 copy.75
  348.5 5.8 convert_reduce_fusion.6
  358.5 24.9 %attention_backward.3 = bf16[3,8,72,1024]{3,2,1,0:T(8,128)(2,1)} custom-call(f32[16,1024]{1,0:T(8,128)} %get-tuple-element.184.mask_ref, f32[16,1024]{1,0:T(8,128)} %get-tuple-element.183.key_mask_ref, bf16[3,8,72,1024]{3,2,1,0:T(8,128)(2,1)} %bitcast.105, bf16[3,8,72,1024]{3,2,1,0:T(8,128)(2,1)} %bitcast.106, bf16[3,8,72,1024]{3,2,1,0:T(8,128)(2,1)} %bitcast.107, ...), custom_call_target="tpu_custom_call" | custom-call | flops 21474836480 | bytes 9437184 | tf_op jit(solution)/shard_map/attention_backward/pallas_call | solution.py:146
  386.2 4.9 convolution_convert_fusion.1
  391.0 24.8 %attention_backward.2 = bf16[3,8,72,1024]{3,2,1,0:T(8,128)(2,1)} custom-call(f32[16,1024]{1,0:T(8,128)} %get-tuple-element.184.mask_ref, f32[16,1024]{1,0:T(8,128)} %get-tuple-element.183.key_mask_ref, bf16[3,8,72,1024]{3,2,1,0:T(8,128)(2,1)} %bitcast.99, bf16[3,8,72,1024]{3,2,1,0:T(8,128)(2,1)} %bitcast.100, bf16[3,8,72,1024]{3,2,1,0:T(8,128)(2,1)} %bitcast.101, ...), custom_call_target="tpu_custom_call" | custom-call | flops 21474836480 | bytes 9437184 | tf_op jit(solution)/shard_map/attention_backward/pallas_call | solution.py:146
  419.0 8.0 %fusion.44 = f32[1024,1152]{0,1:T(8,128)S(1)} fusion(bf16[1728,1024]{1,0:T(8,128)(2,1)} %bitcast.75, bf16[2,1152,1728]{2,1,0:T(8,128)(2,1)} %bitcast.94), kind=kOutput, calls=%fused_computation.76 | convolution fusion | flops 4076863488 | bytes 12386304 | tf_op jit(solution)/shard_map/dot_general | solution.py:29
  427.1 6.6 %convolution_add_fusion = f32[1024,1152]{0,1:T(8,128)S(1)} fusion(f32[1024,1152]{0,1:T(8,128)S(1)} %fusion.44, bf16[1728,1024]{1,0:T(8,128)(2,1)S(1)} %bitcast.74, bf16[2,1152,1728]{2,1,0:T(8,128)(2,1)} %bitcast.95), kind=kOutput, calls=%fused_computation.54 | convolution fusion | flops 4078043136 | bytes 17104896 | tf_op jit(solution)/shard_map/dot_general | solution.py:29
  437.7 5.7 convert_reduce_fusion.5
  443.4 6.2 %copy.76 = f32[1024,1152]{1,0:T(8,128)} copy(f32[1024,1152]{0,1:T(8,128)} %get-tuple-element.161) | data formatting | bytes 9437184
  450.4 8.8 %weight_gradient.7 = bf16[2,1152,576]{2,1,0:T(8,128)(2,1)} custom-call(bf16[1152,1024]{1,0:T(8,128)(2,1)} %bitcast.78, bf16[576,1024]{1,0:T(8,128)(2,1)} %bitcast.109, bf16[576,1024]{1,0:T(8,128)(2,1)} %bitcast.111), custom_call_target="tpu_custom_call" | custom-call | flops 2717908992 | bytes 7372800 | tf_op jit(solution)/shard_map/weight_gradient/pallas_call | solution.py:597
  459.1 15.3 %weight_gradient.6 = bf16[2,1152,1728]{2,1,0:T(8,128)(2,1)} custom-call(bf16[1152,1024]{1,0:T(8,128)(2,1)} %get-tuple-element.159.left_ref, bf16[1728,1024]{1,0:T(8,128)(2,1)} %bitcast.76, bf16[1728,1024]{1,0:T(8,128)(2,1)} %bitcast.73), custom_call_target="tpu_custom_call" | custom-call | flops 8153726976 | bytes 17399808 | tf_op jit(solution)/shard_map/weight_gradient/pallas_call | solution.py:597
  476.3 111.9 %scatter_blocks.1 = (f32[72,1728]{1,0:T(8,128)}, f32[72,576]{1,0:T(8,128)}, f32[112,128]{1,0:T(8,128)}) custom-call(bf16[2,4,2,2,72,1728]{5,4,3,2,1,0:T(8,128)(2,1)} %bitcast.72, bf16[2,4,2,2,72,576]{5,4,3,2,1,0:T(8,128)(2,1)} %bitcast.77, f32[112,128]{1,0:T(8,128)} %pad_bitcast_fusion.refs_2_), custom_call_target="tpu_custom_call" | custom-call | bytes 9953280 | tf_op jit(solution)/shard_map/scatter_blocks/pallas_call | solution.py:557
  (182 shorter events, 57.5 us)
Async XLA Ops:
  7.2 185.9 %all-gather.8.cloned.1.call-start = ((), (), s32[]{:S(2)}) async-start(), calls=%async_computation.3 | async-start | bytes 10340352 | tf_op jit(solution)/shard_map/all_gather | solution.py:678
  82.6 173.9 %all-gather.6.cloned.1.call-start = ((), (), s32[]{:S(2)}) async-start(), calls=%async_computation.2 | async-start | bytes 10340352 | tf_op jit(solution)/shard_map/all_gather | solution.py:678
  83.4 391.1 %reduce-scatter.3.cloned.1.call-start = ((), (), s32[]{:S(2)}) async-start(), calls=%async_computation.4 | async-start | bytes 10948608 | tf_op jit(solution)/shard_map/scatter_project/reduce_scatter | solution.py:683
  87.2 7.7 %copy-start.28 = (f32[576]{0:T(1024)S(1)}, f32[576]{0:T(1024)}, u32[]{:S(2)}) copy-start(f32[576]{0:T(1024)} %param.23) | copy-start | bytes 6916
  87.2 7.9 %copy-start.29 = (f32[576]{0:T(1024)S(1)}, f32[576]{0:T(1024)}, u32[]{:S(2)}) copy-start(f32[576]{0:T(1024)} %param.26) | copy-start | bytes 6916
  87.2 8.2 %copy-start.22 = (f32[2152]{0:T(1024)S(1)}, f32[2152]{0:T(1024)}, u32[]{:S(2)}) copy-start(f32[2152]{0:T(1024)} %param.32) | copy-start | bytes 25828
  87.2 17.2 %copy-start.26 = (s32[2048]{0:T(1024)S(1)}, s32[2048]{0:T(1024)}, u32[]{:S(2)}) copy-start(s32[2048]{0:T(1024)} %param.19) | copy-start | bytes 24580
  90.1 94.7 %copy-start.2 = (bf16[1024,1152]{0,1:T(8,128)(2,1)}, bf16[1024,1152]{0,1:T(8,128)(2,1)S(1)}, u32[]{:S(2)}) copy-start(bf16[1024,1152]{0,1:T(8,128)(2,1)S(1)} %copy.64) | copy-start | bytes 7077892
  106.0 43.9 %copy-start.14 = (f32[1024]{0:T(1024)}, f32[1024]{0:T(1024)S(1)}, u32[]{:S(2)}) copy-start(f32[1024]{0:T(1024)S(1)} %broadcast_multiply_fusion.5) | copy-start | bytes 12292
  106.7 43.2 %copy-start.16 = (f32[1024]{0:T(1024)}, f32[1024]{0:T(1024)S(1)}, u32[]{:S(2)}) copy-start(f32[1024]{0:T(1024)S(1)} %add_rsqrt_fusion.1) | copy-start | bytes 12292
  158.8 26.0 %copy-start.32 = (f32[1152]{0:T(1024)S(1)}, f32[1152]{0:T(1024)}, u32[]{:S(2)}) copy-start(f32[1152]{0:T(1024)} %param.28) | copy-start | bytes 13828
  193.1 18.2 %copy-start.1 = (f32[1024,1152]{0,1:T(8,128)S(1)}, f32[1024,1152]{0,1:T(8,128)}, u32[]{:S(2)}) copy-start(f32[1024,1152]{0,1:T(8,128)} %copy-done) | copy-start | bytes 14155780
  193.1 18.2 %copy-start.30 = (bf16[2304,2152]{1,0:T(8,128)(2,1)S(1)}, bf16[2304,2152]{1,0:T(8,128)(2,1)}, u32[]{:S(2)}) copy-start(bf16[2304,2152]{1,0:T(8,128)(2,1)} %all-gather.8.cloned.1.call-done) | copy-start | bytes 29749252
  244.3 12.3 %copy-start.9 = (bf16[1024,1152]{1,0:T(8,128)(2,1)S(1)}, bf16[1024,1152]{1,0:T(8,128)(2,1)}, u32[]{:S(2)}) copy-start(bf16[1024,1152]{1,0:T(8,128)(2,1)} %param.35) | copy-start | bytes 7077892
  244.3 348.0 %reduce-scatter.5.cloned.1.call-start = ((), (), s32[]{:S(2)}) async-start(), calls=%async_computation.5 | async-start | bytes 10948608 | tf_op jit(solution)/shard_map/scatter_hidden/reduce_scatter | solution.py:683
  256.6 10.9 %copy-start.31 = (bf16[2304,2152]{1,0:T(8,128)(2,1)S(1)}, bf16[2304,2152]{1,0:T(8,128)(2,1)}, u32[]{:S(2)}) copy-start(bf16[2304,2152]{1,0:T(8,128)(2,1)} %all-gather.6.cloned.1.call-done) | copy-start | bytes 29749252
  299.8 11.2 %slice-start = ((s8[4718592]{0:T(1024)(128)(4,1)}), s8[524288]{0:T(1024)(128)(4,1)S(1)}, s32[]{:S(2)}) async-start(s8[4718592]{0:T(1024)(128)(4,1)} %bitcast.63), calls=%async_computation.6 | async-start | bytes 1048576
  299.9 11.2 %slice-start.1 = ((s8[4718592]{0:T(1024)(128)(4,1)}), s8[4194304]{0:T(1024)(128)(4,1)S(1)}, s32[]{:S(2)}) async-start(s8[4718592]{0:T(1024)(128)(4,1)} %bitcast.63), calls=%async_computation.7 | async-start | bytes 8388608
  299.9 24.6 %slice-start.6 = ((s8[10027008]{0:T(1024)(128)(4,1)}), s8[4194304]{0:T(1024)(128)(4,1)S(1)}, s32[]{:S(2)}) async-start(s8[10027008]{0:T(1024)(128)(4,1)} %bitcast.90), calls=%async_computation.12 | async-start | bytes 8388608
  299.9 24.6 %slice-start.7 = ((s8[10027008]{0:T(1024)(128)(4,1)}), s8[4194304]{0:T(1024)(128)(4,1)S(1)}, s32[]{:S(2)}) async-start(s8[10027008]{0:T(1024)(128)(4,1)} %bitcast.90), calls=%async_computation.13 | async-start | bytes 8388608
  311.0 13.5 %slice-start.8 = ((s8[10027008]{0:T(1024)(128)(4,1)}), s8[1638400]{0:T(1024)(128)(4,1)S(1)}, s32[]{:S(2)}) async-start(s8[10027008]{0:T(1024)(128)(4,1)} %bitcast.90), calls=%async_computation.14 | async-start | bytes 3276800
  324.5 9.0 %copy-start.33 = (f32[1152]{0:T(1024)S(1)}, f32[1152]{0:T(1024)}, u32[]{:S(2)}) copy-start(f32[1152]{0:T(1024)} %param.34) | copy-start | bytes 13828
  348.5 7.3 %copy-start.10 = (bf16[1,16,72,576]{3,2,1,0:T(8,128)(2,1)S(1)}, bf16[1,16,72,576]{3,2,1,0:T(8,128)(2,1)}, u32[]{:S(2)}) copy-start(bf16[1,16,72,576]{3,2,1,0:T(8,128)(2,1)} %get-tuple-element.157) | copy-start | bytes 3981316
  419.0 8.0 %copy-start.6 = (bf16[3,8,72,1024]{3,2,1,0:T(8,128)(2,1)S(1)}, bf16[3,8,72,1024]{3,2,1,0:T(8,128)(2,1)}, u32[]{:S(2)}) copy-start(bf16[3,8,72,1024]{3,2,1,0:T(8,128)(2,1)} %attention_backward.3) | copy-start | bytes 10616836
  419.0 18.6 %slice-start.2 = ((s8[4718592]{0:T(1024)(128)(4,1)}), s8[4194304]{0:T(1024)(128)(4,1)S(1)}, s32[]{:S(2)}) async-start(s8[4718592]{0:T(1024)(128)(4,1)} %bitcast.65), calls=%async_computation.8 | async-start | bytes 8388608
  419.0 18.6 %slice-start.4 = ((s8[4718592]{0:T(1024)(128)(4,1)}), s8[4194304]{0:T(1024)(128)(4,1)S(1)}, s32[]{:S(2)}) async-start(s8[4718592]{0:T(1024)(128)(4,1)} %bitcast.68), calls=%async_computation.10 | async-start | bytes 8388608
  427.0 6.7 %copy-start.3 = (bf16[1024,1152]{0,1:T(8,128)(2,1)S(1)}, bf16[1024,1152]{0,1:T(8,128)(2,1)}, u32[]{:S(2)}) copy-start(bf16[1024,1152]{0,1:T(8,128)(2,1)} %copy-done.2) | copy-start | bytes 7077892
  427.1 6.7 %copy-start.15 = (f32[1024]{0:T(1024)S(1)}, f32[1024]{0:T(1024)}, u32[]{:S(2)}) copy-start(f32[1024]{0:T(1024)} %copy-done.14) | copy-start | bytes 12292
  427.1 10.5 %slice-start.3 = ((s8[4718592]{0:T(1024)(128)(4,1)}), s8[524288]{0:T(1024)(128)(4,1)S(1)}, s32[]{:S(2)}) async-start(s8[4718592]{0:T(1024)(128)(4,1)} %bitcast.65), calls=%async_computation.9 | async-start | bytes 1048576
  427.1 10.5 %slice-start.5 = ((s8[4718592]{0:T(1024)(128)(4,1)}), s8[524288]{0:T(1024)(128)(4,1)S(1)}, s32[]{:S(2)}) async-start(s8[4718592]{0:T(1024)(128)(4,1)} %bitcast.68), calls=%async_computation.11 | async-start | bytes 1048576
  476.3 122.7 %copy-start.11 = (bf16[72,576]{1,0:T(8,128)(2,1)S(1)}, bf16[72,576]{1,0:T(8,128)(2,1)}, u32[]{:S(2)}) copy-start(bf16[72,576]{1,0:T(8,128)(2,1)} %param.22) | copy-start | bytes 248836
  476.3 122.7 %copy-start.12 = (bf16[72,576]{1,0:T(8,128)(2,1)S(1)}, bf16[72,576]{1,0:T(8,128)(2,1)}, u32[]{:S(2)}) copy-start(bf16[72,576]{1,0:T(8,128)(2,1)} %param.24) | copy-start | bytes 248836
  (15 other events, 55.6 us)
Sparse Core Ops, SparseCore 0:
  82.8 88.2 all-gather.7
  173.9 82.6 all-gather.5
  262.6 140.7 reduce-scatter.2
  409.3 164.0 reduce-scatter.4

commit v4 on v3

--- a/solution.py
+++ b/solution.py
@@ -18,6 +18,7 @@
 FEATURES = 16
 PICTURES = 10
 QUERY_BLOCK = 256
+FORWARD_BLOCK = 512
 SCALE = HEAD ** (-0.5)
 LOG2E = 1.0 / math.log(2.0)
 EXPONENT = SCALE * LOG2E
@@ -66,9 +67,12 @@
     query_rows = query_operand(query_ref[0, 0], mask_ref[...])
     key_rows = key_operand(key_ref[0, 0], key_mask_ref[...])
     value_rows = rows_below(value_ref[0, 0].astype(F32), [jnp.ones((1, 1), F32)]).astype(BF16)
-    for begin in range(0, HALF, QUERY_BLOCK):
-        block = slice(begin, begin + QUERY_BLOCK)
-        scores = dot(key_rows, query_rows[:, block])
+    blocks = [slice(begin, begin + FORWARD_BLOCK) for begin in range(0, HALF, FORWARD_BLOCK)]
+    following = dot(key_rows, query_rows[:, blocks[0]])
+    for number, block in enumerate(blocks):
+        scores = following
+        if number + 1 < len(blocks):
+            following = dot(key_rows, query_rows[:, blocks[number + 1]])
         top = jnp.max(scores, axis=0, keepdims=True)
         weights = jnp.exp2(scores - top).astype(BF16)
         summed = dot(value_rows, weights)
@@ -170,6 +174,8 @@
 
 
 LINE = 4
+LEVEL_G = 6
+LEVEL_S = 2
 MESH = pl.DeviceIdType.MESH
 
 
@@ -217,16 +223,25 @@
     return chunks
 
 
-def run_stages(stages, count):
-    for step in range(len(stages) + count - 1):
+def run_stages(stages, count, level, between=lambda step: None):
+    for stage in stages[:level]:
         for chunk in range(count):
-            if 0 <= step - chunk < len(stages):
-                stages[step - chunk](chunk)
+            stage(chunk)
+    rest = stages[level:]
+    for step in range(len(rest) + count - 1):
+        between(step)
+        for chunk in range(count):
+            if 0 <= step - chunk < len(rest):
+                rest[step - chunk](chunk)
 
 
 def gather_kernel(arrays, chunks, *refs):
-    shards, wholes = refs[:arrays], refs[arrays : 2 * arrays]
-    own_sem, z_send, z_recv, side_send, side_recv, core_send, core_recv = refs[2 * arrays :]
+    shards, lines = refs[:arrays], refs[arrays]
+    wholes, both = refs[arrays + 1 : 2 * arrays + 1], refs[2 * arrays + 1]
+    (
+        own_sem, z_send, z_recv, side_send, side_recv, core_send, core_recv, line_own, line_send,
+        line_recv,
+    ) = refs[2 * arrays + 2 :]
     z, x, y, core = place_of()
     other, across_x, across_y = neighbours(z, x, y, core)
 
@@ -341,31 +356,44 @@
                 along_z(a, zz, False, z).wait_send()
 
     enter(z, x, y, core)
+    own_lines = pltpu.make_async_copy(lines, both.at[y], line_own)
+    sent_lines = pltpu.make_async_remote_copy(
+        lines, both.at[y], line_send, line_recv, across_y, MESH
+    )
+    landed_lines = pltpu.make_async_remote_copy(
+        lines, both.at[1 - y], line_send, line_recv, across_y, MESH
+    )
+    own_lines.start()
+    sent_lines.start()
     hops = [partial(stage_hop, hop=hop) for hop in range(1, LINE)]
-    run_stages([stage_begin, *hops, stage_turn, stage_last, stage_close], len(chunks))
-
-
-def gather_blocks(shards, pieces, mp):
+    run_stages([stage_begin, *hops, stage_turn, stage_last, stage_close], len(chunks), LEVEL_G)
+    own_lines.wait()
+    sent_lines.wait_send()
+    landed_lines.wait_recv()
+
+
+def gather_blocks(shards, pieces, lines, mp):
     rows, dp = shards[0].shape[0], 16
     chunks = chunks_of([item.shape[1] for item in shards], pieces)
     count = len(chunks)
     anywhere = pl.BlockSpec(memory_space=pl.ANY)
     dma = pltpu.SemaphoreType.DMA
     sent = sum(item.size * 2 for item in shards) * 15
-    wholes = pl.pallas_call(
+    *wholes, both = pl.pallas_call(
         partial(gather_kernel, len(shards), chunks),
-        in_specs=[anywhere] * len(shards),
-        out_specs=[anywhere] * len(shards),
-        out_shape=[jax.ShapeDtypeStruct((mp, dp, rows, item.shape[1]), BF16) for item in shards],
+        in_specs=[anywhere] * (len(shards) + 1),
+        out_specs=[anywhere] * (len(shards) + 1),
+        out_shape=[jax.ShapeDtypeStruct((mp, dp, rows, item.shape[1]), BF16) for item in shards]
+        + [jax.ShapeDtypeStruct((mp, *lines.shape), F32)],
         scratch_shapes=[
             dma((count,)), dma((count, LINE, 2)), dma((count, LINE)), dma((count, 2, 8)),
-            dma((count, 2, 8)), dma((count, 16)), dma((count, 16)),
+            dma((count, 2, 8)), dma((count, 16)), dma((count, 16)), dma(()), dma(()), dma(()),
         ],
         compiler_params=pltpu.CompilerParams(collective_id=0, has_side_effects=True),
         cost_estimate=pl.CostEstimate(flops=0, bytes_accessed=sent, transcendentals=0),
         name="gather_blocks",
-    )(*shards)
-    return [whole.reshape(mp, dp * rows, whole.shape[-1]) for whole in wholes]
+    )(*shards, lines)
+    return [whole.reshape(mp, dp * rows, whole.shape[-1]) for whole in wholes], both
 
 
 def scatter_kernel(arrays, chunks, *refs):
@@ -534,11 +562,7 @@
     enter(z, x, y, core, leap)
     line = [partial(stage_line, hop=hop) for hop in range(LINE - 1)]
     stages = [stage_begin, stage_share, stage_one, stage_two, *line, stage_finish, stage_close]
-    for step in range(len(stages) + count - 1):
-        vector_step(step)
-        for chunk in range(count):
-            if 0 <= step - chunk < len(stages):
-                stages[step - chunk](chunk)
+    run_stages(stages, count, LEVEL_S, vector_step)
 
 
 def scatter_blocks(parts, pieces, vector, mp):
@@ -625,12 +649,11 @@
 
 
 def gelu_parts(rows):
-    cubic = math.sqrt(2.0 / math.pi) * (rows + 0.044715 * rows * rows * rows)
-    bend = jnp.tanh(cubic)
-    value = 0.5 * rows * (1.0 + bend)
-    slope = 0.5 * (1.0 + bend) + 0.5 * rows * (1.0 - bend * bend) * (
-        math.sqrt(2.0 / math.pi) * (1.0 + 3.0 * 0.044715 * rows * rows)
-    )
+    base = math.sqrt(2.0 / math.pi)
+    square = rows * rows
+    share = 0.5 * jnp.tanh(rows * (base + (base * 0.044715) * square)) + 0.5
+    value = rows * share
+    slope = share + value * (1.0 - share) * (2.0 * base + (6.0 * base * 0.044715) * square)
     return value, slope
 
 
@@ -699,23 +722,28 @@
         part = lax.all_to_all(part, "mp", 0, 0, axis_index_groups=groups, tiled=True)
         return part.transpose(1, 0, 2, 3, 4).reshape(kinds, HEADS, HEAD, tokens)
 
-    query_bias_all, value_bias_all, hidden_bias_all = (
-        lax.all_gather(item, "mp", axis=0, tiled=False)
-        for item in (query_bias, value_bias, hidden_bias)
-    )
     half = me // group
     starts = lax.dynamic_slice_in_dim(picture_start, half * HALF, HALF)
     masks = picture_masks(starts)
 
     attn_shard = jnp.concatenate([query_weight, key_weight, value_weight], axis=1)
+    biases = jnp.concatenate([query_bias, value_bias, hidden_bias])
     if fitted:
-        attn_weights, output_all = gather_blocks([attn_shard, output_weight.T], (2, 2), mp)
+        lines = jnp.pad(biases, (0, -biases.shape[0] % 1024)).reshape(-1, 128)
+        (attn_weights, output_all), both = gather_blocks(
+            [attn_shard, output_weight.T], (2, 2), lines, mp
+        )
+        biases_all = both.reshape(mp, -1)
         attn_weights, hidden_shard, project_shard = lax.optimization_barrier(
             (attn_weights, hidden_weight, project_weight)
         )
     else:
         attn_weights, output_all = gather(attn_shard), gather(output_weight.T)
         hidden_shard, project_shard = hidden_weight, project_weight
+        biases_all = lax.all_gather(biases, "mp", axis=0, tiled=False)
+    query_bias_all = biases_all[:, :shard]
+    value_bias_all = biases_all[:, shard : 2 * shard]
+    hidden_bias_all = biases_all[:, 2 * shard : 2 * shard + hidden]
     hidden_all = gather(hidden_shard)
     project_all = gather(project_shard.T)
 

time: 618 us -> 604 us (0.977)
  Pallas kernels: 347 us -> 319 us
  waiting for transfers between devices: 6.68 us -> 29 us
  blocking collectives: 8.41 us -> 0 us
  matrix products: 149 us -> 156 us
    all_gather x2, waiting for transfers between devices: 5.92 us -> 28.2 us  [gather(): whole = lax.all_gather(weight, ('mp', 'dp'), axis=0, tiled=True)]
    pallas_call x2, Pallas kernels: 51.7 us -> 29.7 us  [attention_forward(): pl.pallas_call(forward_kernel, grid=(heads,), in_specs=[features, feature...]
    pallas_call x1, Pallas kernels: 73.6 us -> 64.4 us  [gather_blocks(): pl.pallas_call(partial(gather_kernel, len(shards), chunks), in_specs=[any...]
    unnamed x1 -> x0, blocking collectives: 8.41 us -> none
    dot_general x16, matrix products: 149 us -> 156 us  [dot(): lax.dot_general(left, right, (((left_dim,), (right_dim,)), ((), ())), pre...]
    unnamed x98 -> x88, local copies, waits for them, and re-layouts: 27.5 us -> 25.4 us
  transfers between devices with their start and end apart: 4 -> 4, of which waited for: 1 -> 2; matrix products, arithmetic and copies ran while one was open for 35% -> 37% of each run, Pallas kernels for 45% -> 42%
where the time goes in v4:
time: 604 us; the launch traced here: 600 us
  Pallas kernels  319 us (53%)
  matrix products  156 us (26%)
  local copies, waits for them, and re-layouts  42.1 us (7%)
  other arithmetic  38.2 us (6%)
  waiting for transfers between devices  29 us (5%)
  between operations  14.8 us (2%)
    dot_general x16, matrix products, dot(): lax.dot_general(left, right, (((left_dim,), (right_dim,)), ((), ())), pre...  156 us
    pallas_call x1, Pallas kernels, scatter_blocks(): pl.pallas_call(partial(scatter_kernel, len(parts), chunks), in_specs=[pl....  115 us
    pallas_call x1, Pallas kernels, gather_blocks(): pl.pallas_call(partial(gather_kernel, len(shards), chunks), in_specs=[any...  64.4 us
    pallas_call x4, Pallas kernels, weight_gradient(): pl.pallas_call(partial(gradient_kernel, count), grid=(count, width // til...  60.1 us
    pallas_call x2, Pallas kernels, attention_backward(): pl.pallas_call(backward_kernel, grid=(heads,), in_specs=[features, featur...  49.7 us
    pallas_call x2, Pallas kernels, attention_forward(): pl.pallas_call(forward_kernel, grid=(heads,), in_specs=[features, feature...  29.7 us
    all_gather x2, waiting for transfers between devices, gather(): whole = lax.all_gather(weight, ('mp', 'dp'), axis=0, tiled=True)  28.2 us
    unnamed x88, local copies, waits for them, and re-layouts  25.4 us
  transfers between devices with their start and end apart: 4, of which 2 were waited for; matrix products, arithmetic and copies ran while one was open for 37% of the time, Pallas kernels for 42%

profile of v4, /device:TPU:0, one launch (start us, length us, event | category | flops | bytes accessed | tf_op | source)
XLA Modules:
  0.0 599.9 jit_solution(9774426828553575324)
XLA Ops:
  10.5 64.4 %gather_blocks.1 = (bf16[2,16,72,1728]{3,2,1,0:T(8,128)(2,1)}, bf16[2,16,72,576]{3,2,1,0:T(8,128)(2,1)}, f32[2,32,128]{2,1,0:T(8,128)}) custom-call(bf16[72,1728]{1,0:T(8,128)(2,1)} %concatenate.26.refs_0_, bf16[72,576]{1,0:T(8,128)(2,1)} %bitcast.94, f32[32,128]{1,0:T(8,128)} %pad_bitcast_fusion.1.refs_2_), custom_call_target="tpu_custom_call" | custom-call | bytes 4976640 | tf_op jit(solution)/shard_map/gather_blocks/pallas_call | solution.py:382
  79.9 4.8 copy.67
  89.9 9.0 %add_convert_fusion.3 = bf16[1728,1024]{1,0:T(8,128)(2,1)} fusion(f32[1728]{0:T(1024)S(1)} %concatenate.28, bf16[2,1152,1728]{2,1,0:T(8,128)(2,1)} %bitcast.99, bf16[1024,1152]{0,1:T(8,128)(2,1)S(1)} %copy.64, f32[1152]{0:T(1024)S(1)} %copy-done.23, f32[1152]{0:T(1024)S(1)} %copy-done.18, f32[1024]{0:T(1024)S(1)} %add_rsqrt_fusion.1, ...), kind=kOutput, calls=%fused_computation.15 | convolution fusion | flops 4087480320 | bytes 10051328 | tf_op jit(solution)/shard_map/dot_general | solution.py:30
  98.9 15.0 %attention_forward.2 = (bf16[8,72,1024]{2,1,0:T(8,128)(2,1)}, f32[8,1,1024]{2,1,0:T(1,128)}, f32[8,1,1024]{2,1,0:T(1,128)}) custom-call(f32[16,1024]{1,0:T(8,128)} %get-tuple-element.183.mask_ref, f32[16,1024]{1,0:T(8,128)} %get-tuple-element.182.key_mask_ref, bf16[3,8,72,1024]{3,2,1,0:T(8,128)(2,1)} %bitcast.103, bf16[3,8,72,1024]{3,2,1,0:T(8,128)(2,1)} %bitcast.104, ...), custom_call_target="tpu_custom_call" | custom-call | flops 8589934592 | bytes 4718592 | tf_op jit(solution)/shard_map/attention_forward/pallas_call | solution.py:129
  113.9 5.9 fusion.62
  119.8 9.0 %add_convert_fusion.2 = bf16[1728,1024]{1,0:T(8,128)(2,1)} fusion(f32[1728]{0:T(1024)S(1)} %concatenate.29, bf16[2,1152,1728]{2,1,0:T(8,128)(2,1)} %bitcast.100, bf16[1024,1152]{0,1:T(8,128)(2,1)S(1)} %copy.64, f32[1152]{0:T(1024)S(1)} %copy-done.23, f32[1152]{0:T(1024)S(1)} %copy-done.18, f32[1024]{0:T(1024)S(1)} %add_rsqrt_fusion.1, ...), kind=kOutput, calls=%fused_computation.14 | convolution fusion | flops 4087480320 | bytes 10051328 | tf_op jit(solution)/shard_map/dot_general | solution.py:30
  128.8 14.7 %attention_forward.3 = (bf16[8,72,1024]{2,1,0:T(8,128)(2,1)}, f32[8,1,1024]{2,1,0:T(1,128)}, f32[8,1,1024]{2,1,0:T(1,128)}) custom-call(f32[16,1024]{1,0:T(8,128)} %get-tuple-element.183.mask_ref, f32[16,1024]{1,0:T(8,128)} %get-tuple-element.182.key_mask_ref, bf16[3,8,72,1024]{3,2,1,0:T(8,128)(2,1)} %bitcast.109, bf16[3,8,72,1024]{3,2,1,0:T(8,128)(2,1)} %bitcast.110, ...), custom_call_target="tpu_custom_call" | custom-call | flops 8589934592 | bytes 4718592 | tf_op jit(solution)/shard_map/attention_forward/pallas_call | solution.py:129
  143.6 5.4 fusion.61
  151.7 7.7 %all-gather.5.cloned.1.call-done = bf16[2304,2152]{1,0:T(8,128)(2,1)} async-done(((bf16[72,2152]{1,0:T(8,128)(2,1)}), bf16[2304,2152]{1,0:T(8,128)(2,1)}) %all-gather.5.cloned.1.call-update) | async-done | bytes 9916432 | tf_op jit(solution)/shard_map/all_gather | solution.py:701
  159.5 27.3 %add_convert_fusion.1 = (bf16[2152,1024]{1,0:T(8,128)(2,1)}, bf16[2152,1024]{1,0:T(8,128)(2,1)}) fusion(f32[2152]{0:T(1024)S(1)} %get-tuple-element.149, bf16[2304,2152]{1,0:T(8,128)(2,1)} %all-gather.5.cloned.1.call-done, f32[1024,1152]{0,1:T(8,128)} %copy-done, f32[1152]{0:T(1024)S(1)} %copy-done.27, f32[1152]{0:T(1024)S(1)} %copy-done.13, ...), kind=kOutput, calls=%fused_computation.5 | convolution fusion | flops 5118361600 | bytes 18572704 | tf_op jit(solution)/shard_map/dot_general | solution.py:30
  186.8 13.4 %add_convert_fusion = (bf16[2152,1024]{1,0:T(8,128)(2,1)}, bf16[2152,1024]{1,0:T(8,128)(2,1)}) fusion(f32[2152]{0:T(1024)S(1)} %get-tuple-element.148, bf16[2304,2152]{1,0:T(8,128)(2,1)S(1)} %copy-done.28, f32[1024,1152]{0,1:T(8,128)S(1)} %copy-done.1, f32[1152]{0:T(1024)S(1)} %copy-done.27, f32[1152]{0:T(1024)S(1)} %copy-done.13, ...), kind=kOutput, calls=%fused_computation.4 | convolution fusion | flops 5118361600 | bytes 18583552 | tf_op jit(solution)/shard_map/dot_general | solution.py:30
  200.2 17.9 %weight_gradient.4 = bf16[2,1152,2304]{2,1,0:T(8,128)(2,1)} custom-call(bf16[1152,1024]{1,0:T(8,128)(2,1)} %bitcast.71, bf16[2152,1024]{1,0:T(8,128)(2,1)} %get-tuple-element.65.refs_0_, bf16[2152,1024]{1,0:T(8,128)(2,1)} %get-tuple-element.66.refs_1_), custom_call_target="tpu_custom_call" | custom-call | flops 10154409984 | bytes 21790720 | tf_op jit(solution)/shard_map/weight_gradient/pallas_call | solution.py:621
  224.5 20.5 %all-gather.3.cloned.1.call-done = bf16[2304,2152]{1,0:T(8,128)(2,1)} async-done(((bf16[72,2152]{1,0:T(8,128)(2,1)}), bf16[2304,2152]{1,0:T(8,128)(2,1)}) %all-gather.3.cloned.1.call-update) | async-done | bytes 9916432 | tf_op jit(solution)/shard_map/all_gather | solution.py:701
  245.1 10.9 %multiply_convert_fusion.refs_1_ = bf16[2152,1024]{1,0:T(8,128)(2,1)} fusion(bf16[2152,1024]{1,0:T(8,128)(2,1)} %get-tuple-element.62, bf16[1024,1152]{1,0:T(8,128)(2,1)S(1)} %copy-done.9, bf16[2304,2152]{1,0:T(8,128)(2,1)} %all-gather.3.cloned.1.call-done), kind=kOutput, calls=%fused_computation.2 | convolution fusion | flops 5083815936 | bytes 16187392 | tf_op jit(solution)/shard_map/dot_general | solution.py:30
  255.9 9.6 %multiply_convert_fusion.1.refs_0_ = bf16[2152,1024]{1,0:T(8,128)(2,1)} fusion(bf16[2152,1024]{1,0:T(8,128)(2,1)} %get-tuple-element.61, bf16[1024,1152]{1,0:T(8,128)(2,1)S(1)} %copy-done.9, bf16[2304,2152]{1,0:T(8,128)(2,1)S(1)} %copy-done.29), kind=kOutput, calls=%fused_computation.3 | convolution fusion | flops 5083815936 | bytes 16187392 | tf_op jit(solution)/shard_map/dot_general | solution.py:30
  265.6 18.1 %weight_gradient.5 = bf16[2,1152,2304]{2,1,0:T(8,128)(2,1)} custom-call(bf16[1152,1024]{1,0:T(8,128)(2,1)} %fusion.81.left_ref, bf16[2152,1024]{1,0:T(8,128)(2,1)} %multiply_convert_fusion.1.refs_0_, bf16[2152,1024]{1,0:T(8,128)(2,1)} %multiply_convert_fusion.refs_1_), custom_call_target="tpu_custom_call" | custom-call | flops 10154409984 | bytes 21790720 | tf_op jit(solution)/shard_map/weight_gradient/pallas_call | solution.py:621
  288.4 11.1 %fusion.24 = f32[1024,1152]{0,1:T(8,128)} fusion(bf16[2152,1024]{1,0:T(8,128)(2,1)} %multiply_convert_fusion.1.refs_0_, bf16[2304,2152]{1,0:T(8,128)(2,1)} %all-gather.5.cloned.1.call-done), kind=kOutput, calls=%fused_computation.50 | convolution fusion | flops 5077204992 | bytes 14139392 | tf_op jit(solution)/shard_map/dot_general | solution.py:30
  299.6 13.5 %multiply_reduce_fusion = (f32[1152]{0:T(1024)S(1)}, f32[1024]{0:T(1024)S(1)}, f32[1024]{0:T(1024)S(1)}, f32[1152]{0:T(1024)S(1)}, f32[1024,1152]{0,1:T(8,128)}) fusion(f32[1024,1152]{0,1:T(8,128)S(1)} %bitcast.68, f32[1024]{0:T(1024)S(1)} %add_rsqrt_fusion, f32[1024]{0:T(1024)S(1)} %broadcast_multiply_fusion.4, f32[1152]{0:T(1024)S(1)} %copy-done.13, ...), kind=kOutput, calls=%fused_computation.36 | convolution fusion | flops 5088997376 | bytes 23606784 | tf_op jit(solution)/shard_map/dot_general | solution.py:30
  313.1 9.0 %fusion.28 = f32[1024,1152]{0,1:T(8,128)} fusion(bf16[2152,1024]{1,0:T(8,128)(2,1)} %get-tuple-element.65.refs_0_, bf16[2304,2152]{1,0:T(8,128)(2,1)S(1)} %bitcast.98), kind=kOutput, calls=%fused_computation.54 | convolution fusion | flops 5077204992 | bytes 14139392 | tf_op jit(solution)/shard_map/dot_general | solution.py:30
  322.1 10.2 %add_convert_fusion.4 = bf16[1024,1152]{0,1:T(8,128)(2,1)} fusion(f32[1024,1152]{0,1:T(8,128)S(1)} %bitcast.68, f32[1024,1152]{0,1:T(8,128)} %fusion.28, bf16[2152,1024]{1,0:T(8,128)(2,1)} %get-tuple-element.66.refs_1_, bf16[2304,2152]{1,0:T(8,128)(2,1)S(1)} %bitcast.98, f32[1152]{0:T(1024)S(1)} %copy-done.31), kind=kOutput, calls=%fused_computation.39 | convolution fusion | flops 5081923584 | bytes 21225472 | tf_op jit(solution)/shard_map/dot_general | solution.py:30
  332.3 4.7 copy.75
  337.0 5.8 convert_reduce_fusion.6
  347.1 24.9 %attention_backward.3 = bf16[3,8,72,1024]{3,2,1,0:T(8,128)(2,1)} custom-call(f32[16,1024]{1,0:T(8,128)} %get-tuple-element.183.mask_ref, f32[16,1024]{1,0:T(8,128)} %get-tuple-element.182.key_mask_ref, bf16[3,8,72,1024]{3,2,1,0:T(8,128)(2,1)} %bitcast.112, bf16[3,8,72,1024]{3,2,1,0:T(8,128)(2,1)} %bitcast.113, bf16[3,8,72,1024]{3,2,1,0:T(8,128)(2,1)} %bitcast.114, ...), custom_call_target="tpu_custom_call" | custom-call | flops 21474836480 | bytes 9437184 | tf_op jit(solution)/shard_map/attention_backward/pallas_call | solution.py:150
  374.7 4.9 convolution_convert_fusion.1
  379.6 24.8 %attention_backward.2 = bf16[3,8,72,1024]{3,2,1,0:T(8,128)(2,1)} custom-call(f32[16,1024]{1,0:T(8,128)} %get-tuple-element.183.mask_ref, f32[16,1024]{1,0:T(8,128)} %get-tuple-element.182.key_mask_ref, bf16[3,8,72,1024]{3,2,1,0:T(8,128)(2,1)} %bitcast.106, bf16[3,8,72,1024]{3,2,1,0:T(8,128)(2,1)} %bitcast.107, bf16[3,8,72,1024]{3,2,1,0:T(8,128)(2,1)} %bitcast.108, ...), custom_call_target="tpu_custom_call" | custom-call | flops 21474836480 | bytes 9437184 | tf_op jit(solution)/shard_map/attention_backward/pallas_call | solution.py:150
  407.6 8.0 %fusion.34 = f32[1024,1152]{0,1:T(8,128)S(1)} fusion(bf16[1728,1024]{1,0:T(8,128)(2,1)} %bitcast.79, bf16[2,1152,1728]{2,1,0:T(8,128)(2,1)} %bitcast.101), kind=kOutput, calls=%fused_computation.64 | convolution fusion | flops 4076863488 | bytes 12386304 | tf_op jit(solution)/shard_map/dot_general | solution.py:30
  415.7 6.6 %convolution_add_fusion = f32[1024,1152]{0,1:T(8,128)S(1)} fusion(f32[1024,1152]{0,1:T(8,128)S(1)} %fusion.34, bf16[1728,1024]{1,0:T(8,128)(2,1)S(1)} %bitcast.78, bf16[2,1152,1728]{2,1,0:T(8,128)(2,1)} %bitcast.102), kind=kOutput, calls=%fused_computation.42 | convolution fusion | flops 4078043136 | bytes 17104896 | tf_op jit(solution)/shard_map/dot_general | solution.py:30
  426.2 5.7 convert_reduce_fusion.5
  431.9 6.2 %copy.76 = f32[1024,1152]{1,0:T(8,128)} copy(f32[1024,1152]{0,1:T(8,128)} %get-tuple-element.166) | data formatting | bytes 9437184
  438.9 8.8 %weight_gradient.7 = bf16[2,1152,576]{2,1,0:T(8,128)(2,1)} custom-call(bf16[1152,1024]{1,0:T(8,128)(2,1)} %bitcast.82, bf16[576,1024]{1,0:T(8,128)(2,1)} %bitcast.116, bf16[576,1024]{1,0:T(8,128)(2,1)} %bitcast.118), custom_call_target="tpu_custom_call" | custom-call | flops 2717908992 | bytes 7372800 | tf_op jit(solution)/shard_map/weight_gradient/pallas_call | solution.py:621
  447.7 15.3 %weight_gradient.6 = bf16[2,1152,1728]{2,1,0:T(8,128)(2,1)} custom-call(bf16[1152,1024]{1,0:T(8,128)(2,1)} %get-tuple-element.164.left_ref, bf16[1728,1024]{1,0:T(8,128)(2,1)} %bitcast.80, bf16[1728,1024]{1,0:T(8,128)(2,1)} %bitcast.77), custom_call_target="tpu_custom_call" | custom-call | flops 8153726976 | bytes 17399808 | tf_op jit(solution)/shard_map/weight_gradient/pallas_call | solution.py:621
  464.8 115.0 %scatter_blocks.1 = (f32[72,1728]{1,0:T(8,128)}, f32[72,576]{1,0:T(8,128)}, f32[112,128]{1,0:T(8,128)}) custom-call(bf16[2,4,2,2,72,1728]{5,4,3,2,1,0:T(8,128)(2,1)} %bitcast.76, bf16[2,4,2,2,72,576]{5,4,3,2,1,0:T(8,128)(2,1)} %bitcast.81, f32[112,128]{1,0:T(8,128)} %pad_bitcast_fusion.refs_2_), custom_call_target="tpu_custom_call" | custom-call | bytes 9953280 | tf_op jit(solution)/shard_map/scatter_blocks/pallas_call | solution.py:581
  (173 shorter events, 57.0 us)
Async XLA Ops:
  7.2 152.2 %all-gather.5.cloned.1.call-start = ((), (), s32[]{:S(2)}) async-start(), calls=%async_computation.3 | async-start | bytes 10340352 | tf_op jit(solution)/shard_map/all_gather | solution.py:701
  74.9 170.2 %all-gather.3.cloned.1.call-start = ((), (), s32[]{:S(2)}) async-start(), calls=%async_computation.2 | async-start | bytes 10340352 | tf_op jit(solution)/shard_map/all_gather | solution.py:701
  75.6 387.4 %reduce-scatter.3.cloned.1.call-start = ((), (), s32[]{:S(2)}) async-start(), calls=%async_computation.4 | async-start | bytes 10948608 | tf_op jit(solution)/shard_map/scatter_project/reduce_scatter | solution.py:706
  77.1 7.7 %copy-start.22 = (f32[2,32,128]{2,1,0:T(8,128)S(1)}, f32[2,32,128]{2,1,0:T(8,128)}, u32[]{:S(2)}) copy-start(f32[2,32,128]{2,1,0:T(8,128)} %get-tuple-element.52) | copy-start | bytes 98308
  77.1 8.0 %copy-start.26 = (s32[2048]{0:T(1024)S(1)}, s32[2048]{0:T(1024)}, u32[]{:S(2)}) copy-start(s32[2048]{0:T(1024)} %param.19) | copy-start | bytes 24580
  79.9 63.6 %copy-start.2 = (bf16[1024,1152]{0,1:T(8,128)(2,1)}, bf16[1024,1152]{0,1:T(8,128)(2,1)S(1)}, u32[]{:S(2)}) copy-start(bf16[1024,1152]{0,1:T(8,128)(2,1)S(1)} %copy.64) | copy-start | bytes 7077892
  86.6 33.2 %copy-start.14 = (f32[1024]{0:T(1024)}, f32[1024]{0:T(1024)S(1)}, u32[]{:S(2)}) copy-start(f32[1024]{0:T(1024)S(1)} %broadcast_multiply_fusion.5) | copy-start | bytes 12292
  87.3 32.5 %copy-start.16 = (f32[1024]{0:T(1024)}, f32[1024]{0:T(1024)S(1)}, u32[]{:S(2)}) copy-start(f32[1024]{0:T(1024)S(1)} %add_rsqrt_fusion.1) | copy-start | bytes 12292
  128.8 14.7 %copy-start.30 = (f32[1152]{0:T(1024)S(1)}, f32[1152]{0:T(1024)}, u32[]{:S(2)}) copy-start(f32[1152]{0:T(1024)} %param.28) | copy-start | bytes 13828
  149.0 10.4 %copy-start.13 = (f32[1152]{0:T(1024)S(1)}, f32[1152]{0:T(1024)}, u32[]{:S(2)}) copy-start(f32[1152]{0:T(1024)} %param.29) | copy-start | bytes 13828
  149.0 10.4 %copy-start.27 = (f32[1152]{0:T(1024)S(1)}, f32[1152]{0:T(1024)}, u32[]{:S(2)}) copy-start(f32[1152]{0:T(1024)} %param.30) | copy-start | bytes 13828
  159.4 27.4 %copy-start.1 = (f32[1024,1152]{0,1:T(8,128)S(1)}, f32[1024,1152]{0,1:T(8,128)}, u32[]{:S(2)}) copy-start(f32[1024,1152]{0,1:T(8,128)} %copy-done) | copy-start | bytes 14155780
  159.4 27.4 %copy-start.28 = (bf16[2304,2152]{1,0:T(8,128)(2,1)S(1)}, bf16[2304,2152]{1,0:T(8,128)(2,1)}, u32[]{:S(2)}) copy-start(bf16[2304,2152]{1,0:T(8,128)(2,1)} %all-gather.5.cloned.1.call-done) | copy-start | bytes 29749252
  218.2 26.9 %copy-start.9 = (bf16[1024,1152]{1,0:T(8,128)(2,1)S(1)}, bf16[1024,1152]{1,0:T(8,128)(2,1)}, u32[]{:S(2)}) copy-start(bf16[1024,1152]{1,0:T(8,128)(2,1)} %param.35) | copy-start | bytes 7077892
  218.2 365.6 %reduce-scatter.5.cloned.1.call-start = ((), (), s32[]{:S(2)}) async-start(), calls=%async_computation.5 | async-start | bytes 10948608 | tf_op jit(solution)/shard_map/scatter_hidden/reduce_scatter | solution.py:706
  245.0 10.9 %copy-start.29 = (bf16[2304,2152]{1,0:T(8,128)(2,1)S(1)}, bf16[2304,2152]{1,0:T(8,128)(2,1)}, u32[]{:S(2)}) copy-start(bf16[2304,2152]{1,0:T(8,128)(2,1)} %all-gather.3.cloned.1.call-done) | copy-start | bytes 29749252
  288.3 11.2 %slice-start = ((s8[4718592]{0:T(1024)(128)(4,1)}), s8[524288]{0:T(1024)(128)(4,1)S(1)}, s32[]{:S(2)}) async-start(s8[4718592]{0:T(1024)(128)(4,1)} %bitcast.67), calls=%async_computation.6 | async-start | bytes 1048576
  288.4 11.2 %slice-start.1 = ((s8[4718592]{0:T(1024)(128)(4,1)}), s8[4194304]{0:T(1024)(128)(4,1)S(1)}, s32[]{:S(2)}) async-start(s8[4718592]{0:T(1024)(128)(4,1)} %bitcast.67), calls=%async_computation.7 | async-start | bytes 8388608
  288.4 24.7 %slice-start.6 = ((s8[10027008]{0:T(1024)(128)(4,1)}), s8[4194304]{0:T(1024)(128)(4,1)S(1)}, s32[]{:S(2)}) async-start(s8[10027008]{0:T(1024)(128)(4,1)} %bitcast.97), calls=%async_computation.12 | async-start | bytes 8388608
  288.4 24.7 %slice-start.7 = ((s8[10027008]{0:T(1024)(128)(4,1)}), s8[4194304]{0:T(1024)(128)(4,1)S(1)}, s32[]{:S(2)}) async-start(s8[10027008]{0:T(1024)(128)(4,1)} %bitcast.97), calls=%async_computation.13 | async-start | bytes 8388608
  299.6 13.5 %slice-start.8 = ((s8[10027008]{0:T(1024)(128)(4,1)}), s8[1638400]{0:T(1024)(128)(4,1)S(1)}, s32[]{:S(2)}) async-start(s8[10027008]{0:T(1024)(128)(4,1)} %bitcast.97), calls=%async_computation.14 | async-start | bytes 3276800
  313.1 9.0 %copy-start.31 = (f32[1152]{0:T(1024)S(1)}, f32[1152]{0:T(1024)}, u32[]{:S(2)}) copy-start(f32[1152]{0:T(1024)} %param.34) | copy-start | bytes 13828
  337.0 7.3 %copy-start.10 = (bf16[1,16,72,576]{3,2,1,0:T(8,128)(2,1)S(1)}, bf16[1,16,72,576]{3,2,1,0:T(8,128)(2,1)}, u32[]{:S(2)}) copy-start(bf16[1,16,72,576]{3,2,1,0:T(8,128)(2,1)} %get-tuple-element.162) | copy-start | bytes 3981316
  407.6 8.0 %copy-start.6 = (bf16[3,8,72,1024]{3,2,1,0:T(8,128)(2,1)S(1)}, bf16[3,8,72,1024]{3,2,1,0:T(8,128)(2,1)}, u32[]{:S(2)}) copy-start(bf16[3,8,72,1024]{3,2,1,0:T(8,128)(2,1)} %attention_backward.3) | copy-start | bytes 10616836
  407.6 18.6 %slice-start.2 = ((s8[4718592]{0:T(1024)(128)(4,1)}), s8[4194304]{0:T(1024)(128)(4,1)S(1)}, s32[]{:S(2)}) async-start(s8[4718592]{0:T(1024)(128)(4,1)} %bitcast.69), calls=%async_computation.8 | async-start | bytes 8388608
  407.6 18.6 %slice-start.4 = ((s8[4718592]{0:T(1024)(128)(4,1)}), s8[4194304]{0:T(1024)(128)(4,1)S(1)}, s32[]{:S(2)}) async-start(s8[4718592]{0:T(1024)(128)(4,1)} %bitcast.72), calls=%async_computation.10 | async-start | bytes 8388608
  415.6 6.7 %copy-start.3 = (bf16[1024,1152]{0,1:T(8,128)(2,1)S(1)}, bf16[1024,1152]{0,1:T(8,128)(2,1)}, u32[]{:S(2)}) copy-start(bf16[1024,1152]{0,1:T(8,128)(2,1)} %copy-done.2) | copy-start | bytes 7077892
  415.6 6.7 %copy-start.15 = (f32[1024]{0:T(1024)S(1)}, f32[1024]{0:T(1024)}, u32[]{:S(2)}) copy-start(f32[1024]{0:T(1024)} %copy-done.14) | copy-start | bytes 12292
  415.6 10.5 %slice-start.3 = ((s8[4718592]{0:T(1024)(128)(4,1)}), s8[524288]{0:T(1024)(128)(4,1)S(1)}, s32[]{:S(2)}) async-start(s8[4718592]{0:T(1024)(128)(4,1)} %bitcast.69), calls=%async_computation.9 | async-start | bytes 1048576
  415.7 10.5 %slice-start.5 = ((s8[4718592]{0:T(1024)(128)(4,1)}), s8[524288]{0:T(1024)(128)(4,1)S(1)}, s32[]{:S(2)}) async-start(s8[4718592]{0:T(1024)(128)(4,1)} %bitcast.72), calls=%async_computation.11 | async-start | bytes 1048576
  464.8 125.7 %copy-start.11 = (bf16[72,576]{1,0:T(8,128)(2,1)S(1)}, bf16[72,576]{1,0:T(8,128)(2,1)}, u32[]{:S(2)}) copy-start(bf16[72,576]{1,0:T(8,128)(2,1)} %param.22) | copy-start | bytes 248836
  464.8 125.7 %copy-start.12 = (bf16[72,576]{1,0:T(8,128)(2,1)S(1)}, bf16[72,576]{1,0:T(8,128)(2,1)}, u32[]{:S(2)}) copy-start(bf16[72,576]{1,0:T(8,128)(2,1)} %param.24) | copy-start | bytes 248836
  (13 other events, 50.1 us)
Sparse Core Ops, SparseCore 0:
  75.0 84.4 all-gather.4
  162.3 82.7 all-gather.2
  251.1 140.7 reduce-scatter.2
  397.8 165.6 reduce-scatter.4
